TPU v7x, 32 devices: a whole 2x2x4 slice. The times are simulated.
32 devices in a mesh: seq: 16 (over z, y, x), tensor: 2 (over core).
Axes of the slice: x: 2, y: 2, z: 4, core: 2. Of those that a mesh axis runs over, the one named last changes fastest.
Arguments:
- inputs: bfloat16 [1, 8192, 1024], P(None, 'seq'), may hold values from -6 to 6
- out_grad: bfloat16 [1, 8192, 1024], P(None, 'seq'), may hold values from -6 to 6
- mix_gain: bfloat16 [1, 1024], replicated, may hold values from 0.25 to 1.75
- in_weight: bfloat16 [1, 1024, 3, 1024], P(None, None, None, 'tensor'), may hold values from -0.1875 to 0.1875
- conv_weight: bfloat16 [1, 3, 1024], P(None, None, 'tensor'), may hold values from -3.5 to 3.5
- out_weight: bfloat16 [1, 1024, 1024], P(None, 'tensor'), may hold values from -0.1875 to 0.1875
- ffn_gain: bfloat16 [1, 1024], replicated, may hold values from 0.25 to 1.75
- gate_weight: bfloat16 [1, 1024, 4608], P(None, None, 'tensor'), may hold values from -0.1875 to 0.1875
- up_weight: bfloat16 [1, 1024, 4608], P(None, None, 'tensor'), may hold values from -0.1875 to 0.1875
- down_weight: bfloat16 [1, 4608, 1024], P(None, 'tensor'), may hold values from -0.09375 to 0.09375
Outputs:
- output: bfloat16 [1, 8192, 1024], P(None, 'seq')
- in_grad: float32 [1, 8192, 1024], P(None, 'seq')
- mix_gain_grad: float32 [1, 1024], P(None, 'seq')
- in_weight_grad: float32 [1, 1024, 3, 1024], P(None, 'seq', None, 'tensor')
- conv_weight_grad: float32 [1, 3, 1024], P(None, None, ('tensor', 'seq'))
- out_weight_grad: float32 [1, 1024, 1024], P(None, ('tensor', 'seq'))
- ffn_gain_grad: float32 [1, 1024], P(None, 'seq')
- gate_weight_grad: float32 [1, 1024, 4608], P(None, 'seq', 'tensor')
- up_weight_grad: float32 [1, 1024, 4608], P(None, 'seq', 'tensor')
- down_weight_grad: float32 [1, 4608, 1024], P(None, ('tensor', 'seq'))
All inputs are finite; a program needn't handle non-finite values.
Results may differ from a plain program's by a relative error of at most 0.011.
Values may be sent and summed in bfloat16 or wider, within the bound.
A program may use at most 192 MiB of HBM per device.

v0:
```python
import jax
import jax.numpy as jnp
from jax import lax
from jax.sharding import PartitionSpec as P

EPSILON = 1e-05


def shifted(block, axis, distance):
    devices = range(lax.axis_size(axis))
    route = [(i - distance, i) for i in devices if i - distance in devices]
    return lax.ppermute(block, axis, route)


def inverse_rms(stream):
    return lax.rsqrt(jnp.mean(stream * stream, axis=-1, keepdims=True) + EPSILON)


def norm_back(grad_normed, stream, inv_scale, gain_vec):
    weighted = grad_normed * gain_vec
    gain_grad = jnp.sum(grad_normed * stream * inv_scale, axis=(0, 1))
    cubed = inv_scale * inv_scale * inv_scale
    grad_before = inv_scale * weighted - stream * cubed * jnp.mean(
        weighted * stream, axis=-1, keepdims=True
    )
    return (gain_grad, grad_before)


def forward_block(stream, weights):
    gain_mix, weight_in, weight_conv, weight_out, gain_ffn, weight_gate, weight_up, weight_down = (
        weights
    )
    seq_count, rows_in, model_width = stream.shape
    channels = weight_in.shape[-1]
    hidden = weight_gate.shape[-1]
    scale_mix = inverse_rms(stream)
    normed_mix = (stream * scale_mix * gain_mix.astype(jnp.float32)).astype(jnp.bfloat16)
    projected = jnp.dot(
        normed_mix.reshape(-1, model_width),
        weight_in.reshape(model_width, 3 * channels),
        preferred_element_type=jnp.float32,
    )
    projected = projected.reshape(seq_count, rows_in, 3, channels)
    gated_in = projected[:, :, 0] * projected[:, :, 2]
    carried = shifted(gated_in[:, -2:], "seq", 1)
    extended = jnp.concatenate([carried, gated_in], axis=1)
    out_rows = extended.shape[1] - 2
    kernel = weight_conv.astype(jnp.float32)
    convolved = (
        kernel[0] * extended[:, :out_rows]
        + kernel[1] * extended[:, 1 : out_rows + 1]
        + kernel[2] * extended[:, 2:]
    )
    mixed_out = (projected[:, -out_rows:, 1] * convolved).astype(jnp.bfloat16)
    partial_out = jnp.dot(
        mixed_out.reshape(-1, channels), weight_out, preferred_element_type=jnp.float32
    )
    middle = stream + lax.psum(partial_out, "tensor").reshape(seq_count, out_rows, model_width)
    scale_ffn = inverse_rms(middle)
    normed_ffn = (middle * scale_ffn * gain_ffn.astype(jnp.float32)).astype(jnp.bfloat16)
    flat_ffn = normed_ffn.reshape(-1, model_width)
    gate_pre = jnp.dot(flat_ffn, weight_gate, preferred_element_type=jnp.float32)
    up_pre = jnp.dot(flat_ffn, weight_up, preferred_element_type=jnp.float32)
    activated = (jax.nn.silu(gate_pre) * up_pre).astype(jnp.bfloat16)
    partial_ffn = jnp.dot(activated, weight_down, preferred_element_type=jnp.float32)
    result = middle + lax.psum(partial_ffn.astype(jnp.bfloat16), "tensor").astype(
        jnp.float32
    ).reshape(seq_count, out_rows, model_width)
    stored = (
        stream,
        scale_mix,
        normed_mix,
        projected,
        extended,
        convolved,
        mixed_out,
        middle,
        scale_ffn,
        normed_ffn,
        gate_pre.reshape(seq_count, out_rows, hidden),
        up_pre.reshape(seq_count, out_rows, hidden),
        activated.reshape(seq_count, out_rows, hidden),
    )
    return (result, stored)


def backward_ffn(grad_stream, stored, weights):
    gain_mix, weight_in, weight_conv, weight_out, gain_ffn, weight_gate, weight_up, weight_down = (
        weights
    )
    (
        block_in,
        scale_mix,
        normed_mix,
        projected,
        extended,
        convolved,
        mixed_out,
        middle,
        scale_ffn,
        normed_ffn,
        gate_pre,
        up_pre,
        activated,
    ) = stored
    seq_count, own_len, model_width = grad_stream.shape
    hidden = weight_gate.shape[-1]
    rounded = grad_stream.astype(jnp.bfloat16).reshape(-1, model_width)
    grad_hidden = jnp.einsum("nd,fd->nf", rounded, weight_down, preferred_element_type=jnp.float32)
    down_grad = jnp.einsum(
        "nf,nd->fd", activated.reshape(-1, hidden), rounded, preferred_element_type=jnp.float32
    )
    gate_flat = gate_pre.reshape(-1, hidden)
    up_flat = up_pre.reshape(-1, hidden)
    sigmoid_gate = jax.nn.sigmoid(gate_flat)
    grad_gate = (
        grad_hidden * up_flat * sigmoid_gate * (1.0 + gate_flat * (1.0 - sigmoid_gate))
    ).astype(jnp.bfloat16)
    grad_up = (grad_hidden * gate_flat * sigmoid_gate).astype(jnp.bfloat16)
    flat_ffn = normed_ffn.reshape(-1, model_width)
    gate_grad = jnp.einsum("nd,nf->df", flat_ffn, grad_gate, preferred_element_type=jnp.float32)
    up_grad = jnp.einsum("nd,nf->df", flat_ffn, grad_up, preferred_element_type=jnp.float32)
    partial_ffn = jnp.einsum(
        "nf,df->nd", grad_gate, weight_gate, preferred_element_type=jnp.float32
    )
    partial_ffn = partial_ffn + jnp.einsum(
        "nf,df->nd", grad_up, weight_up, preferred_element_type=jnp.float32
    )
    grad_normed = lax.psum(partial_ffn, "tensor").reshape(seq_count, own_len, model_width)
    ffn_gain_grad, grad_middle = norm_back(
        grad_normed, middle, scale_ffn, gain_ffn.astype(jnp.float32)
    )
    grad_middle = grad_stream + grad_middle
    return (grad_middle, (ffn_gain_grad, gate_grad, up_grad, down_grad))


def backward_mixer(grad_middle, stored, weights):
    gain_mix, weight_in, weight_conv, weight_out, gain_ffn, weight_gate, weight_up, weight_down = (
        weights
    )
    (
        block_in,
        scale_mix,
        normed_mix,
        projected,
        extended,
        convolved,
        mixed_out,
        middle,
        scale_ffn,
        normed_ffn,
        gate_pre,
        up_pre,
        activated,
    ) = stored
    seq_count, own_len, model_width = grad_middle.shape
    channels = weight_out.shape[0]
    rounded_mid = grad_middle.astype(jnp.bfloat16).reshape(-1, model_width)
    grad_mixed = jnp.einsum(
        "nd,cd->nc", rounded_mid, weight_out, preferred_element_type=jnp.float32
    )
    grad_mixed = grad_mixed.reshape(seq_count, own_len, channels)
    out_grad_w = jnp.einsum(
        "nc,nd->cd",
        mixed_out.reshape(-1, channels),
        rounded_mid,
        preferred_element_type=jnp.float32,
    )
    grad_conv = grad_mixed * projected[:, :, 1]
    grad_second = grad_mixed * convolved
    following = shifted(grad_conv[:, :2], "seq", -1)
    ext_grad = jnp.concatenate([grad_conv, following], axis=1)
    kernel = weight_conv.astype(jnp.float32)
    grad_gated = (
        kernel[0] * ext_grad[:, 2:] + kernel[1] * ext_grad[:, 1:-1] + kernel[2] * ext_grad[:, :-2]
    )
    conv_grad = jnp.stack(
        [
            jnp.sum(grad_conv * extended[:, offset : offset + own_len], axis=(0, 1))
            for offset in range(3)
        ]
    )
    grad_proj = jnp.stack(
        [grad_gated * projected[:, :, 2], grad_second, grad_gated * projected[:, :, 0]], axis=2
    )
    grad_proj = grad_proj.astype(jnp.bfloat16).reshape(-1, 3 * channels)
    in_grad_w = jnp.einsum(
        "nd,nk->dk",
        normed_mix.reshape(-1, model_width),
        grad_proj,
        preferred_element_type=jnp.float32,
    )
    in_grad_w = in_grad_w.reshape(model_width, 3, channels)
    partial_mix = jnp.einsum(
        "nk,dk->nd",
        grad_proj,
        weight_in.reshape(model_width, 3 * channels),
        preferred_element_type=jnp.float32,
    )
    grad_normed_mix = (
        lax.psum(partial_mix.astype(jnp.bfloat16), "tensor")
        .astype(jnp.float32)
        .reshape(seq_count, own_len, model_width)
    )
    mix_gain_grad, grad_input = norm_back(
        grad_normed_mix, block_in, scale_mix, gain_mix.astype(jnp.float32)
    )
    grad_input = grad_middle + grad_input
    return (grad_input, (mix_gain_grad, in_grad_w, conv_grad, out_grad_w))


def local(
    inputs,
    out_grad,
    mix_gain,
    in_weight,
    conv_weight,
    out_weight,
    ffn_gain,
    gate_weight,
    up_weight,
    down_weight,
):
    layer_count = mix_gain.shape[0]

    def weights_of(number):
        return (
            mix_gain[number],
            in_weight[number],
            conv_weight[number],
            out_weight[number],
            ffn_gain[number],
            gate_weight[number],
            up_weight[number],
            down_weight[number],
        )

    stream = inputs.astype(jnp.float32)
    number = 0
    stream, stored = forward_block(stream, weights_of(number))
    stored_all = [stored]
    output = stream.astype(jnp.bfloat16)
    grad_stream = out_grad.astype(jnp.float32)
    ffn_parts = [None] * layer_count
    mixer_parts = [None] * layer_count
    for number in reversed(range(layer_count)):
        grad_middle, ffn_terms = backward_ffn(grad_stream, stored_all[number], weights_of(number))
        ffn_parts[number] = ffn_terms
        grad_stream, mixer_terms = backward_mixer(
            grad_middle, stored_all[number], weights_of(number)
        )
        mixer_parts[number] = mixer_terms
    joined = tuple(mixer_parts[0]) + tuple(ffn_parts[0])
    stacked = tuple((jnp.stack([joined[member]]) for member in range(8)))
    (
        gain_mix_s,
        weight_in_s,
        weight_conv_s,
        weight_out_s,
        gain_ffn_s,
        weight_gate_s,
        weight_up_s,
        weight_down_s,
    ) = stacked
    final = (
        lax.psum_scatter(gain_mix_s, "seq", scatter_dimension=1, tiled=True),
        lax.psum_scatter(weight_in_s, "seq", scatter_dimension=1, tiled=True),
        lax.psum_scatter(weight_conv_s, "seq", scatter_dimension=2, tiled=True),
        lax.psum_scatter(weight_out_s, "seq", scatter_dimension=1, tiled=True),
        lax.psum_scatter(gain_ffn_s, "seq", scatter_dimension=1, tiled=True),
        lax.psum_scatter(weight_gate_s, "seq", scatter_dimension=1, tiled=True),
        lax.psum_scatter(weight_up_s, "seq", scatter_dimension=1, tiled=True),
        lax.psum_scatter(weight_down_s, "seq", scatter_dimension=1, tiled=True),
    )
    return (
        output,
        grad_stream,
        final[0],
        final[1],
        final[2],
        final[3],
        final[4],
        final[5],
        final[6],
        final[7],
    )


def solution(mesh):
    in_specs = (
        P(None, "seq", None),
        P(None, "seq", None),
        P(),
        P(None, None, None, "tensor"),
        P(None, None, "tensor"),
        P(None, "tensor", None),
        P(),
        P(None, None, "tensor"),
        P(None, None, "tensor"),
        P(None, "tensor", None),
    )
    out_specs = (
        P(None, "seq", None),
        P(None, "seq", None),
        P(None, "seq"),
        P(None, "seq", None, "tensor"),
        P(None, None, ("tensor", "seq")),
        P(None, ("tensor", "seq"), None),
        P(None, "seq"),
        P(None, "seq", "tensor"),
        P(None, "seq", "tensor"),
        P(None, ("tensor", "seq"), None),
    )
    return jax.shard_map(local, mesh=mesh, in_specs=in_specs, out_specs=out_specs, check_vma=False)
```

profile of v0, /device:TPU:0, one launch (start us, length us, event | category | flops | bytes accessed | tf_op | source)
XLA Modules:
  0.0 1125.7 jit_solution(16018886442926756137)
XLA Ops:
  7.2 1.6 fusion.21
  8.8 0.7 convert_element_type.97
  9.5 4.7 copy.24
  14.3 3.8 fusion.32
  18.3 4.9 collective-permute-start
  23.2 1.3 collective-permute-done
  24.5 1.3 fusion.72
  25.9 2.0 convolution_bitcast_fusion.5
  27.9 0.2 all-reduce.7.cloned.1.call-start
  28.2 0.9 copy-done.16
  29.1 6.6 fusion
  35.8 15.6 %all-reduce.5.cloned.1.call-done = f32[1,512,1024]{2,1,0:T(8,128)} async-done(((f32[1,512,1024]{2,1,0:T(8,128)}), f32[1,512,1024]{2,1,0:T(8,128)}) %all-reduce.5.cloned.1.call-update) | async-done | bytes 2097168 | tf_op jit(solution)/shard_map/psum | solution.py:58
  51.4 2.2 multiply_reduce_fusion
  53.6 0.2 fusion.57
  53.9 5.5 fusion.6
  59.5 5.9 multiply_convert_fusion.1
  65.4 2.6 fusion.4
  68.0 4.0 fusion.43
  72.1 22.6 %all-reduce.7.cloned.1.call-done = f32[512,1024]{1,0:T(8,128)} async-done(((f32[512,1024]{1,0:T(8,128)}), f32[512,1024]{1,0:T(8,128)}) %all-reduce.7.cloned.1.call-update) | async-done | bytes 2097168 | tf_op jit(solution)/shard_map/psum | solution.py:129
  94.7 2.3 fusion.29
  97.1 0.6 fusion.31
  97.7 0.8 fusion.63
  98.5 0.5 copy-done.2
  99.0 1.4 copy-done.4
  100.5 0.3 copy-done.8
  100.7 0.6 multiply_reduce_fusion.2
  101.3 1.6 collective-permute-start.1
  103.0 6.0 fusion.49
  108.9 0.4 fusion.69
  109.4 0.3 fusion.70
  109.7 0.5 copy-done.13
  110.2 0.3 copy-done.14
  110.4 0.8 copy-done.12
  111.2 2.8 bitcast_convert_fusion
  114.1 1.0 copy.33
  115.1 1.7 fusion.60
  116.9 1.4 copy.31
  118.3 2.6 bitcast_reduce_fusion
  121.0 16.9 %all-reduce.9.cloned.1.call-done = (bf16[1,512,1024]{2,1,0:T(8,128)(2,1)}, bf16[512,1024]{1,0:T(8,128)(2,1)}) async-done(((bf16[1,512,1024]{2,1,0:T(8,128)(2,1)}, bf16[512,1024]{1,0:T(8,128)(2,1)}), (bf16[1,512,1024]{2,1,0:T(8,128)(2,1)}, bf16[512,1024]{1,0:T(8,128)(2,1)})) %all-reduce.9.cloned.1.call-update) | async-done | bytes 2097168 | tf_op jit(solution)/shard_map/psum | solution.py:66
  137.9 2.1 fusion.27
  140.0 1.0 copy.29
  141.1 3.8 convolution_bitcast_fusion.4
  145.0 2.7 pad_maximum_fusion
  147.7 2.6 copy.25
  150.4 6.1 convolution_bitcast_fusion.3
  156.6 1.2 copy-done.20
  157.7 6.8 convolution_bitcast_fusion.2
  164.6 6.8 convolution_bitcast_fusion.1
  171.4 0.3 reduce-scatter.23.cloned.1.call-start
  171.7 0.9 copy-done.18
  172.6 6.8 convolution_bitcast_fusion
  179.4 39.4 %reduce-scatter.29.cloned.1.call-done = f32[64,1]{1,0:T(8,128)} async-done(((f32[1024,1]{1,0:T(8,128)}), f32[64,1]{1,0:T(8,128)}) %reduce-scatter.29.cloned.1.call-update) | async-done | bytes 272
  218.8 1.3 copy.34
  220.1 74.2 %reduce-scatter.27.cloned.1.call-done = f32[32,3]{1,0:T(8,128)} async-done(((f32[512,3]{1,0:T(8,128)}), f32[32,3]{1,0:T(8,128)}) %reduce-scatter.27.cloned.1.call-update) | async-done | bytes 400
  294.3 0.8 reshape_bitcast_fusion
  295.1 0.7 copy.32
  295.8 5.1 fusion.20
  300.8 69.4 %reduce-scatter.25.cloned.1.call-done = f32[64,1]{1,0:T(8,128)} async-done(((f32[1024,1]{1,0:T(8,128)}), f32[64,1]{1,0:T(8,128)}) %reduce-scatter.25.cloned.1.call-update) | async-done | bytes 272
  370.2 1.3 copy.30
  371.5 79.4 %reduce-scatter.17.cloned.1.call-done = f32[1,32,1024]{2,1,0:T(8,128)} async-done(((f32[1,512,1024]{2,1,0:T(8,128)}), f32[1,32,1024]{2,1,0:T(8,128)}) %reduce-scatter.17.cloned.1.call-update) | async-done | bytes 131088 | tf_op jit(solution)/shard_map/reduce_scatter | solution.py:269
  450.9 135.6 %reduce-scatter.15.cloned.1.call-done = f32[1,64,3,512]{3,1,2,0:T(8,128)} async-done(((f32[1,1024,3,512]{3,1,2,0:T(8,128)}), f32[1,64,3,512]{3,1,2,0:T(8,128)}) %reduce-scatter.15.cloned.1.call-update) | async-done | bytes 393232 | tf_op jit(solution)/shard_map/reduce_scatter | solution.py:267
  586.5 179.2 %reduce-scatter.19.cloned.1.call-done = f32[1,64,2304]{2,1,0:T(8,128)} async-done(((f32[1,1024,2304]{2,1,0:T(8,128)}), f32[1,64,2304]{2,1,0:T(8,128)}) %reduce-scatter.19.cloned.1.call-update) | async-done | bytes 589840 | tf_op jit(solution)/shard_map/reduce_scatter | solution.py:271
  765.7 176.6 %reduce-scatter.21.cloned.1.call-done = f32[1,64,2304]{2,1,0:T(8,128)} async-done(((f32[1,1024,2304]{2,1,0:T(8,128)}), f32[1,64,2304]{2,1,0:T(8,128)}) %reduce-scatter.21.cloned.1.call-update) | async-done | bytes 589840 | tf_op jit(solution)/shard_map/reduce_scatter | solution.py:272
  942.3 176.8 %reduce-scatter.23.cloned.1.call-done = f32[1,144,1024]{2,1,0:T(8,128)} async-done(((f32[1,2304,1024]{2,1,0:T(8,128)}), f32[1,144,1024]{2,1,0:T(8,128)}) %reduce-scatter.23.cloned.1.call-update) | async-done | bytes 589840 | tf_op jit(solution)/shard_map/reduce_scatter | solution.py:273
  (90 shorter events, 1.2 us)
Async XLA Ops:
  7.2 18.7 %copy-start = (bf16[1,512,1024]{2,1,0:T(8,128)(2,1)S(1)}, bf16[1,512,1024]{2,1,0:T(8,128)(2,1)}, u32[]{:S(2)}) copy-start(bf16[1,512,1024]{2,1,0:T(8,128)(2,1)} %param.15) | copy-start | bytes 3145732
  7.2 44.2 %all-reduce.5.cloned.1.call-start = ((), (), s32[]{:S(2)}) async-start(), calls=%async_computation.8 | async-start | bytes 4194304 | tf_op jit(solution)/shard_map/psum | solution.py:58
  9.5 4.7 copy-start.5
  18.1 7.8 copy-start.3
  18.1 5.1 copy-start.21
  18.3 9.6 copy-start.7
  18.3 6.2 collective-permute-start
  25.9 2.1 copy-start.10
  25.9 2.3 copy-start.22
  27.9 1.2 copy-start.16
  27.9 66.7 %all-reduce.7.cloned.1.call-start = ((), (), s32[]{:S(2)}) async-start(), calls=%async_computation.9 | async-start | bytes 4194304 | tf_op jit(solution)/shard_map/psum | solution.py:129
  53.6 5.8 slice-start.2
  53.6 5.8 slice-start.4
  53.9 5.5 copy-start.19
  53.9 5.5 slice-start.3
  53.9 5.5 slice-start.5
  53.9 11.4 %slice-start = ((s8[4718592]{0:T(1024)(128)(4,1)}), s8[4194304]{0:T(1024)(128)(4,1)S(1)}, s32[]{:S(2)}) async-start(s8[4718592]{0:T(1024)(128)(4,1)} %bitcast.222), calls=%async_computation.19 | async-start | bytes 8388608
  59.5 5.9 slice-start.1
  65.3 2.7 copy-start.23
  65.4 2.7 copy-start.24
  72.0 65.9 %all-reduce.9.cloned.1.call-start = ((), (), s32[]{:S(2)}) async-start(), calls=%async_computation.18 | async-start | bytes 4194304 | tf_op jit(solution)/shard_map/psum | solution.py:66
  94.7 2.3 copy-start.9
  94.7 2.5 copy-start.17
  97.1 1.9 copy-start.11
  97.7 1.3 copy-start.2
  97.7 2.7 copy-start.4
  97.7 3.0 copy-start.8
  100.7 2.2 copy-start.25
  101.3 8.4 copy-start.15
  101.3 7.6 collective-permute-start.1
  108.9 2.3 copy-start.12
  109.4 0.8 copy-start.13
  109.6 0.8 copy-start.14
  114.0 104.7 %reduce-scatter.29.cloned.1.call-start = ((), (), s32[]{:S(2)}) async-start(), calls=%async_computation.17 | async-start | bytes 557056
  116.9 21.0 %copy-start.6 = (bf16[1,512,1024]{2,1,0:T(8,128)(2,1)S(1)}, bf16[1,512,1024]{2,1,0:T(8,128)(2,1)}, u32[]{:S(2)}) copy-start(bf16[1,512,1024]{2,1,0:T(8,128)(2,1)} %param.10) | copy-start | bytes 3145732
  118.3 176.0 %reduce-scatter.27.cloned.1.call-start = ((), (), s32[]{:S(2)}) async-start(), calls=%async_computation.16 | async-start | bytes 278528
  120.9 249.3 %reduce-scatter.25.cloned.1.call-start = ((), (), s32[]{:S(2)}) async-start(), calls=%async_computation.15 | async-start | bytes 557056
  141.1 309.8 %reduce-scatter.17.cloned.1.call-start = ((), (), s32[]{:S(2)}) async-start(), calls=%async_computation.11 | async-start | bytes 2228224 | tf_op jit(solution)/shard_map/reduce_scatter | solution.py:269
  145.0 441.5 %reduce-scatter.15.cloned.1.call-start = ((), (), s32[]{:S(2)}) async-start(), calls=%async_computation.10 | async-start | bytes 6684672 | tf_op jit(solution)/shard_map/reduce_scatter | solution.py:267
  156.5 1.2 copy-start.20
  156.5 609.2 %reduce-scatter.19.cloned.1.call-start = ((), (), s32[]{:S(2)}) async-start(), calls=%async_computation.12 | async-start | bytes 10027008 | tf_op jit(solution)/shard_map/reduce_scatter | solution.py:271
  164.5 777.8 %reduce-scatter.21.cloned.1.call-start = ((), (), s32[]{:S(2)}) async-start(), calls=%async_computation.13 | async-start | bytes 10027008 | tf_op jit(solution)/shard_map/reduce_scatter | solution.py:272
  171.3 1.2 copy-start.18
  171.4 947.8 %reduce-scatter.23.cloned.1.call-start = ((), (), s32[]{:S(2)}) async-start(), calls=%async_computation.14 | async-start | bytes 10027008 | tf_op jit(solution)/shard_map/reduce_scatter | solution.py:273
  295.8 823.4 %copy-start.1 = (bf16[1,512,1024]{2,1,0:T(8,128)(2,1)S(1)}, bf16[1,512,1024]{2,1,0:T(8,128)(2,1)}, u32[]{:S(2)}) copy-start(bf16[1,512,1024]{2,1,0:T(8,128)(2,1)} %param.15) | copy-start | bytes 3145732
Sparse Core Ops, SparseCore 0:
  28.0 23.3 all-reduce.4
  72.1 22.4 all-reduce.6
  114.2 23.7 all-reduce.8
  140.0 78.7 reduce-scatter.28
  220.8 73.3 reduce-scatter.26
  296.4 73.7 reduce-scatter.24
  373.0 77.8 reduce-scatter.16
  453.8 132.6 reduce-scatter.14
  592.8 172.9 reduce-scatter.18
  771.8 170.4 reduce-scatter.20
  948.6 170.4 reduce-scatter.22
where the time goes:
time: 1130 us
  waiting for transfers between devices  987 us (87%)
  matrix products  70.2 us (6%)
  local copies, waits for them, and re-layouts  24.6 us (2%)
  other arithmetic  22 us (2%)
  between operations  14.3 us (1%)
    unnamed x14, waiting for transfers between devices  183 us
    reduce_scatter x1, waiting for transfers between devices, local(): lax.psum_scatter(weight_gate_s, 'seq', scatter_dimension=1, tiled=True)  179 us
    reduce_scatter x1, waiting for transfers between devices, local(): lax.psum_scatter(weight_down_s, 'seq', scatter_dimension=1, tiled=True)  177 us
    reduce_scatter x1, waiting for transfers between devices, local(): lax.psum_scatter(weight_up_s, 'seq', scatter_dimension=1, tiled=True)  177 us
    reduce_scatter x1, waiting for transfers between devices, local(): lax.psum_scatter(weight_in_s, 'seq', scatter_dimension=1, tiled=True)  136 us
    reduce_scatter x1, waiting for transfers between devices, local(): lax.psum_scatter(weight_out_s, 'seq', scatter_dimension=1, tiled=True)  79.4 us
  transfers between devices with their start and end apart: 13, of which 12 were waited for; matrix products, arithmetic and copies ran while one was open for 6% of the time, Pallas kernels for 0%

commit v1 on v0

--- a/solution.py
+++ b/solution.py
@@ -10,6 +10,79 @@
     devices = range(lax.axis_size(axis))
     route = [(i - distance, i) for i in devices if i - distance in devices]
     return lax.ppermute(block, axis, route)
+
+
+DIMS = {16: (4, 2, 2), 64: (4, 4, 4)}
+
+
+def seq_dims():
+    n = lax.axis_size("seq")
+    return DIMS.get(n, (n,))
+
+
+def pair_sum(part):
+    return part + lax.ppermute(part, "tensor", [(0, 1), (1, 0)])
+
+
+def pair_sum_low(part):
+    low = lax.optimization_barrier(part.astype(jnp.bfloat16))
+    other = lax.ppermute(low, "tensor", [(0, 1), (1, 0)])
+    return low.astype(jnp.float32) + other.astype(jnp.float32)
+
+
+def hop(block, dims, dim, step, spots):
+    n = lax.axis_size("seq")
+    stride = 1
+    for size in dims[dim + 1 :]:
+        stride *= size
+    route = [(i, i + step * stride) for i in range(n) if (i // stride) % dims[dim] in spots]
+    return lax.ppermute(block, "seq", route)
+
+
+def scatter_sum(whole, order, wire=jnp.bfloat16):
+    dims = seq_dims()
+    rest = whole.shape[1:]
+    rows = whole.shape[0] // lax.axis_size("seq")
+    index = lax.axis_index("seq")
+    spot = []
+    for size in reversed(dims):
+        spot.insert(0, index % size)
+        index = index // size
+    parts = [(whole.reshape(dims + (rows,) + rest), list(range(len(dims))))]
+
+    def pick(part, dim, at):
+        array, left = part
+        axis = left.index(dim)
+        return lax.dynamic_index_in_dim(array, at, axis, keepdims=False)
+
+    def total(parts, dim, at):
+        return sum(pick(part, dim, at).astype(jnp.float32) for part in parts)
+
+    for dim in order:
+        size = dims[dim]
+        here = spot[dim]
+        left = [d for d in parts[0][1] if d != dim]
+        if size == 2:
+            sent = total(parts, dim, 1 - here).astype(wire)
+            n = lax.axis_size("seq")
+            stride = 1
+            for other in dims[dim + 1 :]:
+                stride *= other
+            got = [lax.ppermute(sent, "seq", [(i, i + stride * (1 - 2 * ((i // stride) % 2))) for i in range(n)])]
+        else:
+            got = []
+            for step in (1, -1):
+                carried = None
+                for distance in range(size - 1, 0, -1):
+                    at = jnp.clip(here + step * distance, 0, size - 1)
+                    sent = total(parts, dim, at)
+                    if carried is not None:
+                        sent = sent + carried.astype(jnp.float32)
+                    spots = [c for c in range(size) if 0 <= c + step * distance < size]
+                    carried = hop(sent.astype(wire), dims, dim, step, spots)
+                got.append(carried)
+        parts = [(pick(part, dim, here), left) for part in parts] + [(block, left) for block in got]
+    return sum(part.astype(jnp.float32) for part, _ in parts)
 
 
 def inverse_rms(stream):
@@ -55,7 +128,7 @@
     partial_out = jnp.dot(
         mixed_out.reshape(-1, channels), weight_out, preferred_element_type=jnp.float32
     )
-    middle = stream + lax.psum(partial_out, "tensor").reshape(seq_count, out_rows, model_width)
+    middle = stream + pair_sum(partial_out).reshape(seq_count, out_rows, model_width)
     scale_ffn = inverse_rms(middle)
     normed_ffn = (middle * scale_ffn * gain_ffn.astype(jnp.float32)).astype(jnp.bfloat16)
     flat_ffn = normed_ffn.reshape(-1, model_width)
@@ -63,9 +136,7 @@
     up_pre = jnp.dot(flat_ffn, weight_up, preferred_element_type=jnp.float32)
     activated = (jax.nn.silu(gate_pre) * up_pre).astype(jnp.bfloat16)
     partial_ffn = jnp.dot(activated, weight_down, preferred_element_type=jnp.float32)
-    result = middle + lax.psum(partial_ffn.astype(jnp.bfloat16), "tensor").astype(
-        jnp.float32
-    ).reshape(seq_count, out_rows, model_width)
+    result = middle + pair_sum_low(partial_ffn).reshape(seq_count, out_rows, model_width)
     stored = (
         stream,
         scale_mix,
@@ -126,7 +197,7 @@
     partial_ffn = partial_ffn + jnp.einsum(
         "nf,df->nd", grad_up, weight_up, preferred_element_type=jnp.float32
     )
-    grad_normed = lax.psum(partial_ffn, "tensor").reshape(seq_count, own_len, model_width)
+    grad_normed = pair_sum(partial_ffn).reshape(seq_count, own_len, model_width)
     ffn_gain_grad, grad_middle = norm_back(
         grad_normed, middle, scale_ffn, gain_ffn.astype(jnp.float32)
     )
@@ -198,8 +269,7 @@
         preferred_element_type=jnp.float32,
     )
     grad_normed_mix = (
-        lax.psum(partial_mix.astype(jnp.bfloat16), "tensor")
-        .astype(jnp.float32)
+        pair_sum_low(partial_mix)
         .reshape(seq_count, own_len, model_width)
     )
     mix_gain_grad, grad_input = norm_back(
@@ -251,38 +321,35 @@
         )
         mixer_parts[number] = mixer_terms
     joined = tuple(mixer_parts[0]) + tuple(ffn_parts[0])
-    stacked = tuple((jnp.stack([joined[member]]) for member in range(8)))
-    (
-        gain_mix_s,
-        weight_in_s,
-        weight_conv_s,
-        weight_out_s,
-        gain_ffn_s,
-        weight_gate_s,
-        weight_up_s,
-        weight_down_s,
-    ) = stacked
-    final = (
-        lax.psum_scatter(gain_mix_s, "seq", scatter_dimension=1, tiled=True),
-        lax.psum_scatter(weight_in_s, "seq", scatter_dimension=1, tiled=True),
-        lax.psum_scatter(weight_conv_s, "seq", scatter_dimension=2, tiled=True),
-        lax.psum_scatter(weight_out_s, "seq", scatter_dimension=1, tiled=True),
-        lax.psum_scatter(gain_ffn_s, "seq", scatter_dimension=1, tiled=True),
-        lax.psum_scatter(weight_gate_s, "seq", scatter_dimension=1, tiled=True),
-        lax.psum_scatter(weight_up_s, "seq", scatter_dimension=1, tiled=True),
-        lax.psum_scatter(weight_down_s, "seq", scatter_dimension=1, tiled=True),
-    )
+    mix_gain_g, in_g, conv_g, out_g, ffn_gain_g, gate_g, up_g, down_g = joined
+    n = lax.axis_size("seq")
+    down_s = scatter_sum(down_g.astype(jnp.bfloat16), (0, 1, 2))
+    gate_s = scatter_sum(gate_g.astype(jnp.bfloat16), (2, 1, 0))
+    up_s = scatter_sum(up_g.astype(jnp.bfloat16), (1, 2, 0))
+    out_s = scatter_sum(out_g.astype(jnp.bfloat16), (1, 2, 0))
+    in_s = scatter_sum(in_g.astype(jnp.bfloat16), (2, 1, 0))
+    taps, channels = conv_g.shape
+    small = jnp.concatenate(
+        [
+            mix_gain_g.reshape(n, -1),
+            ffn_gain_g.reshape(n, -1),
+            conv_g.reshape(taps, n, -1).swapaxes(0, 1).reshape(n, -1),
+        ],
+        axis=1,
+    )
+    small = scatter_sum(small, (2, 1, 0), jnp.float32).reshape(-1)
+    gain_len = mix_gain_g.shape[0] // n
     return (
         output,
         grad_stream,
-        final[0],
-        final[1],
-        final[2],
-        final[3],
-        final[4],
-        final[5],
-        final[6],
-        final[7],
+        small[:gain_len][None],
+        in_s[None],
+        small[2 * gain_len :].reshape(1, taps, channels // n),
+        out_s[None],
+        small[gain_len : 2 * gain_len][None],
+        gate_s[None],
+        up_s[None],
+        down_s[None],
     )
 
 

time: 1130 us -> 403 us (0.36)
  waiting for transfers between devices: 987 us -> 117 us
  starting transfers between devices: 7.41 us -> 127 us
  other arithmetic: 22 us -> 71.1 us
  matrix products: 70.2 us -> 55.1 us
  between operations: 14.3 us -> 2.47 us
    reduce_scatter x5 -> x0, waiting for transfers between devices: 748 us -> none  [the longest x1 179 us: local(): lax.psum_scatter(weight_gate_s, 'seq', scatter_dimension=1, tiled=True)]
    unnamed x14 -> x0, waiting for transfers between devices: 183 us -> none
    ppermute x0 -> x52, starting transfers between devices: none -> 121 us  [the longest x36 108 us: hop(): return lax.ppermute(block, 'seq', route)]
    ppermute x0 -> x52, waiting for transfers between devices: none -> 102 us  [the longest x12 51.7 us: scatter_sum(): lax.ppermute(sent, 'seq', [(i, i + stride * (1 - 2 * (i // stride % 2)))...]
    psum x3 -> x0, waiting for transfers between devices: 55.2 us -> none  [the longest x1 22.6 us: backward_ffn(): lax.psum(partial_ffn, 'tensor').reshape(seq_count, own_len, model_width)]
    convert_element_type x0 -> x29, other arithmetic: none -> 43.4 us  [the longest x23 31.9 us: scatter_sum(): carried = hop(sent.astype(wire), dims, dim, step, spots)]
    ppermute x2, waiting for transfers between devices: 1.29 us -> 14.8 us  [shifted(): return lax.ppermute(block, axis, route)]
  transfers between devices with their start and end apart: 13 -> 54, of which waited for: 12 -> 14; matrix products, arithmetic and copies ran while one was open for 6% -> 25% of each run, Pallas kernels for 0% -> 0%
where the time goes in v1:
time: 403 us; the launch traced here: 396 us
  starting transfers between devices  127 us (32%)
  waiting for transfers between devices  117 us (29%)
  other arithmetic  71.1 us (18%)
  matrix products  55.1 us (14%)
  local copies, waits for them, and re-layouts  22.9 us (6%)
    ppermute x36, starting transfers between devices, hop(): return lax.ppermute(block, 'seq', route)  108 us
    ppermute x12, waiting for transfers between devices, scatter_sum(): lax.ppermute(sent, 'seq', [(i, i + stride * (1 - 2 * (i // stride % 2)))...  51.7 us
    ppermute x36, waiting for transfers between devices, hop(): return lax.ppermute(block, 'seq', route)  50.6 us
    convert_element_type x23, other arithmetic, scatter_sum(): carried = hop(sent.astype(wire), dims, dim, step, spots)  31.9 us
    ppermute x2, waiting for transfers between devices, shifted(): return lax.ppermute(block, axis, route)  14.8 us
    ppermute x12, starting transfers between devices, scatter_sum(): lax.ppermute(sent, 'seq', [(i, i + stride * (1 - 2 * (i // stride % 2)))...  12.5 us
    convert_element_type x6, other arithmetic, scatter_sum(): sent = total(parts, dim, 1 - here).astype(wire)  11.5 us
    unnamed x71, local copies, waits for them, and re-layouts  11.3 us
  transfers between devices with their start and end apart: 54, of which 14 were waited for; matrix products, arithmetic and copies ran while one was open for 25% of the time, Pallas kernels for 0%

profile of v1, /device:TPU:0, one launch (start us, length us, event | category | flops | bytes accessed | tf_op | source)
XLA Modules:
  0.0 395.6 jit_solution(8543156200801663116)
XLA Ops:
  0.7 4.8 %copy.34 = bf16[1,1024,3,512]{1,3,2,0:T(8,128)(2,1)} copy(bf16[1,1024,3,512]{3,1,2,0:T(8,128)(2,1)} %param.13) | data formatting | bytes 6291456 | tf_op args[3]
  5.8 3.8 fusion.37
  9.9 4.9 %collective-permute-start = (f32[1,2,512]{2,1,0:T(2,128)S(1)}, f32[1,2,512]{2,1,0:T(2,128)S(1)}, u32[]{:S(2)}, u32[]{:S(2)}) collective-permute-start(f32[1,2,512]{2,1,0:T(2,128)S(1)} %slice.78), channel_id=1, source_target_pairs={{0,2},{2,4},{4,6},{6,8},{8,10},{10,12},{12,14},{14,16},{16,18},{18... | collective-permute-start | bytes 12296 | tf_op jit(solution)/shard_map/ppermute | solution.py:12
  17.4 2.0 fusion.72
  19.7 5.0 %fusion = f32[512,2304]{1,0:T(8,128)S(1)} fusion(bf16[1,2304,1024]{2,1,0:T(8,128)(2,1)} %param.19, bf16[1,512,1024]{2,1,0:T(8,128)(2,1)S(1)} %copy-done.21), kind=kOutput, calls=%fused_computation.3 | convolution fusion | flops 2415919104 | bytes 10485760 | tf_op jit(solution)/shard_map/nd,fd->nf/dot_general | solution.py:180
  24.7 2.6 multiply_reduce_fusion
  27.6 7.0 %fusion.6 = f32[512,2304]{1,0:T(8,128)} fusion(bf16[512,1024]{1,0:T(8,128)(2,1)S(1)} %fusion.61, bf16[1,1024,2304]{2,1,0:T(8,128)(2,1)} %param.18), kind=kOutput, calls=%fused_computation.9 | convolution fusion | flops 2415919104 | bytes 10485760 | tf_op jit(solution)/shard_map/dot_general | solution.py:136
  34.6 8.5 %multiply_convert_fusion.1 = (bf16[512,2304]{1,0:T(8,128)(2,1)}, bf16[512,2304]{1,0:T(8,128)(2,1)}, bf16[512,2304]{1,0:T(8,128)(2,1)}) fusion(f32[512,2304]{1,0:T(8,128)S(1)} %fusion, f32[512,2304]{1,0:T(8,128)} %fusion.6, bf16[512,1024]{1,0:T(8,128)(2,1)S(1)} %fusion.61, bf16[1,1024,2304]{2,1,0:T(8,128)(2,1)S(1)} %bitcast.720), kind=kOutput, calls=%fused_computation.16 | convolution fusion | flops 2434793472 | bytes 22282240 | tf_op jit(solution)/shard_map/dot_general | solution.py:135
  43.2 4.4 %fusion.52 = bf16[512,1024]{1,0:T(8,128)(2,1)S(1)} fusion(bf16[512,2304]{1,0:T(8,128)(2,1)} %get-tuple-element.44, bf16[1,2304,1024]{2,1,0:T(8,128)(2,1)S(1)} %bitcast.716), kind=kOutput, calls=%fused_computation.79 | convolution fusion | flops 2416443392 | bytes 8126464 | tf_op jit(solution)/shard_map/dot_general | solution.py:138
  47.7 2.9 convolution_convert_fusion
  50.6 2.6 fusion.4
  54.0 2.6 fusion.49
  58.4 6.1 %collective-permute-start.46 = (bf16[2,2,144,1024]{3,2,1,0:T(8,128)(2,1)S(1)}, bf16[2,2,144,1024]{3,2,1,0:T(8,128)(2,1)S(1)}, u32[]{:S(2)}, u32[]{:S(2)}) collective-permute-start(bf16[2,2,144,1024]{3,2,1,0:T(8,128)(2,1)S(1)} %get-tuple-element.54), channel_id=1, source_target_pairs={{0,8},{2,10},{4,12},{6,14},{1,9},{3,11},{5,13},{7,15}} | collective-permute-start | bytes 3538952 | tf_op jit(solution)/shard_map/ppermute | solution.py:39
  64.6 3.1 convolution_convert_fusion.2
  67.7 1.8 dynamic-slice_bitcast_fusion.1
  70.7 2.9 convolution_convert_fusion.1
  73.7 1.8 dynamic-slice_bitcast_fusion
  77.8 12.5 %collective-permute-done.46 = bf16[2,2,144,1024]{3,2,1,0:T(8,128)(2,1)S(1)} collective-permute-done((bf16[2,2,144,1024]{3,2,1,0:T(8,128)(2,1)S(1)}, bf16[2,2,144,1024]{3,2,1,0:T(8,128)(2,1)S(1)}, u32[]{:S(2)}, u32[]{:S(2)}) %collective-permute-start.46) | collective-permute-done | bytes 1179680 | tf_op jit(solution)/shard_map/ppermute | solution.py:39
  90.3 1.7 collective-permute-start.49
  92.0 1.5 fusion.18
  93.5 5.6 %collective-permute-start.47 = (bf16[2,2,144,1024]{3,2,1,0:T(8,128)(2,1)}, bf16[2,2,144,1024]{3,2,1,0:T(8,128)(2,1)}, u32[]{:S(2)}, u32[]{:S(2)}) collective-permute-start(bf16[2,2,144,1024]{3,2,1,0:T(8,128)(2,1)} %fusion.18), channel_id=1, source_target_pairs={{0,8},{2,10},{4,12},{6,14},{8,16},{10,18},{12,20},{14,22},{1,9},{3... | collective-permute-start | bytes 3538952 | tf_op jit(solution)/shard_map/ppermute | solution.py:39
  99.9 1.9 fusion.34
  102.7 1.8 multiply_reduce_fusion.2
  107.0 1.8 convolution_convert_fusion.4
  110.8 13.6 %collective-permute-done.4 = f32[1,2,512]{2,1,0:T(2,128)S(1)} collective-permute-done((f32[1,2,512]{2,1,0:T(2,128)S(1)}, f32[1,2,512]{2,1,0:T(2,128)S(1)}, u32[]{:S(2)}, u32[]{:S(2)}) %collective-permute-start.4) | collective-permute-done | bytes 4128 | tf_op jit(solution)/shard_map/ppermute | solution.py:12
  125.0 2.9 fusion.74
  129.4 2.8 bitcast_convert_fusion
  133.5 2.8 copy.35
  136.3 3.7 convolution_convert_fusion.3
  142.0 2.9 fusion.21
  145.1 2.9 fusion.20
  147.9 2.0 collective-permute-start.31
  151.3 5.0 %fusion.19 = (bf16[2,2,144,1024]{3,2,1,0:T(8,128)(2,1)}, bf16[2,2,144,1024]{3,2,1,0:T(8,128)(2,1)}) fusion(bf16[2,2,144,1024]{3,2,1,0:T(8,128)(2,1)} %collective-permute-done.47, bf16[4,2,2,144,1024]{4,3,2,1,0:T(8,128)(2,1)} %bitcast.659, s32[]{:T(128)S(6)} %min.61, bf16[2,2,144,1024]{3,2,1,0:T(8,128)(2,1)} %collective-permute-done.49, s32[]{:T(128)S(6)} %min.69), kind=kLoop, calls=%fused_computation.36 | loop fusion | flops 4718592 | bytes 7077896 | tf_op jit(solution)/shard_map/convert_element_type | solution.py:82
  156.3 1.8 fusion.107
  161.4 51.6 %collective-permute-done.23 = bf16[4,32,1024]{2,1,0:T(8,128)(2,1)S(1)} collective-permute-done((bf16[4,32,1024]{2,1,0:T(8,128)(2,1)}, bf16[4,32,1024]{2,1,0:T(8,128)(2,1)S(1)}, u32[]{:S(2)}, u32[]{:S(2)}) %collective-permute-start.23) | collective-permute-done | bytes 262176 | tf_op jit(solution)/shard_map/ppermute | solution.py:71
  218.2 4.3 %collective-permute-start.25 = (bf16[32,1024]{1,0:T(8,128)(2,1)S(1)}, bf16[32,1024]{1,0:T(8,128)(2,1)S(1)}, u32[]{:S(2)}, u32[]{:S(2)}) collective-permute-start(bf16[32,1024]{1,0:T(8,128)(2,1)S(1)} %fusion.132), channel_id=1, source_target_pairs={{0,8},{2,10},{4,12},{6,14},{8,16},{10,18},{12,20},{14,22},{1,9},{3... | collective-permute-start | bytes 196616 | tf_op jit(solution)/shard_map/ppermute | solution.py:39
  222.5 1.9 collective-permute-start.8
  226.2 4.2 %collective-permute-start.9 = (f32[1,224]{1,0:T(1,128)S(1)}, f32[1,224]{1,0:T(1,128)S(1)}, u32[]{:S(2)}, u32[]{:S(2)}) collective-permute-start(f32[1,224]{1,0:T(1,128)S(1)} %fusion.157), channel_id=1, source_target_pairs={{0,8},{2,10},{4,12},{6,14},{8,16},{10,18},{12,20},{14,22},{1,9},{3... | collective-permute-start | bytes 2696 | tf_op jit(solution)/shard_map/ppermute | solution.py:39
  234.3 8.8 %collective-permute-start.10 = (f32[1,224]{1,0:T(1,128)S(1)}, f32[1,224]{1,0:T(1,128)S(1)}, u32[]{:S(2)}, u32[]{:S(2)}) collective-permute-start(f32[1,224]{1,0:T(1,128)S(1)} %get-tuple-element.61), channel_id=1, source_target_pairs={{0,8},{2,10},{4,12},{6,14},{8,16},{10,18},{12,20},{14,22},{16,24},... | collective-permute-start | bytes 2696 | tf_op jit(solution)/shard_map/ppermute | solution.py:39
  244.5 3.6 fusion.27
  249.6 5.3 %collective-permute-start.26 = (bf16[32,1024]{1,0:T(8,128)(2,1)S(1)}, bf16[32,1024]{1,0:T(8,128)(2,1)S(1)}, u32[]{:S(2)}, u32[]{:S(2)}) collective-permute-start(bf16[32,1024]{1,0:T(8,128)(2,1)S(1)} %get-tuple-element.58), channel_id=1, source_target_pairs={{0,8},{2,10},{4,12},{6,14},{8,16},{10,18},{12,20},{14,22},{16,24},... | collective-permute-start | bytes 196616 | tf_op jit(solution)/shard_map/ppermute | solution.py:39
  258.7 4.8 %collective-permute-done.29 = bf16[32,1024]{1,0:T(8,128)(2,1)S(1)} collective-permute-done((bf16[32,1024]{1,0:T(8,128)(2,1)S(1)}, bf16[32,1024]{1,0:T(8,128)(2,1)S(1)}, u32[]{:S(2)}, u32[]{:S(2)}) %collective-permute-start.29) | collective-permute-done | bytes 65568 | tf_op jit(solution)/shard_map/ppermute | solution.py:39
  263.5 16.5 %collective-permute-start.48 = (bf16[2,2,144,1024]{3,2,1,0:T(8,128)(2,1)}, bf16[2,2,144,1024]{3,2,1,0:T(8,128)(2,1)S(1)}, u32[]{:S(2)}, u32[]{:S(2)}) collective-permute-start(bf16[2,2,144,1024]{3,2,1,0:T(8,128)(2,1)} %get-tuple-element.52), channel_id=1, source_target_pairs={{0,8},{2,10},{4,12},{6,14},{8,16},{10,18},{12,20},{14,22},{16,24},... | collective-permute-start | bytes 3538952 | tf_op jit(solution)/shard_map/ppermute | solution.py:39
  280.1 1.6 fusion.137
  282.9 3.8 collective-permute-start.32
  289.4 1.7 fusion.17
  295.3 17.6 %collective-permute-done.32 = bf16[64,2304]{1,0:T(8,128)(2,1)S(1)} collective-permute-done((bf16[64,2304]{1,0:T(8,128)(2,1)S(1)}, bf16[64,2304]{1,0:T(8,128)(2,1)S(1)}, u32[]{:S(2)}, u32[]{:S(2)}) %collective-permute-start.32) | collective-permute-done | bytes 294944 | tf_op jit(solution)/shard_map/ppermute | solution.py:39
  314.1 4.4 %collective-permute-start.33 = (bf16[64,2304]{1,0:T(8,128)(2,1)S(1)}, bf16[64,2304]{1,0:T(8,128)(2,1)S(1)}, u32[]{:S(2)}, u32[]{:S(2)}) collective-permute-start(bf16[64,2304]{1,0:T(8,128)(2,1)S(1)} %fusion.100), channel_id=1, source_target_pairs={{0,8},{2,10},{4,12},{6,14},{8,16},{10,18},{12,20},{14,22},{1,9},{3... | collective-permute-start | bytes 884744 | tf_op jit(solution)/shard_map/ppermute | solution.py:39
  320.0 4.4 %collective-permute-start.41 = (bf16[64,2304]{1,0:T(8,128)(2,1)S(1)}, bf16[64,2304]{1,0:T(8,128)(2,1)S(1)}, u32[]{:S(2)}, u32[]{:S(2)}) collective-permute-start(bf16[64,2304]{1,0:T(8,128)(2,1)S(1)} %fusion.87), channel_id=1, source_target_pairs={{0,8},{2,10},{4,12},{6,14},{8,16},{10,18},{12,20},{14,22},{1,9},{3... | collective-permute-start | bytes 884744 | tf_op jit(solution)/shard_map/ppermute | solution.py:39
  324.4 1.7 fusion.102
  326.8 2.4 collective-permute-done.41
  329.2 4.4 %collective-permute-start.34 = (bf16[64,2304]{1,0:T(8,128)(2,1)S(1)}, bf16[64,2304]{1,0:T(8,128)(2,1)S(1)}, u32[]{:S(2)}, u32[]{:S(2)}) collective-permute-start(bf16[64,2304]{1,0:T(8,128)(2,1)S(1)} %get-tuple-element.48), channel_id=1, source_target_pairs={{0,8},{2,10},{4,12},{6,14},{8,16},{10,18},{12,20},{14,22},{16,24},... | collective-permute-start | bytes 884744 | tf_op jit(solution)/shard_map/ppermute | solution.py:39
  333.6 1.7 fusion.89
  339.0 2.8 collective-permute-start.16
  343.1 1.9 collective-permute-done.16
  347.0 5.0 %collective-permute-start.17 = (bf16[64,3,512]{2,0,1:T(8,128)(2,1)S(1)}, bf16[64,3,512]{2,0,1:T(8,128)(2,1)S(1)}, u32[]{:S(2)}, u32[]{:S(2)}) collective-permute-start(bf16[64,3,512]{2,0,1:T(8,128)(2,1)S(1)} %fusion.117), channel_id=1, source_target_pairs={{0,8},{2,10},{4,12},{6,14},{8,16},{10,18},{12,20},{14,22},{1,9},{3... | collective-permute-start | bytes 589832 | tf_op jit(solution)/shard_map/ppermute | solution.py:39
  353.3 1.9 collective-permute-done.17
  355.1 4.6 %collective-permute-start.42 = (bf16[64,2304]{1,0:T(8,128)(2,1)S(1)}, bf16[64,2304]{1,0:T(8,128)(2,1)S(1)}, u32[]{:S(2)}, u32[]{:S(2)}) collective-permute-start(bf16[64,2304]{1,0:T(8,128)(2,1)S(1)} %get-tuple-element.46), channel_id=1, source_target_pairs={{0,8},{2,10},{4,12},{6,14},{8,16},{10,18},{12,20},{14,22},{16,24},... | collective-permute-start | bytes 884744 | tf_op jit(solution)/shard_map/ppermute | solution.py:39
  369.4 5.6 %collective-permute-start.18 = (bf16[64,3,512]{2,0,1:T(8,128)(2,1)S(1)}, bf16[64,3,512]{2,0,1:T(8,128)(2,1)S(1)}, u32[]{:S(2)}, u32[]{:S(2)}) collective-permute-start(bf16[64,3,512]{2,0,1:T(8,128)(2,1)S(1)} %get-tuple-element.50), channel_id=1, source_target_pairs={{0,8},{2,10},{4,12},{6,14},{8,16},{10,18},{12,20},{14,22},{16,24},... | collective-permute-start | bytes 589832 | tf_op jit(solution)/shard_map/ppermute | solution.py:39
  375.8 2.1 fusion.105
  382.2 2.1 fusion.92
  384.3 6.9 %collective-permute-done.21 = bf16[64,3,512]{2,0,1:T(8,128)(2,1)S(1)} collective-permute-done((bf16[64,3,512]{2,0,1:T(8,128)(2,1)S(1)}, bf16[64,3,512]{2,0,1:T(8,128)(2,1)S(1)}, u32[]{:S(2)}, u32[]{:S(2)}) %collective-permute-start.21) | collective-permute-done | bytes 196640 | tf_op jit(solution)/shard_map/ppermute | solution.py:39
  391.3 1.8 fusion.122
  393.1 2.0 fusion.79
  (214 shorter events, 77.7 us)
Async XLA Ops:
  0.6 16.7 %copy-start = (bf16[1,512,1024]{2,1,0:T(8,128)(2,1)S(1)}, bf16[1,512,1024]{2,1,0:T(8,128)(2,1)}, u32[]{:S(2)}) copy-start(bf16[1,512,1024]{2,1,0:T(8,128)(2,1)} %param.15) | copy-start | bytes 3145732
  9.8 9.6 %copy-start.8 = (f32[1,512,512]{2,1,0:T(8,128)}, f32[1,512,512]{2,1,0:T(8,128)S(1)}, u32[]{:S(2)}) copy-start(f32[1,512,512]{2,1,0:T(8,128)S(1)} %bitcast_multiply_fusion.6) | copy-start | bytes 3145732
  9.9 6.2 %collective-permute-start = (f32[1,2,512]{2,1,0:T(2,128)S(1)}, f32[1,2,512]{2,1,0:T(2,128)S(1)}, u32[]{:S(2)}, u32[]{:S(2)}) collective-permute-start(f32[1,2,512]{2,1,0:T(2,128)S(1)} %slice.78), channel_id=1, source_target_pairs={{0,2},{2,4},{4,6},{6,8},{8,10},{10,12},{12,14},{14,16},{16,18},{18... | collective-permute-start | bytes 12296 | tf_op jit(solution)/shard_map/ppermute | solution.py:12
  19.4 5.2 %collective-permute-start.1 = (f32[512,1024]{1,0:T(8,128)}, f32[512,1024]{1,0:T(8,128)}, u32[]{:S(2)}, u32[]{:S(2)}) collective-permute-start(f32[512,1024]{1,0:T(8,128)} %fusion.72), channel_id=1, source_target_pairs={{0,1},{1,0},{2,3},{3,2},{4,5},{5,4},{6,7},{7,6},{8,9},{9,8},{10,11... | collective-permute-start | bytes 6291464 | tf_op jit(solution)/shard_map/ppermute | solution.py:24
  27.6 15.6 %slice-start = ((s8[4718592]{0:T(1024)(128)(4,1)}), s8[4194304]{0:T(1024)(128)(4,1)S(1)}, s32[]{:S(2)}) async-start(s8[4718592]{0:T(1024)(128)(4,1)} %bitcast.715), calls=%async_computation | async-start | bytes 8388608
  27.6 23.0 %slice-start.2 = ((s8[4718592]{0:T(1024)(128)(4,1)}), s8[4194304]{0:T(1024)(128)(4,1)S(1)}, s32[]{:S(2)}) async-start(s8[4718592]{0:T(1024)(128)(4,1)} %bitcast.717), calls=%async_computation.2 | async-start | bytes 8388608
  34.6 8.6 %slice-start.1 = ((s8[4718592]{0:T(1024)(128)(4,1)}), s8[524288]{0:T(1024)(128)(4,1)S(1)}, s32[]{:S(2)}) async-start(s8[4718592]{0:T(1024)(128)(4,1)} %bitcast.715), calls=%async_computation.1 | async-start | bytes 1048576
  34.6 16.0 %slice-start.3 = ((s8[4718592]{0:T(1024)(128)(4,1)}), s8[524288]{0:T(1024)(128)(4,1)S(1)}, s32[]{:S(2)}) async-start(s8[4718592]{0:T(1024)(128)(4,1)} %bitcast.717), calls=%async_computation.3 | async-start | bytes 1048576
  50.6 41.4 %copy-start.7 = (bf16[2304,1024]{1,0:T(8,128)(2,1)}, bf16[2304,1024]{1,0:T(8,128)(2,1)S(1)}, u32[]{:S(2)}) copy-start(bf16[2304,1024]{1,0:T(8,128)(2,1)S(1)} %convolution_convert_fusion) | copy-start | bytes 14155780
  56.6 36.9 %collective-permute-start.3 = (f32[512,1024]{1,0:T(8,128)S(1)}, f32[512,1024]{1,0:T(8,128)S(1)}, u32[]{:S(2)}, u32[]{:S(2)}) collective-permute-start(f32[512,1024]{1,0:T(8,128)S(1)} %fusion.49), channel_id=1, source_target_pairs={{0,1},{1,0},{2,3},{3,2},{4,5},{5,4},{6,7},{7,6},{8,9},{9,8},{10,11... | collective-permute-start | bytes 6291464 | tf_op jit(solution)/shard_map/ppermute | solution.py:24
  57.1 42.7 %collective-permute-start.2 = (bf16[512,1024]{1,0:T(8,128)(2,1)S(1)}, bf16[512,1024]{1,0:T(8,128)(2,1)S(1)}, u32[]{:S(2)}, u32[]{:S(2)}) collective-permute-start(bf16[512,1024]{1,0:T(8,128)(2,1)S(1)} %fusion.52), channel_id=1, source_target_pairs={{0,1},{1,0},{2,3},{3,2},{4,5},{5,4},{6,7},{7,6},{8,9},{9,8},{10,11... | collective-permute-start | bytes 3145736 | tf_op jit(solution)/shard_map/ppermute | solution.py:29
  58.4 31.9 %collective-permute-start.46 = (bf16[2,2,144,1024]{3,2,1,0:T(8,128)(2,1)S(1)}, bf16[2,2,144,1024]{3,2,1,0:T(8,128)(2,1)S(1)}, u32[]{:S(2)}, u32[]{:S(2)}) collective-permute-start(bf16[2,2,144,1024]{3,2,1,0:T(8,128)(2,1)S(1)} %get-tuple-element.54), channel_id=1, source_target_pairs={{0,8},{2,10},{4,12},{6,14},{1,9},{3,11},{5,13},{7,15}} | collective-permute-start | bytes 3538952 | tf_op jit(solution)/shard_map/ppermute | solution.py:39
  70.7 70.6 %collective-permute-start.30 = (bf16[4,2,64,2304]{3,2,1,0:T(8,128)(2,1)}, bf16[4,2,64,2304]{3,2,1,0:T(8,128)(2,1)}, u32[]{:S(2)}, u32[]{:S(2)}) collective-permute-start(bf16[4,2,64,2304]{3,2,1,0:T(8,128)(2,1)} %dynamic-slice_bitcast_fusion.1), channel_id=1, source_target_pairs={{0,2},{2,0},{4,6},{6,4},{8,10},{10,8},{12,14},{14,12},{16,18},{18,... | collective-permute-start | bytes 7077896 | tf_op jit(solution)/shard_map/ppermute | solution.py:71
  76.6 68.4 %collective-permute-start.38 = (bf16[4,2,64,2304]{3,2,1,0:T(8,128)(2,1)}, bf16[4,2,64,2304]{3,2,1,0:T(8,128)(2,1)}, u32[]{:S(2)}, u32[]{:S(2)}) collective-permute-start(bf16[4,2,64,2304]{3,2,1,0:T(8,128)(2,1)} %dynamic-slice_bitcast_fusion), channel_id=1, source_target_pairs={{0,4},{2,6},{4,0},{6,2},{8,12},{10,14},{12,8},{14,10},{16,20},{18,... | collective-permute-start | bytes 7077896 | tf_op jit(solution)/shard_map/ppermute | solution.py:71
  90.3 57.6 %collective-permute-start.49 = (bf16[2,2,144,1024]{3,2,1,0:T(8,128)(2,1)}, bf16[2,2,144,1024]{3,2,1,0:T(8,128)(2,1)}, u32[]{:S(2)}, u32[]{:S(2)}) collective-permute-start(bf16[2,2,144,1024]{3,2,1,0:T(8,128)(2,1)} %get-tuple-element.55), channel_id=1, source_target_pairs={{24,16},{26,18},{28,20},{30,22},{25,17},{27,19},{29,21},{31,23}} | collective-permute-start | bytes 3538952 | tf_op jit(solution)/shard_map/ppermute | solution.py:39
  93.5 56.5 %collective-permute-start.47 = (bf16[2,2,144,1024]{3,2,1,0:T(8,128)(2,1)}, bf16[2,2,144,1024]{3,2,1,0:T(8,128)(2,1)}, u32[]{:S(2)}, u32[]{:S(2)}) collective-permute-start(bf16[2,2,144,1024]{3,2,1,0:T(8,128)(2,1)} %fusion.18), channel_id=1, source_target_pairs={{0,8},{2,10},{4,12},{6,14},{8,16},{10,18},{12,20},{14,22},{1,9},{3... | collective-permute-start | bytes 3538952 | tf_op jit(solution)/shard_map/ppermute | solution.py:39
  105.4 18.9 %collective-permute-start.4 = (f32[1,2,512]{2,1,0:T(2,128)S(1)}, f32[1,2,512]{2,1,0:T(2,128)S(1)}, u32[]{:S(2)}, u32[]{:S(2)}) collective-permute-start(f32[1,2,512]{2,1,0:T(2,128)S(1)} %slice.83), channel_id=1, source_target_pairs={{2,0},{4,2},{6,4},{8,6},{10,8},{12,10},{14,12},{16,14},{18,16},{20... | collective-permute-start | bytes 12296 | tf_op jit(solution)/shard_map/ppermute | solution.py:12
  124.4 31.9 %collective-permute-start.22 = (bf16[4,2,32,1024]{3,2,1,0:T(8,128)(2,1)}, bf16[4,2,32,1024]{3,2,1,0:T(8,128)(2,1)}, u32[]{:S(2)}, u32[]{:S(2)}) collective-permute-start(bf16[4,2,32,1024]{3,2,1,0:T(8,128)(2,1)} %dynamic-slice_bitcast_fusion.4), channel_id=1, source_target_pairs={{0,4},{2,6},{4,0},{6,2},{8,12},{10,14},{12,8},{14,10},{16,20},{18,... | collective-permute-start | bytes 1572872 | tf_op jit(solution)/shard_map/ppermute | solution.py:71
  142.0 16.8 %collective-permute-start.5 = (bf16[512,1024]{1,0:T(8,128)(2,1)S(1)}, bf16[512,1024]{1,0:T(8,128)(2,1)S(1)}, u32[]{:S(2)}, u32[]{:S(2)}) collective-permute-start(bf16[512,1024]{1,0:T(8,128)(2,1)S(1)} %copy-done.17), channel_id=1, source_target_pairs={{0,1},{1,0},{2,3},{3,2},{4,5},{5,4},{6,7},{7,6},{8,9},{9,8},{10,11... | collective-permute-start | bytes 3145736 | tf_op jit(solution)/shard_map/ppermute | solution.py:29
  145.0 147.4 %collective-permute-start.14 = (bf16[4,2,64,3,512]{4,2,3,1,0:T(8,128)(2,1)}, bf16[4,2,64,3,512]{4,2,3,1,0:T(8,128)(2,1)}, u32[]{:S(2)}, u32[]{:S(2)}) collective-permute-start(bf16[4,2,64,3,512]{4,2,3,1,0:T(8,128)(2,1)} %copy_bitcast_fusion), channel_id=1, source_target_pairs={{0,2},{2,0},{4,6},{6,4},{8,10},{10,8},{12,14},{14,12},{16,18},{18,... | collective-permute-start | bytes 4718600 | tf_op jit(solution)/shard_map/ppermute | solution.py:71
  147.9 10.9 %copy-start.5 = (bf16[1,512,1024]{2,1,0:T(8,128)(2,1)S(1)}, bf16[1,512,1024]{2,1,0:T(8,128)(2,1)}, u32[]{:S(2)}) copy-start(bf16[1,512,1024]{2,1,0:T(8,128)(2,1)} %param.10) | copy-start | bytes 3145732
  147.9 133.7 %collective-permute-start.31 = (bf16[4,64,2304]{2,1,0:T(8,128)(2,1)}, bf16[4,64,2304]{2,1,0:T(8,128)(2,1)}, u32[]{:S(2)}, u32[]{:S(2)}) collective-permute-start(bf16[4,64,2304]{2,1,0:T(8,128)(2,1)} %fusion.21), channel_id=1, source_target_pairs={{0,4},{2,6},{4,0},{6,2},{8,12},{10,14},{12,8},{14,10},{16,20},{18,... | collective-permute-start | bytes 3538952 | tf_op jit(solution)/shard_map/ppermute | solution.py:71
  150.0 136.8 %collective-permute-start.39 = (bf16[4,64,2304]{2,1,0:T(8,128)(2,1)}, bf16[4,64,2304]{2,1,0:T(8,128)(2,1)}, u32[]{:S(2)}, u32[]{:S(2)}) collective-permute-start(bf16[4,64,2304]{2,1,0:T(8,128)(2,1)} %fusion.20), channel_id=1, source_target_pairs={{0,2},{2,0},{4,6},{6,4},{8,10},{10,8},{12,14},{14,12},{16,18},{18,... | collective-permute-start | bytes 3538952 | tf_op jit(solution)/shard_map/ppermute | solution.py:71
  158.1 54.9 %collective-permute-start.23 = (bf16[4,32,1024]{2,1,0:T(8,128)(2,1)}, bf16[4,32,1024]{2,1,0:T(8,128)(2,1)S(1)}, u32[]{:S(2)}, u32[]{:S(2)}) collective-permute-start(bf16[4,32,1024]{2,1,0:T(8,128)(2,1)} %fusion.107), channel_id=1, source_target_pairs={{0,2},{2,0},{4,6},{6,4},{8,10},{10,8},{12,14},{14,12},{16,18},{18,... | collective-permute-start | bytes 786440 | tf_op jit(solution)/shard_map/ppermute | solution.py:71
  159.8 84.6 %copy-start.6 = (bf16[1,512,1024]{2,1,0:T(8,128)(2,1)S(1)}, bf16[1,512,1024]{2,1,0:T(8,128)(2,1)}, u32[]{:S(2)}) copy-start(bf16[1,512,1024]{2,1,0:T(8,128)(2,1)} %param.10) | copy-start | bytes 3145732
  160.0 55.4 %collective-permute-start.6 = (f32[4,2,1,224]{3,2,1,0:T(1,128)S(1)}, f32[4,2,1,224]{3,2,1,0:T(1,128)S(1)}, u32[]{:S(2)}, u32[]{:S(2)}) collective-permute-start(f32[4,2,1,224]{3,2,1,0:T(1,128)S(1)} %fusion.138), channel_id=1, source_target_pairs={{0,2},{2,0},{4,6},{6,4},{8,10},{10,8},{12,14},{14,12},{16,18},{18,... | collective-permute-start | bytes 21512 | tf_op jit(solution)/shard_map/ppermute | solution.py:71
  213.9 3.4 collective-permute-start.24
  215.4 7.0 %collective-permute-start.7 = (f32[4,1,224]{2,1,0:T(1,128)S(1)}, f32[4,1,224]{2,1,0:T(1,128)S(1)}, u32[]{:S(2)}, u32[]{:S(2)}) collective-permute-start(f32[4,1,224]{2,1,0:T(1,128)S(1)} %fusion.140), channel_id=1, source_target_pairs={{0,4},{2,6},{4,0},{6,2},{8,12},{10,14},{12,8},{14,10},{16,20},{18,... | collective-permute-start | bytes 10760 | tf_op jit(solution)/shard_map/ppermute | solution.py:71
  218.2 6.2 %collective-permute-start.25 = (bf16[32,1024]{1,0:T(8,128)(2,1)S(1)}, bf16[32,1024]{1,0:T(8,128)(2,1)S(1)}, u32[]{:S(2)}, u32[]{:S(2)}) collective-permute-start(bf16[32,1024]{1,0:T(8,128)(2,1)S(1)} %fusion.132), channel_id=1, source_target_pairs={{0,8},{2,10},{4,12},{6,14},{8,16},{10,18},{12,20},{14,22},{1,9},{3... | collective-permute-start | bytes 196616 | tf_op jit(solution)/shard_map/ppermute | solution.py:39
  222.5 3.6 collective-permute-start.8
  225.5 4.9 %collective-permute-start.27 = (bf16[32,1024]{1,0:T(8,128)(2,1)S(1)}, bf16[32,1024]{1,0:T(8,128)(2,1)S(1)}, u32[]{:S(2)}, u32[]{:S(2)}) collective-permute-start(bf16[32,1024]{1,0:T(8,128)(2,1)S(1)} %get-tuple-element.59), channel_id=1, source_target_pairs={{24,16},{26,18},{28,20},{30,22},{25,17},{27,19},{29,21},{31,23}} | collective-permute-start | bytes 196616 | tf_op jit(solution)/shard_map/ppermute | solution.py:39
  226.2 5.8 %collective-permute-start.9 = (f32[1,224]{1,0:T(1,128)S(1)}, f32[1,224]{1,0:T(1,128)S(1)}, u32[]{:S(2)}, u32[]{:S(2)}) collective-permute-start(f32[1,224]{1,0:T(1,128)S(1)} %fusion.157), channel_id=1, source_target_pairs={{0,8},{2,10},{4,12},{6,14},{8,16},{10,18},{12,20},{14,22},{1,9},{3... | collective-permute-start | bytes 2696 | tf_op jit(solution)/shard_map/ppermute | solution.py:39
  231.3 1.4 collective-permute-start.28
  232.0 1.6 collective-permute-start.11
  233.6 9.5 %collective-permute-start.12 = (f32[1,224]{1,0:T(1,128)S(1)}, f32[1,224]{1,0:T(1,128)S(1)}, u32[]{:S(2)}, u32[]{:S(2)}) collective-permute-start(f32[1,224]{1,0:T(1,128)S(1)} %fusion.174), channel_id=1, source_target_pairs={{16,8},{18,10},{20,12},{22,14},{24,16},{26,18},{28,20},{30,22},{17... | collective-permute-start | bytes 2696 | tf_op jit(solution)/shard_map/ppermute | solution.py:39
  234.3 13.7 %collective-permute-start.10 = (f32[1,224]{1,0:T(1,128)S(1)}, f32[1,224]{1,0:T(1,128)S(1)}, u32[]{:S(2)}, u32[]{:S(2)}) collective-permute-start(f32[1,224]{1,0:T(1,128)S(1)} %get-tuple-element.61), channel_id=1, source_target_pairs={{0,8},{2,10},{4,12},{6,14},{8,16},{10,18},{12,20},{14,22},{16,24},... | collective-permute-start | bytes 2696 | tf_op jit(solution)/shard_map/ppermute | solution.py:39
  243.2 6.4 %collective-permute-start.13 = (f32[1,224]{1,0:T(1,128)S(1)}, f32[1,224]{1,0:T(1,128)S(1)}, u32[]{:S(2)}, u32[]{:S(2)}) collective-permute-start(f32[1,224]{1,0:T(1,128)S(1)} %fusion.168), channel_id=1, source_target_pairs={{8,0},{10,2},{12,4},{14,6},{16,8},{18,10},{20,12},{22,14},{24,16},... | collective-permute-start | bytes 2696 | tf_op jit(solution)/shard_map/ppermute | solution.py:39
  248.0 41.3 %collective-permute-start.50 = (bf16[2,2,144,1024]{3,2,1,0:T(8,128)(2,1)}, bf16[2,2,144,1024]{3,2,1,0:T(8,128)(2,1)S(1)}, u32[]{:S(2)}, u32[]{:S(2)}) collective-permute-start(bf16[2,2,144,1024]{3,2,1,0:T(8,128)(2,1)} %get-tuple-element.53), channel_id=1, source_target_pairs={{16,8},{18,10},{20,12},{22,14},{24,16},{26,18},{28,20},{30,22},{17... | collective-permute-start | bytes 3538952 | tf_op jit(solution)/shard_map/ppermute | solution.py:39
  249.6 7.2 %collective-permute-start.26 = (bf16[32,1024]{1,0:T(8,128)(2,1)S(1)}, bf16[32,1024]{1,0:T(8,128)(2,1)S(1)}, u32[]{:S(2)}, u32[]{:S(2)}) collective-permute-start(bf16[32,1024]{1,0:T(8,128)(2,1)S(1)} %get-tuple-element.58), channel_id=1, source_target_pairs={{0,8},{2,10},{4,12},{6,14},{8,16},{10,18},{12,20},{14,22},{16,24},... | collective-permute-start | bytes 196616 | tf_op jit(solution)/shard_map/ppermute | solution.py:39
  256.8 6.8 %collective-permute-start.29 = (bf16[32,1024]{1,0:T(8,128)(2,1)S(1)}, bf16[32,1024]{1,0:T(8,128)(2,1)S(1)}, u32[]{:S(2)}, u32[]{:S(2)}) collective-permute-start(bf16[32,1024]{1,0:T(8,128)(2,1)S(1)} %fusion.129), channel_id=1, source_target_pairs={{8,0},{10,2},{12,4},{14,6},{16,8},{18,10},{20,12},{22,14},{24,16},... | collective-permute-start | bytes 196616 | tf_op jit(solution)/shard_map/ppermute | solution.py:39
  263.5 99.4 %collective-permute-start.48 = (bf16[2,2,144,1024]{3,2,1,0:T(8,128)(2,1)}, bf16[2,2,144,1024]{3,2,1,0:T(8,128)(2,1)S(1)}, u32[]{:S(2)}, u32[]{:S(2)}) collective-permute-start(bf16[2,2,144,1024]{3,2,1,0:T(8,128)(2,1)} %get-tuple-element.52), channel_id=1, source_target_pairs={{0,8},{2,10},{4,12},{6,14},{8,16},{10,18},{12,20},{14,22},{16,24},... | collective-permute-start | bytes 3538952 | tf_op jit(solution)/shard_map/ppermute | solution.py:39
  282.9 9.5 %copy-start.15 = (bf16[1024,3,512]{2,0,1:T(8,128)(2,1)S(1)}, bf16[1024,3,512]{2,0,1:T(8,128)(2,1)}, u32[]{:S(2)}) copy-start(bf16[1024,3,512]{2,0,1:T(8,128)(2,1)} %copy-done.14) | copy-start | bytes 9437188
  282.9 29.9 %collective-permute-start.32 = (bf16[64,2304]{1,0:T(8,128)(2,1)S(1)}, bf16[64,2304]{1,0:T(8,128)(2,1)S(1)}, u32[]{:S(2)}, u32[]{:S(2)}) collective-permute-start(bf16[64,2304]{1,0:T(8,128)(2,1)S(1)} %fusion.98), channel_id=1, source_target_pairs={{0,8},{2,10},{4,12},{6,14},{1,9},{3,11},{5,13},{7,15}} | collective-permute-start | bytes 884744 | tf_op jit(solution)/shard_map/ppermute | solution.py:39
  288.0 30.7 %collective-permute-start.40 = (bf16[64,2304]{1,0:T(8,128)(2,1)S(1)}, bf16[64,2304]{1,0:T(8,128)(2,1)S(1)}, u32[]{:S(2)}, u32[]{:S(2)}) collective-permute-start(bf16[64,2304]{1,0:T(8,128)(2,1)S(1)} %fusion.85), channel_id=1, source_target_pairs={{0,8},{2,10},{4,12},{6,14},{1,9},{3,11},{5,13},{7,15}} | collective-permute-start | bytes 884744 | tf_op jit(solution)/shard_map/ppermute | solution.py:39
  291.1 73.1 %collective-permute-start.51 = (bf16[2,2,144,1024]{3,2,1,0:T(8,128)(2,1)S(1)}, bf16[2,2,144,1024]{3,2,1,0:T(8,128)(2,1)S(1)}, u32[]{:S(2)}, u32[]{:S(2)}) collective-permute-start(bf16[2,2,144,1024]{3,2,1,0:T(8,128)(2,1)S(1)} %fusion.17), channel_id=1, source_target_pairs={{8,0},{10,2},{12,4},{14,6},{16,8},{18,10},{20,12},{22,14},{24,16},... | collective-permute-start | bytes 3538952 | tf_op jit(solution)/shard_map/ppermute | solution.py:39
  293.8 43.4 %collective-permute-start.15 = (bf16[4,64,3,512]{3,1,2,0:T(8,128)(2,1)S(1)}, bf16[4,64,3,512]{3,1,2,0:T(8,128)(2,1)S(1)}, u32[]{:S(2)}, u32[]{:S(2)}) collective-permute-start(bf16[4,64,3,512]{3,1,2,0:T(8,128)(2,1)S(1)} %fusion.47), channel_id=1, source_target_pairs={{0,4},{2,6},{4,0},{6,2},{8,12},{10,14},{12,8},{14,10},{16,20},{18,... | collective-permute-start | bytes 2359304 | tf_op jit(solution)/shard_map/ppermute | solution.py:71
  314.1 10.3 %collective-permute-start.33 = (bf16[64,2304]{1,0:T(8,128)(2,1)S(1)}, bf16[64,2304]{1,0:T(8,128)(2,1)S(1)}, u32[]{:S(2)}, u32[]{:S(2)}) collective-permute-start(bf16[64,2304]{1,0:T(8,128)(2,1)S(1)} %fusion.100), channel_id=1, source_target_pairs={{0,8},{2,10},{4,12},{6,14},{8,16},{10,18},{12,20},{14,22},{1,9},{3... | collective-permute-start | bytes 884744 | tf_op jit(solution)/shard_map/ppermute | solution.py:39
  320.0 9.2 %collective-permute-start.41 = (bf16[64,2304]{1,0:T(8,128)(2,1)S(1)}, bf16[64,2304]{1,0:T(8,128)(2,1)S(1)}, u32[]{:S(2)}, u32[]{:S(2)}) collective-permute-start(bf16[64,2304]{1,0:T(8,128)(2,1)S(1)} %fusion.87), channel_id=1, source_target_pairs={{0,8},{2,10},{4,12},{6,14},{8,16},{10,18},{12,20},{14,22},{1,9},{3... | collective-permute-start | bytes 884744 | tf_op jit(solution)/shard_map/ppermute | solution.py:39
  326.1 9.1 %collective-permute-start.35 = (bf16[64,2304]{1,0:T(8,128)(2,1)S(1)}, bf16[64,2304]{1,0:T(8,128)(2,1)S(1)}, u32[]{:S(2)}, u32[]{:S(2)}) collective-permute-start(bf16[64,2304]{1,0:T(8,128)(2,1)S(1)} %get-tuple-element.49), channel_id=1, source_target_pairs={{24,16},{26,18},{28,20},{30,22},{25,17},{27,19},{29,21},{31,23}} | collective-permute-start | bytes 884744 | tf_op jit(solution)/shard_map/ppermute | solution.py:39
  329.2 40.3 %collective-permute-start.34 = (bf16[64,2304]{1,0:T(8,128)(2,1)S(1)}, bf16[64,2304]{1,0:T(8,128)(2,1)S(1)}, u32[]{:S(2)}, u32[]{:S(2)}) collective-permute-start(bf16[64,2304]{1,0:T(8,128)(2,1)S(1)} %get-tuple-element.48), channel_id=1, source_target_pairs={{0,8},{2,10},{4,12},{6,14},{8,16},{10,18},{12,20},{14,22},{16,24},... | collective-permute-start | bytes 884744 | tf_op jit(solution)/shard_map/ppermute | solution.py:39
  335.3 3.7 collective-permute-start.43
  337.3 9.7 %collective-permute-start.36 = (bf16[64,2304]{1,0:T(8,128)(2,1)S(1)}, bf16[64,2304]{1,0:T(8,128)(2,1)S(1)}, u32[]{:S(2)}, u32[]{:S(2)}) collective-permute-start(bf16[64,2304]{1,0:T(8,128)(2,1)S(1)} %fusion.95), channel_id=1, source_target_pairs={{16,8},{18,10},{20,12},{22,14},{24,16},{26,18},{28,20},{30,22},{17... | collective-permute-start | bytes 884744 | tf_op jit(solution)/shard_map/ppermute | solution.py:39
  339.0 6.0 %collective-permute-start.16 = (bf16[64,3,512]{2,0,1:T(8,128)(2,1)S(1)}, bf16[64,3,512]{2,0,1:T(8,128)(2,1)S(1)}, u32[]{:S(2)}, u32[]{:S(2)}) collective-permute-start(bf16[64,3,512]{2,0,1:T(8,128)(2,1)S(1)} %fusion.115), channel_id=1, source_target_pairs={{0,8},{2,10},{4,12},{6,14},{1,9},{3,11},{5,13},{7,15}} | collective-permute-start | bytes 589832 | tf_op jit(solution)/shard_map/ppermute | solution.py:39
  344.9 16.0 %collective-permute-start.44 = (bf16[64,2304]{1,0:T(8,128)(2,1)S(1)}, bf16[64,2304]{1,0:T(8,128)(2,1)S(1)}, u32[]{:S(2)}, u32[]{:S(2)}) collective-permute-start(bf16[64,2304]{1,0:T(8,128)(2,1)S(1)} %fusion.82), channel_id=1, source_target_pairs={{16,8},{18,10},{20,12},{22,14},{24,16},{26,18},{28,20},{30,22},{17... | collective-permute-start | bytes 884744 | tf_op jit(solution)/shard_map/ppermute | solution.py:39
  347.0 8.2 %collective-permute-start.17 = (bf16[64,3,512]{2,0,1:T(8,128)(2,1)S(1)}, bf16[64,3,512]{2,0,1:T(8,128)(2,1)S(1)}, u32[]{:S(2)}, u32[]{:S(2)}) collective-permute-start(bf16[64,3,512]{2,0,1:T(8,128)(2,1)S(1)} %fusion.117), channel_id=1, source_target_pairs={{0,8},{2,10},{4,12},{6,14},{8,16},{10,18},{12,20},{14,22},{1,9},{3... | collective-permute-start | bytes 589832 | tf_op jit(solution)/shard_map/ppermute | solution.py:39
  355.1 27.1 %collective-permute-start.42 = (bf16[64,2304]{1,0:T(8,128)(2,1)S(1)}, bf16[64,2304]{1,0:T(8,128)(2,1)S(1)}, u32[]{:S(2)}, u32[]{:S(2)}) collective-permute-start(bf16[64,2304]{1,0:T(8,128)(2,1)S(1)} %get-tuple-element.46), channel_id=1, source_target_pairs={{0,8},{2,10},{4,12},{6,14},{8,16},{10,18},{12,20},{14,22},{16,24},... | collective-permute-start | bytes 884744 | tf_op jit(solution)/shard_map/ppermute | solution.py:39
  360.9 6.0 %collective-permute-start.19 = (bf16[64,3,512]{2,0,1:T(8,128)(2,1)S(1)}, bf16[64,3,512]{2,0,1:T(8,128)(2,1)S(1)}, u32[]{:S(2)}, u32[]{:S(2)}) collective-permute-start(bf16[64,3,512]{2,0,1:T(8,128)(2,1)S(1)} %get-tuple-element.51), channel_id=1, source_target_pairs={{24,16},{26,18},{28,20},{30,22},{25,17},{27,19},{29,21},{31,23}} | collective-permute-start | bytes 589832 | tf_op jit(solution)/shard_map/ppermute | solution.py:39
  362.9 12.2 %collective-permute-start.37 = (bf16[64,2304]{1,0:T(8,128)(2,1)S(1)}, bf16[64,2304]{1,0:T(8,128)(2,1)S(1)}, u32[]{:S(2)}, u32[]{:S(2)}) collective-permute-start(bf16[64,2304]{1,0:T(8,128)(2,1)S(1)} %fusion.97), channel_id=1, source_target_pairs={{8,0},{10,2},{12,4},{14,6},{16,8},{18,10},{20,12},{22,14},{24,16},... | collective-permute-start | bytes 884744 | tf_op jit(solution)/shard_map/ppermute | solution.py:39
  364.2 18.0 %collective-permute-start.45 = (bf16[64,2304]{1,0:T(8,128)(2,1)S(1)}, bf16[64,2304]{1,0:T(8,128)(2,1)S(1)}, u32[]{:S(2)}, u32[]{:S(2)}) collective-permute-start(bf16[64,2304]{1,0:T(8,128)(2,1)S(1)} %fusion.84), channel_id=1, source_target_pairs={{8,0},{10,2},{12,4},{14,6},{16,8},{18,10},{20,12},{22,14},{24,16},... | collective-permute-start | bytes 884744 | tf_op jit(solution)/shard_map/ppermute | solution.py:39
  366.9 13.3 %collective-permute-start.52 = (bf16[2,144,1024]{2,1,0:T(8,128)(2,1)S(1)}, bf16[2,144,1024]{2,1,0:T(8,128)(2,1)S(1)}, u32[]{:S(2)}, u32[]{:S(2)}) collective-permute-start(bf16[2,144,1024]{2,1,0:T(8,128)(2,1)S(1)} %fusion.55), channel_id=1, source_target_pairs={{0,4},{2,6},{4,0},{6,2},{8,12},{10,14},{12,8},{14,10},{16,20},{18,... | collective-permute-start | bytes 1769480 | tf_op jit(solution)/shard_map/ppermute | solution.py:71
  369.4 14.9 %collective-permute-start.18 = (bf16[64,3,512]{2,0,1:T(8,128)(2,1)S(1)}, bf16[64,3,512]{2,0,1:T(8,128)(2,1)S(1)}, u32[]{:S(2)}, u32[]{:S(2)}) collective-permute-start(bf16[64,3,512]{2,0,1:T(8,128)(2,1)S(1)} %get-tuple-element.50), channel_id=1, source_target_pairs={{0,8},{2,10},{4,12},{6,14},{8,16},{10,18},{12,20},{14,22},{16,24},... | collective-permute-start | bytes 589832 | tf_op jit(solution)/shard_map/ppermute | solution.py:39
  375.1 2.8 collective-permute-start.20
  379.0 12.3 %collective-permute-start.21 = (bf16[64,3,512]{2,0,1:T(8,128)(2,1)S(1)}, bf16[64,3,512]{2,0,1:T(8,128)(2,1)S(1)}, u32[]{:S(2)}, u32[]{:S(2)}) collective-permute-start(bf16[64,3,512]{2,0,1:T(8,128)(2,1)S(1)} %fusion.114), channel_id=1, source_target_pairs={{8,0},{10,2},{12,4},{14,6},{16,8},{18,10},{20,12},{22,14},{24,16},... | collective-permute-start | bytes 589832 | tf_op jit(solution)/shard_map/ppermute | solution.py:39
  381.4 11.6 %collective-permute-start.53 = (bf16[144,1024]{1,0:T(8,128)(2,1)S(1)}, bf16[144,1024]{1,0:T(8,128)(2,1)S(1)}, u32[]{:S(2)}, u32[]{:S(2)}) collective-permute-start(bf16[144,1024]{1,0:T(8,128)(2,1)S(1)} %fusion.77), channel_id=1, source_target_pairs={{0,2},{2,0},{4,6},{6,4},{8,10},{10,8},{12,14},{14,12},{16,18},{18,... | collective-permute-start | bytes 884744 | tf_op jit(solution)/shard_map/ppermute | solution.py:71
  (25 other events, 89.4 us)

commit v2 on v1

--- a/solution.py
+++ b/solution.py
@@ -1,6 +1,10 @@
+import functools
+
 import jax
 import jax.numpy as jnp
 from jax import lax
+from jax.experimental import pallas as pl
+from jax.experimental.pallas import tpu as pltpu
 from jax.sharding import PartitionSpec as P
 
 EPSILON = 1e-05
@@ -85,6 +89,150 @@
     return sum(part.astype(jnp.float32) for part, _ in parts)
 
 
+MESH = pl.DeviceIdType.MESH
+VMEM_BYTES = 67043328
+
+
+class Unit:
+    def __init__(self, member, start, width, x_first):
+        self.member, self.start, self.width, self.x_first = member, start, width, x_first
+
+
+def device_of(z, y, x):
+    return {"seq": z * 4 + y * 2 + x}
+
+
+def scatter_kernel(units, members, *refs):
+    part_refs, out_refs = refs[:members], refs[members : 2 * members]
+    refs = refs[2 * members :]
+    count = len(units)
+    first, second, third = refs[:count], refs[count : 2 * count], refs[2 * count : 3 * count]
+    send1, recv1, send2, recv2, send3, recv3 = refs[3 * count :]
+    me = lax.axis_index("seq")
+    z, y, x = me // 4, (me // 2) % 2, me % 2
+
+    def own(u, at_z, at_y, at_x):
+        unit = units[u]
+        return part_refs[unit.member].at[at_z, at_y, at_x, :, pl.ds(unit.start, unit.width)]
+
+    def stage1(u):
+        unit = units[u]
+        cols = pl.ds(unit.start, unit.width)
+        if unit.x_first:
+            source, target = part_refs[unit.member].at[:, :, 1 - x, :, cols], device_of(z, y, 1 - x)
+        else:
+            source, target = part_refs[unit.member].at[:, 1 - y, :, :, cols], device_of(z, 1 - y, x)
+        return pltpu.make_async_remote_copy(
+            source, first[u], send1.at[u], recv1.at[u], device_id=target, device_id_type=MESH
+        )
+
+    def stage2(u):
+        unit = units[u]
+        if unit.x_first:
+            source, target = first[u].at[:, 1 - y], device_of(z, 1 - y, x)
+        else:
+            source, target = first[u].at[:, 1 - x], device_of(z, y, 1 - x)
+        return pltpu.make_async_remote_copy(
+            source, second[u], send2.at[u], recv2.at[u], device_id=target, device_id_type=MESH
+        )
+
+    def stage3(u, d):
+        other = (z + d) % 4
+        return pltpu.make_async_remote_copy(
+            second[u].at[other], third[u].at[d - 1], send3.at[u, d - 1], recv3.at[u, d - 1],
+            device_id=device_of(other, y, x), device_id_type=MESH,
+        )
+
+    def run2(u):
+        unit = units[u]
+        stage1(u).wait_recv()
+
+        @pl.loop(0, 4)
+        def _(at):
+            if unit.x_first:
+                mine, spot = own(u, at, 1 - y, x), first[u].at[at, 1 - y]
+            else:
+                mine, spot = own(u, at, y, 1 - x), first[u].at[at, 1 - x]
+            spot[...] = (mine[...].astype(jnp.float32) + spot[...].astype(jnp.float32)).astype(spot.dtype)
+
+        stage2(u).start()
+
+    def kept(u, at):
+        unit = units[u]
+        near = first[u].at[at, y if unit.x_first else x]
+        return (
+            own(u, at, y, x)[...].astype(jnp.float32)
+            + near[...].astype(jnp.float32)
+            + second[u].at[at][...].astype(jnp.float32)
+        )
+
+    def run3(u):
+        stage2(u).wait_recv()
+
+        @pl.loop(1, 4)
+        def _(d):
+            other = (z + d) % 4
+            second[u].at[other][...] = kept(u, other).astype(second[u].dtype)
+
+        for d in range(1, 4):
+            stage3(u, d).start()
+
+    def run4(u):
+        unit = units[u]
+        for d in range(1, 4):
+            stage3(u, d).wait_recv()
+        total = kept(u, z)
+        for d in range(1, 4):
+            total = total + third[u].at[d - 1][...].astype(jnp.float32)
+        out_refs[unit.member].at[:, pl.ds(unit.start, unit.width)][...] = total
+
+    barrier = pltpu.get_barrier_semaphore()
+    for target in (device_of(z, y, 1 - x), device_of(z, 1 - y, x), *(device_of((z + d) % 4, y, x) for d in range(1, 4))):
+        pl.semaphore_signal(barrier, inc=1, device_id=target, device_id_type=MESH)
+    pl.semaphore_wait(barrier, 5)
+
+    AHEAD, LAG = 4, 2
+    for u in range(min(AHEAD, count)):
+        stage1(u).start()
+    for step in range(count + 2 * LAG):
+        if step < count:
+            run2(step)
+            if step + AHEAD < count:
+                stage1(step + AHEAD).start()
+        if 0 <= step - LAG < count:
+            run3(step - LAG)
+        if 0 <= step - 2 * LAG < count:
+            run4(step - 2 * LAG)
+    for u in range(count):
+        stage1(u).wait_send()
+        stage2(u).wait_send()
+        for d in range(1, 4):
+            stage3(u, d).wait_send()
+
+
+def scatter_all(parts, units):
+    count = len(units)
+
+    def buffer(unit, lead):
+        part = parts[unit.member]
+        return pltpu.VMEM((*lead, part.shape[3], unit.width), part.dtype)
+
+    return pl.pallas_call(
+        functools.partial(scatter_kernel, units, len(parts)),
+        out_shape=[jax.ShapeDtypeStruct(part.shape[3:], jnp.float32) for part in parts],
+        in_specs=[pl.BlockSpec(memory_space=pltpu.VMEM)] * len(parts),
+        out_specs=[pl.BlockSpec(memory_space=pltpu.VMEM)] * len(parts),
+        scratch_shapes=[buffer(unit, (4, 2)) for unit in units]
+        + [buffer(unit, (4,)) for unit in units]
+        + [buffer(unit, (3,)) for unit in units]
+        + [pltpu.SemaphoreType.DMA((count,))] * 4
+        + [pltpu.SemaphoreType.DMA((count, 3))] * 2,
+        compiler_params=pltpu.CompilerParams(
+            collective_id=0, has_side_effects=True, vmem_limit_bytes=VMEM_BYTES
+        ),
+    )(*parts)
+
+
 def inverse_rms(stream):
     return lax.rsqrt(jnp.mean(stream * stream, axis=-1, keepdims=True) + EPSILON)
 
@@ -323,11 +471,6 @@
     joined = tuple(mixer_parts[0]) + tuple(ffn_parts[0])
     mix_gain_g, in_g, conv_g, out_g, ffn_gain_g, gate_g, up_g, down_g = joined
     n = lax.axis_size("seq")
-    down_s = scatter_sum(down_g.astype(jnp.bfloat16), (0, 1, 2))
-    gate_s = scatter_sum(gate_g.astype(jnp.bfloat16), (2, 1, 0))
-    up_s = scatter_sum(up_g.astype(jnp.bfloat16), (1, 2, 0))
-    out_s = scatter_sum(out_g.astype(jnp.bfloat16), (1, 2, 0))
-    in_s = scatter_sum(in_g.astype(jnp.bfloat16), (2, 1, 0))
     taps, channels = conv_g.shape
     small = jnp.concatenate(
         [
@@ -337,7 +480,28 @@
         ],
         axis=1,
     )
-    small = scatter_sum(small, (2, 1, 0), jnp.float32).reshape(-1)
+    if n == 16:
+        low = [gate_g, up_g, down_g, in_g.reshape(in_g.shape[0], -1), out_g]
+        parts = [g.astype(jnp.bfloat16).reshape(4, 2, 2, g.shape[0] // n, -1) for g in low]
+        length = small.shape[1]
+        padded = jnp.pad(small, ((0, 0), (0, 1024 - length)))
+        parts.append(padded.reshape(4, 2, 2, 8, 128))
+        units = [Unit(5, 0, 128, True)]
+        for start in range(0, 2304, 768):
+            units += [Unit(0, start, 768, True), Unit(1, start, 768, False)]
+        units += [Unit(2, 0, 512, True), Unit(2, 512, 512, False)]
+        units += [Unit(3, 0, 512, True), Unit(3, 512, 512, False), Unit(3, 1024, 256, True), Unit(3, 1280, 256, False)]
+        units += [Unit(4, 0, 512, True), Unit(4, 512, 512, False)]
+        gate_s, up_s, down_s, in_s, out_s, small = scatter_all(parts, units)
+        in_s = in_s.reshape(-1, 3, in_g.shape[2])
+        small = small.reshape(-1)[:length]
+    else:
+        down_s = scatter_sum(down_g.astype(jnp.bfloat16), (0, 1, 2))
+        gate_s = scatter_sum(gate_g.astype(jnp.bfloat16), (2, 1, 0))
+        up_s = scatter_sum(up_g.astype(jnp.bfloat16), (1, 2, 0))
+        out_s = scatter_sum(out_g.astype(jnp.bfloat16), (1, 2, 0))
+        in_s = scatter_sum(in_g.astype(jnp.bfloat16), (2, 1, 0))
+        small = scatter_sum(small, (2, 1, 0), jnp.float32).reshape(-1)
     gain_len = mix_gain_g.shape[0] // n
     return (
         output,

time: 403 us -> 296 us (0.73); the launches traced: 396 us -> 296 us
  Pallas kernels: 0 us -> 194 us
  starting transfers between devices: 127 us -> 7.38 us
  waiting for transfers between devices: 117 us -> 1.41 us
  other arithmetic: 71.1 us -> 16.9 us
  local copies, waits for them, and re-layouts: 22.9 us -> 17.3 us
    pallas_call x0 -> x1, Pallas kernels: none -> 194 us  [scatter_all(): pl.pallas_call(functools.partial(scatter_kernel, units, len(parts)), out_...]
    ppermute x48 -> x0, starting transfers between devices: 120 us -> none  [the longest x36 108 us: hop(): return lax.ppermute(block, 'seq', route)]
    ppermute x48 -> x0, waiting for transfers between devices: 102 us -> none  [the longest x12 51.7 us: scatter_sum(): lax.ppermute(sent, 'seq', [(i, i + stride * (1 - 2 * (i // stride % 2)))...]
    convert_element_type x29 -> x0, other arithmetic: 43.4 us -> none  [the longest x23 31.9 us: scatter_sum(): carried = hop(sent.astype(wire), dims, dim, step, spots)]
    ppermute x2, waiting for transfers between devices: 14.8 us -> 1.4 us  [shifted(): return lax.ppermute(block, axis, route)]
    broadcast_in_dim x5 -> x0, other arithmetic: 9.65 us -> none  [the longest x1 2.14 us: local(): gate_s[None]]
    squeeze x6 -> x0, local copies, waits for them, and re-layouts: 6.99 us -> none  [pick(): return lax.dynamic_index_in_dim(array, at, axis, keepdims=False)]
  transfers between devices with their start and end apart: 54 -> 6, of which waited for: 14 -> 2; matrix products, arithmetic and copies ran while one was open for 25% -> 11% of each run, Pallas kernels for 0% -> 0%
where the time goes in v2:
time: 296 us
  Pallas kernels  194 us (66%)
  matrix products  57.9 us (20%)
  local copies, waits for them, and re-layouts  17.3 us (6%)
  other arithmetic  16.9 us (6%)
  starting transfers between devices  7.38 us (2%)
    pallas_call x1, Pallas kernels, scatter_all(): pl.pallas_call(functools.partial(scatter_kernel, units, len(parts)), out_...  194 us
    unnamed x71, local copies, waits for them, and re-layouts  11.1 us
    dot_general x1, matrix products, forward_block(): jnp.dot(flat_ffn, weight_gate, preferred_element_type=jnp.float32)  8.69 us
    ppermute x2, starting transfers between devices, shifted(): return lax.ppermute(block, axis, route)  6.3 us
  transfers between devices with their start and end apart: 6, of which 2 were waited for; matrix products, arithmetic and copies ran while one was open for 11% of the time, Pallas kernels for 0%

profile of v2, /device:TPU:0, one launch (start us, length us, event | category | flops | bytes accessed | tf_op | source)
XLA Modules:
  0.0 295.8 jit_solution(10321488516312804661)
XLA Ops:
  0.6 1.5 fusion.16
  2.1 0.6 multiply_multiply_fusion
  2.7 0.7 convert_element_type.140
  3.4 0.0 slice-start.4
  3.5 4.8 %copy.22 = bf16[1,1024,3,512]{1,3,2,0:T(8,128)(2,1)} copy(bf16[1,1024,3,512]{3,1,2,0:T(8,128)(2,1)} %param.13) | data formatting | bytes 6291456 | tf_op args[3]
  8.3 3.9 %fusion.31 = f32[1,512,3,512]{3,1,2,0:T(8,128)S(1)} fusion(bf16[1,1024,3,512]{1,3,2,0:T(8,128)(2,1)} %copy.22, bf16[1,512,1024]{2,1,0:T(8,128)(2,1)S(1)} %copy-done.1, f32[1024]{0:T(1024)S(1)} %bitcast.195, f32[512]{0:T(512)S(1)} %get-tuple-element.67), kind=kOutput, calls=%fused_computation.53 | convolution fusion | flops 1612709888 | bytes 7346176 | tf_op jit(solution)/shard_map/dot_general | solution.py:259
  12.2 0.2 bitcast_multiply_fusion.6
  12.5 5.0 %collective-permute-start = (f32[1,2,512]{2,1,0:T(2,128)S(1)}, f32[1,2,512]{2,1,0:T(2,128)S(1)}, u32[]{:S(2)}, u32[]{:S(2)}) collective-permute-start(f32[1,2,512]{2,1,0:T(2,128)S(1)} %slice.79), channel_id=1, source_target_pairs={{0,2},{2,4},{4,6},{6,8},{8,10},{10,12},{12,14},{14,16},{16,18},{18... | collective-permute-start | bytes 12296 | tf_op jit(solution)/shard_map/ppermute | solution.py:16
  17.5 1.3 collective-permute-done
  18.8 1.2 fusion.69
  20.0 1.9 fusion.62
  21.8 0.1 collective-permute-start.1
  22.0 0.0 slice-start.1
  22.0 4.5 %fusion = f32[512,2304]{1,0:T(8,128)} fusion(bf16[1,2304,1024]{2,1,0:T(8,128)(2,1)S(1)} %bitcast.212, bf16[1,512,1024]{2,1,0:T(8,128)(2,1)S(1)} %copy-done.11), kind=kOutput, calls=%fused_computation.3 | convolution fusion | flops 2415919104 | bytes 10485760 | tf_op jit(solution)/shard_map/nd,fd->nf/dot_general | solution.py:328
  26.5 0.5 multiply_reduce_fusion
  27.1 0.2 fusion.52
  27.4 0.0 slice-start.3
  27.4 4.3 %fusion.6 = f32[512,2304]{1,0:T(8,128)} fusion(bf16[512,1024]{1,0:T(8,128)(2,1)S(1)} %fusion.52, bf16[1,1024,2304]{2,1,0:T(8,128)(2,1)S(1)} %bitcast.208), kind=kOutput, calls=%fused_computation.9 | convolution fusion | flops 2415919104 | bytes 10485760 | tf_op jit(solution)/shard_map/dot_general | solution.py:284
  31.7 8.7 %multiply_convert_fusion.1 = (bf16[512,2304]{1,0:T(8,128)(2,1)}, bf16[512,2304]{1,0:T(8,128)(2,1)}, bf16[512,2304]{1,0:T(8,128)(2,1)S(1)}) fusion(f32[512,2304]{1,0:T(8,128)} %fusion, f32[512,2304]{1,0:T(8,128)} %fusion.6, bf16[512,1024]{1,0:T(8,128)(2,1)S(1)} %fusion.52, bf16[1,1024,2304]{2,1,0:T(8,128)(2,1)S(1)} %bitcast.210), kind=kOutput, calls=%fused_computation.16 | convolution fusion | flops 2434793472 | bytes 22282240 | tf_op jit(solution)/shard_map/dot_general | solution.py:283
  40.4 2.6 fusion.4
  43.0 0.0 slice-start.7
  43.1 4.5 %fusion.41 = f32[512,1024]{1,0:T(8,128)S(1)} fusion(f32[512,1024]{1,0:T(8,128)S(1)} %fusion.4, bf16[512,2304]{1,0:T(8,128)(2,1)} %get-tuple-element.55, bf16[1,1024,2304]{2,1,0:T(8,128)(2,1)S(1)} %bitcast.210), kind=kOutput, calls=%fused_computation.60 | convolution fusion | flops 2416443392 | bytes 11272192 | tf_op jit(solution)/shard_map/nf,df->nd/dot_general | solution.py:342
  47.5 0.5 collective-permute-start.3
  48.1 2.6 fusion.44
  50.7 0.1 collective-permute-start.2
  50.8 4.4 %convolution_convert_fusion.2 = bf16[1024,2304]{1,0:T(8,128)(2,1)} fusion(bf16[512,1024]{1,0:T(8,128)(2,1)S(1)} %fusion.52, bf16[512,2304]{1,0:T(8,128)(2,1)S(1)} %copy-done.22), kind=kOutput, calls=%fused_computation.2 | convolution fusion | flops 2418278400 | bytes 8126464 | tf_op jit(solution)/shard_map/nd,nf->df/dot_general | solution.py:340
  55.2 4.3 %convolution_convert_fusion.1 = bf16[1024,2304]{1,0:T(8,128)(2,1)} fusion(bf16[512,1024]{1,0:T(8,128)(2,1)S(1)} %fusion.52, bf16[512,2304]{1,0:T(8,128)(2,1)S(1)} %copy-done.21), kind=kOutput, calls=%fused_computation.1 | convolution fusion | flops 2418278400 | bytes 8126464 | tf_op jit(solution)/shard_map/nd,nf->df/dot_general | solution.py:341
  59.6 0.7 fusion.26
  60.3 1.9 fusion.28
  62.2 1.0 multiply_reduce_fusion.2
  63.2 1.3 collective-permute-start.4
  64.5 4.4 %convolution_convert_fusion = bf16[2304,1024]{1,0:T(8,128)(2,1)} fusion(bf16[512,2304]{1,0:T(8,128)(2,1)S(1)} %copy-done.23, bf16[1,512,1024]{2,1,0:T(8,128)(2,1)S(1)} %copy-done.11), kind=kOutput, calls=%fused_computation | convolution fusion | flops 2418278400 | bytes 8126464 | tf_op jit(solution)/shard_map/nf,nd->fd/dot_general | solution.py:329
  68.9 0.1 collective-permute-done.4
  69.0 0.4 fusion.64
  69.4 0.3 fusion.65
  69.7 1.5 copy-done.4
  71.2 2.8 bitcast_convert_fusion
  74.1 0.4 collective-permute-start.5
  74.4 0.4 fusion.54
  74.8 0.1 reshape.355
  74.9 0.1 stack.42
  75.0 0.1 stack.40
  75.1 0.1 stack.41
  75.2 0.1 reshape.356
  75.3 2.9 convolution_convert_fusion.4
  78.2 0.2 pad_maximum_fusion
  78.4 1.6 copy.23
  80.0 5.1 %convolution_convert_fusion.3 = bf16[1024,1536]{1,0:T(8,128)(2,1)} fusion(bf16[512,1536]{0,1:T(8,128)(2,1)} %bitcast.186, bf16[1,512,1024]{2,1,0:T(8,128)(2,1)S(1)} %copy-done.1, f32[1024]{0:T(1024)S(1)} %bitcast.196, f32[512]{0:T(512)S(1)} %get-tuple-element.67), kind=kOutput, calls=%fused_computation.25 | convolution fusion | flops 1614282752 | bytes 5773312 | tf_op jit(solution)/shard_map/nd,nk->dk/dot_general | solution.py:406
  85.1 3.0 %fusion.24 = (f32[1024]{0:T(1024)S(1)}, f32[512]{0:T(512)}) fusion(bf16[1,512,1024]{2,1,0:T(8,128)(2,1)S(1)} %copy-done.1, bf16[512,1024]{1,0:T(8,128)(2,1)} %collective-permute-done.5, bf16[512,1024]{1,0:T(8,128)(2,1)} %bitcast_convert_fusion, f32[512]{0:T(512)S(1)} %get-tuple-element.67, f32[1024]{0:T(1024)S(1)} %bitcast.197), kind=kLoop, calls=%fused_computation.38 | loop fusion | flops 5241344 | bytes 3158016 | tf_op jit(solution)/shard_map/reduce_sum | solution.py:242
  88.1 0.1 reshape.353
  88.2 0.1 fusion.74
  88.3 0.6 copy.26
  88.9 193.8 %shard_map.177 = (f32[64,2304]{1,0:T(8,128)}, f32[64,2304]{1,0:T(8,128)}, f32[144,1024]{1,0:T(8,128)}, f32[64,1536]{1,0:T(8,128)}, f32[32,1024]{1,0:T(8,128)}, /*index=5*/f32[8,128]{1,0:T(8,128)}) custom-call(bf16[4,2,2,64,2304]{4,3,2,1,0:T(8,128)(2,1)} %bitcast.175, bf16[4,2,2,64,2304]{4,3,2,1,0:T(8,128)(2,1)} %bitcast.176, ...), custom_call_target="tpu_custom_call" | custom-call | tf_op jit(solution)/shard_map/pallas_call | solution.py:220
  282.8 0.8 slice.73
  283.5 1.3 slice_bitcast_fusion
  284.9 0.7 broadcast_multiply_fusion
  285.6 0.6 reshape.364
  286.2 1.3 broadcast_in_dim_reshape.3
  287.5 0.9 copy.24
  288.4 4.3 %fusion.21 = f32[1,512,1024]{2,1,0:T(8,128)} fusion(f32[1,512,1024]{2,1,0:T(8,128)} %copy-done, bf16[1,512,1024]{2,1,0:T(8,128)(2,1)S(1)} %copy-done.2, bf16[512,1024]{1,0:T(8,128)(2,1)} %collective-permute-done.5, bf16[512,1024]{1,0:T(8,128)(2,1)} %bitcast_convert_fusion, f32[512]{0:T(512)S(1)} %broadcast_multiply_fusion, f32[512]{0:T(512)} %get-tuple-element.66, ...), kind=kLoop, calls=%fused_computation.35 | loop fusion | flops 5242880 | bytes 7350272 | tf_op jit(solution)/shard_map/add | solution.py:426
  292.7 0.7 copy.31
  293.3 0.8 copy.32
  294.2 0.8 copy.33
  295.0 0.8 copy.34
  (74 shorter events, 0.2 us)
Async XLA Ops:
  2.7 82.4 %copy-start.17 = (f32[512]{0:T(512)}, f32[512]{0:T(512)S(1)}, u32[]{:S(2)}) copy-start(f32[512]{0:T(512)S(1)} %get-tuple-element.67) | copy-start | bytes 6148
  3.4 81.7 %copy-start.16 = (f32[1,1024]{1,0:T(1,128)}, f32[1,1024]{1,0:T(1,128)S(1)}, u32[]{:S(2)}) copy-start(f32[1,1024]{1,0:T(1,128)S(1)} %convert_element_type.140) | copy-start | bytes 12292
  3.4 4.8 %copy-start.1 = (bf16[1,512,1024]{2,1,0:T(8,128)(2,1)S(1)}, bf16[1,512,1024]{2,1,0:T(8,128)(2,1)}, u32[]{:S(2)}) copy-start(bf16[1,512,1024]{2,1,0:T(8,128)(2,1)} %param.10) | copy-start | bytes 3145732
  3.4 18.5 %slice-start.4 = ((s8[4718592]{0:T(1024)(128)(4,1)}), s8[524288]{0:T(1024)(128)(4,1)S(1)}, s32[]{:S(2)}) async-start(s8[4718592]{0:T(1024)(128)(4,1)} %bitcast.211), calls=%async_computation.4 | async-start | bytes 1048576
  8.3 13.7 %slice-start.5 = ((s8[4718592]{0:T(1024)(128)(4,1)}), s8[4194304]{0:T(1024)(128)(4,1)S(1)}, s32[]{:S(2)}) async-start(s8[4718592]{0:T(1024)(128)(4,1)} %bitcast.211), calls=%async_computation.5 | async-start | bytes 8388608
  12.2 5.3 %copy-start.18 = (bf16[1,3,512]{2,1,0:T(4,128)(2,1)S(1)}, bf16[1,3,512]{2,1,0:T(4,128)(2,1)}, u32[]{:S(2)}) copy-start(bf16[1,3,512]{2,1,0:T(4,128)(2,1)} %param.14) | copy-start | bytes 9220
  12.4 7.5 %copy-start.3 = (bf16[1,512,1024]{2,1,0:T(8,128)(2,1)S(1)}, bf16[1,512,1024]{2,1,0:T(8,128)(2,1)}, u32[]{:S(2)}) copy-start(bf16[1,512,1024]{2,1,0:T(8,128)(2,1)} %param.15) | copy-start | bytes 3145732
  12.5 6.3 %collective-permute-start = (f32[1,2,512]{2,1,0:T(2,128)S(1)}, f32[1,2,512]{2,1,0:T(2,128)S(1)}, u32[]{:S(2)}, u32[]{:S(2)}) collective-permute-start(f32[1,2,512]{2,1,0:T(2,128)S(1)} %slice.79), channel_id=1, source_target_pairs={{0,2},{2,4},{4,6},{6,8},{8,10},{10,12},{12,14},{14,16},{16,18},{18... | collective-permute-start | bytes 12296 | tf_op jit(solution)/shard_map/ppermute | solution.py:16
  20.0 2.0 copy-start.19
  20.0 2.0 copy-start.11
  21.8 4.7 %collective-permute-start.1 = (f32[512,1024]{1,0:T(8,128)S(1)}, f32[512,1024]{1,0:T(8,128)S(1)}, u32[]{:S(2)}, u32[]{:S(2)}) collective-permute-start(f32[512,1024]{1,0:T(8,128)S(1)} %fusion.62), channel_id=1, source_target_pairs={{0,1},{1,0},{2,3},{3,2},{4,5},{5,4},{6,7},{7,6},{8,9},{9,8},{10,11... | collective-permute-start | bytes 6291464 | tf_op jit(solution)/shard_map/ppermute | solution.py:28
  21.9 5.4 %slice-start = ((s8[4718592]{0:T(1024)(128)(4,1)}), s8[4194304]{0:T(1024)(128)(4,1)S(1)}, s32[]{:S(2)}) async-start(s8[4718592]{0:T(1024)(128)(4,1)} %bitcast.207), calls=%async_computation | async-start | bytes 8388608
  22.0 5.3 %slice-start.1 = ((s8[4718592]{0:T(1024)(128)(4,1)}), s8[524288]{0:T(1024)(128)(4,1)S(1)}, s32[]{:S(2)}) async-start(s8[4718592]{0:T(1024)(128)(4,1)} %bitcast.207), calls=%async_computation.1 | async-start | bytes 1048576
  27.1 4.6 %slice-start.2 = ((s8[4718592]{0:T(1024)(128)(4,1)}), s8[4194304]{0:T(1024)(128)(4,1)S(1)}, s32[]{:S(2)}) async-start(s8[4718592]{0:T(1024)(128)(4,1)} %bitcast.209), calls=%async_computation.2 | async-start | bytes 8388608
  27.4 4.4 %slice-start.3 = ((s8[4718592]{0:T(1024)(128)(4,1)}), s8[524288]{0:T(1024)(128)(4,1)S(1)}, s32[]{:S(2)}) async-start(s8[4718592]{0:T(1024)(128)(4,1)} %bitcast.209), calls=%async_computation.3 | async-start | bytes 1048576
  40.4 2.6 copy-start.20
  40.4 7.7 %slice-start.6 = ((s8[4718592]{0:T(1024)(128)(4,1)}), s8[4194304]{0:T(1024)(128)(4,1)S(1)}, s32[]{:S(2)}) async-start(s8[4718592]{0:T(1024)(128)(4,1)} %bitcast.213), calls=%async_computation.6 | async-start | bytes 8388608
  43.0 5.0 %slice-start.7 = ((s8[4718592]{0:T(1024)(128)(4,1)}), s8[524288]{0:T(1024)(128)(4,1)S(1)}, s32[]{:S(2)}) async-start(s8[4718592]{0:T(1024)(128)(4,1)} %bitcast.213), calls=%async_computation.7 | async-start | bytes 1048576
  43.1 5.0 %copy-start.23 = (bf16[512,2304]{1,0:T(8,128)(2,1)S(1)}, bf16[512,2304]{1,0:T(8,128)(2,1)}, u32[]{:S(2)}) copy-start(bf16[512,2304]{1,0:T(8,128)(2,1)} %get-tuple-element.56) | copy-start | bytes 7077892
  47.5 12.0 %collective-permute-start.3 = (f32[512,1024]{1,0:T(8,128)S(1)}, f32[512,1024]{1,0:T(8,128)S(1)}, u32[]{:S(2)}, u32[]{:S(2)}) collective-permute-start(f32[512,1024]{1,0:T(8,128)S(1)} %fusion.41), channel_id=1, source_target_pairs={{0,1},{1,0},{2,3},{3,2},{4,5},{5,4},{6,7},{7,6},{8,9},{9,8},{10,11... | collective-permute-start | bytes 6291464 | tf_op jit(solution)/shard_map/ppermute | solution.py:28
  48.1 2.8 copy-start.22
  50.7 4.5 %copy-start.21 = (bf16[512,2304]{1,0:T(8,128)(2,1)S(1)}, bf16[512,2304]{1,0:T(8,128)(2,1)}, u32[]{:S(2)}) copy-start(bf16[512,2304]{1,0:T(8,128)(2,1)} %copy-done.20) | copy-start | bytes 7077892
  50.7 9.6 %collective-permute-start.2 = (bf16[512,1024]{1,0:T(8,128)(2,1)S(1)}, bf16[512,1024]{1,0:T(8,128)(2,1)S(1)}, u32[]{:S(2)}, u32[]{:S(2)}) collective-permute-start(bf16[512,1024]{1,0:T(8,128)(2,1)S(1)} %fusion.44), channel_id=1, source_target_pairs={{0,1},{1,0},{2,3},{3,2},{4,5},{5,4},{6,7},{7,6},{8,9},{9,8},{10,11... | collective-permute-start | bytes 3145736 | tf_op jit(solution)/shard_map/ppermute | solution.py:33
  62.2 13.1 %copy-start = (f32[1,512,1024]{2,1,0:T(8,128)}, f32[1,512,1024]{2,1,0:T(8,128)S(1)}, u32[]{:S(2)}) copy-start(f32[1,512,1024]{2,1,0:T(8,128)S(1)} %get-tuple-element.58) | copy-start | bytes 6291460
  63.2 6.5 %copy-start.5 = (bf16[1,512,512]{2,1,0:T(8,128)(2,1)}, bf16[1,512,512]{2,1,0:T(8,128)(2,1)S(1)}, u32[]{:S(2)}) copy-start(bf16[1,512,512]{2,1,0:T(8,128)(2,1)S(1)} %get-tuple-element.60) | copy-start | bytes 1572868
  63.2 5.8 %collective-permute-start.4 = (f32[1,2,512]{2,1,0:T(2,128)S(1)}, f32[1,2,512]{2,1,0:T(2,128)S(1)}, u32[]{:S(2)}, u32[]{:S(2)}) collective-permute-start(f32[1,2,512]{2,1,0:T(2,128)S(1)} %slice.84), channel_id=1, source_target_pairs={{2,0},{4,2},{6,4},{8,6},{10,8},{12,10},{14,12},{16,14},{18,16},{20... | collective-permute-start | bytes 12296 | tf_op jit(solution)/shard_map/ppermute | solution.py:16
  69.0 2.3 copy-start.4
  69.4 4.7 %copy-start.7 = (bf16[1,512,512]{2,1,0:T(8,128)(2,1)}, bf16[1,512,512]{2,1,0:T(8,128)(2,1)S(1)}, u32[]{:S(2)}) copy-start(bf16[1,512,512]{2,1,0:T(8,128)(2,1)S(1)} %get-tuple-element.49) | copy-start | bytes 1572868
  69.7 4.4 %copy-start.9 = (bf16[1,512,512]{2,1,0:T(8,128)(2,1)}, bf16[1,512,512]{2,1,0:T(8,128)(2,1)S(1)}, u32[]{:S(2)}) copy-start(bf16[1,512,512]{2,1,0:T(8,128)(2,1)S(1)} %fusion.65) | copy-start | bytes 1572868
  74.1 11.0 %collective-permute-start.5 = (bf16[512,1024]{1,0:T(8,128)(2,1)}, bf16[512,1024]{1,0:T(8,128)(2,1)}, u32[]{:S(2)}, u32[]{:S(2)}) collective-permute-start(bf16[512,1024]{1,0:T(8,128)(2,1)} %bitcast_convert_fusion), channel_id=1, source_target_pairs={{0,1},{1,0},{2,3},{3,2},{4,5},{5,4},{6,7},{7,6},{8,9},{9,8},{10,11... | collective-permute-start | bytes 3145736 | tf_op jit(solution)/shard_map/ppermute | solution.py:33
  75.3 2.9 copy-start.6
  75.3 2.9 copy-start.8
  75.3 2.9 copy-start.10
  282.8 5.6 %copy-start.2 = (bf16[1,512,1024]{2,1,0:T(8,128)(2,1)S(1)}, bf16[1,512,1024]{2,1,0:T(8,128)(2,1)}, u32[]{:S(2)}) copy-start(bf16[1,512,1024]{2,1,0:T(8,128)(2,1)} %param.10) | copy-start | bytes 3145732
  288.4 4.3 %copy-start.15 = (f32[32,1024]{1,0:T(8,128)S(1)}, f32[32,1024]{1,0:T(8,128)}, u32[]{:S(2)}) copy-start(f32[32,1024]{1,0:T(8,128)} %get-tuple-element.18) | copy-start | bytes 393220
  288.4 5.0 %copy-start.14 = (f32[64,2304]{1,0:T(8,128)S(1)}, f32[64,2304]{1,0:T(8,128)}, u32[]{:S(2)}) copy-start(f32[64,2304]{1,0:T(8,128)} %get-tuple-element.19) | copy-start | bytes 1769476
  288.4 5.8 %copy-start.13 = (f32[64,2304]{1,0:T(8,128)S(1)}, f32[64,2304]{1,0:T(8,128)}, u32[]{:S(2)}) copy-start(f32[64,2304]{1,0:T(8,128)} %get-tuple-element.20) | copy-start | bytes 1769476
  292.7 2.3 copy-start.12

commit v3 on v1

--- a/solution.py
+++ b/solution.py
@@ -1,6 +1,8 @@
 import jax
 import jax.numpy as jnp
 from jax import lax
+from jax.experimental import pallas as pl
+from jax.experimental.pallas import tpu as pltpu
 from jax.sharding import PartitionSpec as P
 
 EPSILON = 1e-05
@@ -85,6 +87,611 @@
     return sum(part.astype(jnp.float32) for part, _ in parts)
 
 
+MESH = pl.DeviceIdType.MESH
+VMEM_BYTES = 67043328
+F32, BF16 = jnp.float32, jnp.bfloat16
+WIDE = 256
+
+
+def times(a, b):
+    return jnp.dot(a, b, preferred_element_type=F32)
+
+
+def times_t(a, b):
+    return lax.dot_general(a, b, (((1,), (1,)), ((), ())), preferred_element_type=F32)
+
+
+def device_of(z, y, x):
+    return {"seq": z * 4 + y * 2 + x}
+
+
+class Scatter:
+    def __init__(self, base, part, first, second, third, sems):
+        self.base, self.part = base, part
+        self.first, self.second, self.third = first, second, third
+        self.send1, self.recv1, self.send2, self.recv2, self.send3, self.recv3 = sems
+        me = lax.axis_index("seq")
+        self.z, self.y, self.x = me // 4, (me // 2) % 2, me % 2
+
+    def stage1(self, u, x_first):
+        z, y, x = self.z, self.y, self.x
+        if x_first:
+            source, target = self.part.at[u, :, :, 1 - x], device_of(z, y, 1 - x)
+        else:
+            source, target = self.part.at[u, :, 1 - y], device_of(z, 1 - y, x)
+        k = self.base + u
+        return pltpu.make_async_remote_copy(
+            source, self.first.at[u], self.send1.at[k], self.recv1.at[k], device_id=target, device_id_type=MESH
+        )
+
+    def stage2(self, u, x_first):
+        z, y, x = self.z, self.y, self.x
+        if x_first:
+            source, target = self.first.at[u, :, 1 - y], device_of(z, 1 - y, x)
+        else:
+            source, target = self.first.at[u, :, 1 - x], device_of(z, y, 1 - x)
+        k = self.base + u
+        return pltpu.make_async_remote_copy(
+            source, self.second.at[u], self.send2.at[k], self.recv2.at[k], device_id=target, device_id_type=MESH
+        )
+
+    def stage3(self, u, d):
+        other = (self.z + d) % 4
+        k = self.base + u
+        return pltpu.make_async_remote_copy(
+            self.second.at[u, other], self.third.at[u, d - 1], self.send3.at[k, d - 1], self.recv3.at[k, d - 1],
+            device_id=device_of(other, self.y, self.x), device_id_type=MESH,
+        )
+
+    def run1(self, u, x_first):
+        self.stage1(u, x_first).start()
+
+    def run2(self, u, x_first):
+        y, x = self.y, self.x
+        self.stage1(u, x_first).wait_recv()
+
+        @pl.loop(0, 4)
+        def _(at):
+            if x_first:
+                mine, spot = self.part.at[u, at, 1 - y, x], self.first.at[u, at, 1 - y]
+            else:
+                mine, spot = self.part.at[u, at, y, 1 - x], self.first.at[u, at, 1 - x]
+            spot[...] = (mine[...].astype(F32) + spot[...].astype(F32)).astype(spot.dtype)
+
+        self.stage2(u, x_first).start()
+
+    def kept(self, u, x_first, at):
+        y, x = self.y, self.x
+        near = self.first.at[u, at, y if x_first else x]
+        return (
+            self.part[u, at, y, x].astype(F32) + near[...].astype(F32) + self.second[u, at].astype(F32)
+        )
+
+    def run3(self, u, x_first):
+        self.stage2(u, x_first).wait_recv()
+
+        @pl.loop(1, 4)
+        def _(d):
+            other = (self.z + d) % 4
+            self.second[u, other] = self.kept(u, x_first, other).astype(self.second.dtype)
+
+        for d in range(1, 4):
+            self.stage3(u, d).start()
+
+    def run4(self, u, x_first):
+        for d in range(1, 4):
+            self.stage3(u, d).wait_recv()
+        total = self.kept(u, x_first, self.z)
+        for d in range(1, 4):
+            total = total + self.third[u, d - 1].astype(F32)
+        return total
+
+    def drain(self, u, x_first):
+        self.stage1(u, x_first).wait_send()
+        self.stage2(u, x_first).wait_send()
+        for d in range(1, 4):
+            self.stage3(u, d).wait_send()
+
+
+def block_kernel(
+    x_hbm, og_hbm, win_hbm, wout_hbm, wg_hbm, wu_hbm, wd_hbm, gain_mix, taps, gain_ffn,
+    out_hbm, in_grad_hbm, gate_hbm, up_hbm, down_hbm, in_hbm, outw_hbm, small_hbm,
+    og, acts, nt, mid, proj, gext, gcon, mixed, wout, wbuf, wdbuf, out_acc, gn_acc,
+    sa, sb, ra, rb, gp, hid, sums, taps_sum,
+    part_q, first_q, second_q, third_q,
+    part_d, first_d, second_d, third_d,
+    part_o, first_o, second_o, third_o,
+    part_s, first_s, second_s, third_s,
+    stage_q, stage_d, stage_o, stage_s,
+    send1, recv1, send2, recv2, send3, recv3,
+    load_sem, w_sem, wd_sem, ex_send, ex_recv, halo_send, halo_recv, store_sem,
+):
+    rows, width = og.shape
+    me = lax.axis_index("seq")
+    last = lax.axis_size("seq") - 1
+    core = lax.axis_index("tensor")
+    chunks = wd_hbm.shape[0] // WIDE
+    cols = width // WIDE
+    sems = (send1, recv1, send2, recv2, send3, recv3)
+    quads = Scatter(0, part_q, first_q, second_q, third_q, sems)
+    downs = Scatter(24, part_d, first_d, second_d, third_d, sems)
+    outs = Scatter(28, part_o, first_o, second_o, third_o, sems)
+    smalls = Scatter(32, part_s, first_s, second_s, third_s, sems)
+
+    def load(index, source, target):
+        return pltpu.make_async_copy(source, target, load_sem.at[index])
+
+    def win(i, slot):
+        return pltpu.make_async_copy(win_hbm.at[:, pl.ds(i * WIDE, WIDE)], wbuf.at[slot], w_sem.at[slot])
+
+    def wgate(j, slot):
+        return pltpu.make_async_copy(wg_hbm.at[:, pl.ds(pl.multiple_of(j * WIDE, WIDE), WIDE)], wbuf.at[slot], w_sem.at[slot])
+
+    def wup(j, slot):
+        return pltpu.make_async_copy(wu_hbm.at[:, pl.ds(pl.multiple_of(j * WIDE, WIDE), WIDE)], wbuf.at[slot], w_sem.at[slot])
+
+    def wdown(j, slot):
+        return pltpu.make_async_copy(wd_hbm.at[pl.ds(pl.multiple_of(j * WIDE, WIDE), WIDE)], wdbuf.at[slot], wd_sem.at[slot])
+
+    order = (0, 4, 1, 5, 2, 3)
+    load(0, x_hbm, sb).start()
+    for place in range(4):
+        win(order[place], place).start()
+    load(1, og_hbm, og).start()
+    load(2, wout_hbm, wout).start()
+    wdown(0, 0).start()
+
+    barrier = pltpu.get_barrier_semaphore()
+    z, y, x = quads.z, quads.y, quads.x
+    near = [device_of(z, y, 1 - x), device_of(z, 1 - y, x), *(device_of((z + d) % 4, y, x) for d in range(1, 4))]
+    near += [{"tensor": 1 - core}, {"seq": (me + last) % (last + 1)}, {"seq": (me + 1) % (last + 1)}]
+    for target in near:
+        pl.semaphore_signal(barrier, inc=1, device_id=target, device_id_type=MESH)
+
+    load(0, x_hbm, sb).wait()
+
+    @pl.loop(0, rows // 16)
+    def _(r):
+        at = pl.ds(pl.multiple_of(r * 16, 16), 16)
+        stream = sb[at, :].astype(F32)
+        scale = lax.rsqrt(jnp.mean(stream * stream, axis=-1, keepdims=True) + EPSILON)
+        acts[at, :] = (stream * scale * gain_mix[...].astype(F32)).astype(BF16)
+
+    pl.semaphore_wait(barrier, len(near))
+
+    def halo_fwd(c):
+        return pltpu.make_async_remote_copy(
+            gext.at[c, pl.ds(rows, 8)], gext.at[c, pl.ds(0, 8)], halo_send.at[c], halo_recv.at[c],
+            device_id={"seq": me + 1}, device_id_type=MESH,
+        )
+
+    def halo_back(c):
+        return pltpu.make_async_remote_copy(
+            gcon.at[c, pl.ds(0, 8)], gcon.at[c, pl.ds(rows, 8)], halo_send.at[2 + c], halo_recv.at[2 + c],
+            device_id={"seq": me - 1}, device_id_type=MESH,
+        )
+
+    for place, i in enumerate(order):
+        slot = place % 4
+        win(i, slot).wait()
+        proj[i] = times(acts[...], wbuf[slot])
+        if place + 4 < len(order):
+            win(order[place + 4], slot).start()
+        if i >= 4:
+            c = i - 4
+
+            @pl.loop(0, rows // 64)
+            def _(r):
+                at = pl.ds(pl.multiple_of(r * 64, 64), 64)
+                to = pl.ds(pl.multiple_of(r * 64 + 8, 8), 64)
+                gext[c, to, :] = proj[c, at, :] * proj[4 + c, at, :]
+
+            @pl.when(me < last)
+            def _():
+                halo_fwd(c).start()
+
+            @pl.when(me == 0)
+            def _():
+                gext[c, 0:8, :] = jnp.zeros((8, WIDE), F32)
+
+    wgate(0, 0).start()
+    wup(0, 2).start()
+
+    def tap(k, c):
+        return taps[k : k + 1, c * WIDE : (c + 1) * WIDE].astype(F32)
+
+    def convolved(c, r):
+        span = gext[c, pl.ds(pl.multiple_of(r * 64, 64), 72), :]
+        return tap(0, c) * span[6:70] + tap(1, c) * span[7:71] + tap(2, c) * span[8:72]
+
+    for c in range(2):
+
+        @pl.when(me > 0)
+        def _():
+            halo_fwd(c).wait_recv()
+
+        @pl.loop(0, rows // 64)
+        def _(r):
+            at = pl.ds(pl.multiple_of(r * 64, 64), 64)
+            mixed[c, at, :] = (proj[2 + c, at, :] * convolved(c, r)).astype(BF16)
+
+    def exchange(index, source, target, q):
+        span = pl.ds(q * WIDE, WIDE)
+        return pltpu.make_async_remote_copy(
+            source.at[:, span], target.at[:, span], ex_send.at[index, q], ex_recv.at[index, q],
+            device_id={"tensor": 1 - core}, device_id_type=MESH,
+        )
+
+    load(2, wout_hbm, wout).wait()
+    for q in range(cols):
+        span = slice(q * WIDE, (q + 1) * WIDE)
+        half = mixed.shape[2]
+        sa[:, span] = (times(mixed[0], wout[0:half, span]) + times(mixed[1], wout[half : 2 * half, span])).astype(BF16)
+        exchange(0, sa, ra, q).start()
+    for q in range(cols):
+        exchange(0, sa, ra, q).wait_recv()
+
+    def mean_of(value):
+        return jnp.mean(value, axis=-1, keepdims=True)
+
+    @pl.loop(0, rows // 16)
+    def _(r):
+        at = pl.ds(pl.multiple_of(r * 16, 16), 16)
+        stream = sb[at, :].astype(F32) + (sa[at, :].astype(F32) + ra[at, :].astype(F32))
+        mid[at, :] = stream
+        scale = lax.rsqrt(mean_of(stream * stream) + EPSILON)
+        acts[at, :] = (stream * scale * gain_ffn[...].astype(F32)).astype(BF16)
+
+    @pl.loop(0, rows // 128)
+    def _(r):
+        at = pl.ds(pl.multiple_of(r * 128, 128), 128)
+        nt[:, at] = acts[at, :].T
+
+    out_acc[...] = jnp.zeros_like(out_acc)
+    gn_acc[...] = jnp.zeros_like(gn_acc)
+    load(1, og_hbm, og).wait()
+
+    @pl.loop(0, chunks)
+    def _(j):
+        slot = j % 2
+        wgate(j, slot).wait()
+        wup(j, 2 + slot).wait()
+        wdown(j, slot).wait()
+
+        @pl.when(j + 1 < chunks)
+        def _():
+            wgate(j + 1, 1 - slot).start()
+            wup(j + 1, 3 - slot).start()
+            wdown(j + 1, 1 - slot).start()
+
+        hid[0] = times(acts[...], wbuf[slot])
+        hid[1] = times(acts[...], wbuf[2 + slot])
+        hid[2] = times_t(og[...], wdbuf[slot])
+
+        @pl.loop(0, rows // 32)
+        def _(r):
+            at = pl.ds(pl.multiple_of(r * 32, 32), 32)
+            gate, up, back = hid[0, at, :], hid[1, at, :], hid[2, at, :]
+            s = jax.nn.sigmoid(gate)
+            silu = gate * s
+            gp[0, at, :] = (silu * up).astype(BF16)
+            gp[1, at, :] = (back * up * s * (1.0 + gate * (1.0 - s))).astype(BF16)
+            gp[2, at, :] = (back * silu).astype(BF16)
+
+        part_q[j] = times(nt[...], gp[1]).astype(BF16).reshape(part_q.shape[1:])
+        quads.run1(j, True)
+        part_q[chunks + j] = times(nt[...], gp[2]).astype(BF16).reshape(part_q.shape[1:])
+        quads.run1(chunks + j, False)
+        act_t = gp[0].T
+        for q in range(cols):
+            block = times(act_t, og[:, q * WIDE : (q + 1) * WIDE]).astype(BF16)
+            for g in range(WIDE // 16):
+                group = j * (WIDE // 16) + g
+                shard, row = group // 9, pl.multiple_of((group % 9) * 16, 16)
+                part_d[q, shard // 4, (shard // 2) % 2, shard % 2, pl.ds(row, 16), :] = block[g * 16 : (g + 1) * 16]
+        for q in range(cols):
+            span = slice(q * WIDE, (q + 1) * WIDE)
+            gn_acc[:, span] += times_t(gp[1], wbuf[slot, span, :]) + times_t(gp[2], wbuf[2 + slot, span, :])
+            out_acc[:, span] += times(gp[0], wdbuf[slot, :, span])
+
+        @pl.when(j >= 4)
+        def _():
+            quads.run2(j - 4, True)
+            quads.run2(chunks + j - 4, False)
+
+    for q in range(cols):
+        downs.run1(q, q % 2 == 0)
+
+    for q in range(cols):
+        span = slice(q * WIDE, (q + 1) * WIDE)
+        sb[:, span] = gn_acc[:, span].astype(BF16)
+        exchange(1, sb, rb, q).start()
+    for q in range(cols):
+        exchange(0, sa, ra, q).wait_send()
+    sa[...] = out_acc[...].astype(BF16)
+    for slot, i in enumerate((0, 1, 2, 3)):
+        win(i, slot).start()
+    sums[...] = jnp.zeros_like(sums)
+    for q in range(cols):
+        exchange(1, sb, rb, q).wait_recv()
+
+    def fold(value):
+        return value[0:8] + value[8:16]
+
+    @pl.loop(0, rows // 16)
+    def _(r):
+        at = pl.ds(pl.multiple_of(r * 16, 16), 16)
+        grad = sb[at, :].astype(F32) + rb[at, :].astype(F32)
+        stream = mid[at, :]
+        scale = lax.rsqrt(mean_of(stream * stream) + EPSILON)
+        weighted = grad * gain_ffn[...].astype(F32)
+        sums[1] += fold(grad * stream * scale)
+        middle = og[at, :].astype(F32) + (
+            scale * weighted - stream * (scale * scale * scale) * mean_of(weighted * stream)
+        )
+        gn_acc[at, :] = middle
+        acts[at, :] = middle.astype(BF16)
+
+    for q in range(cols):
+        exchange(2, sa, ra, q).start()
+
+    load(3, x_hbm, og).start()
+    half = mixed.shape[2]
+    for c in range(2):
+        hid[c] = times_t(acts[...], wout[c * half : (c + 1) * half, :])
+
+        @pl.loop(0, rows // 64)
+        def _(r):
+            at = pl.ds(pl.multiple_of(r * 64, 64), 64)
+            grad = hid[c, at, :]
+            gcon[c, at, :] = grad * proj[2 + c, at, :]
+            gp[2 + c, at, :] = (grad * convolved(c, r)).astype(BF16)
+
+        @pl.when(me > 0)
+        def _():
+            halo_back(c).start()
+
+        @pl.when(me == last)
+        def _():
+            gcon[c, rows : rows + 8, :] = jnp.zeros((8, WIDE), F32)
+
+    for c in range(2):
+        mixed_t = mixed[c].T
+        for q in range(cols):
+            block = times(mixed_t, acts[:, q * WIDE : (q + 1) * WIDE]).astype(BF16)
+            part_o[q, 2 * c : 2 * c + 2] = block.reshape(2, *part_o.shape[2:])
+    for q in range(cols):
+        outs.run1(q, q % 2 == 1)
+
+    load(3, x_hbm, og).wait()
+
+    @pl.loop(0, rows // 128)
+    def _(r):
+        at = pl.ds(pl.multiple_of(r * 128, 128), 128)
+        stream = og[at, :].astype(F32)
+        scale = lax.rsqrt(mean_of(stream * stream) + EPSILON)
+        nt[:, at] = (stream * scale * gain_mix[...].astype(F32)).astype(BF16).T
+
+    for c in range(2):
+
+        @pl.when(me < last)
+        def _():
+            halo_back(c).wait_recv()
+
+        taps_sum[c] = jnp.zeros_like(taps_sum[c])
+
+        @pl.loop(0, rows // 64)
+        def _(r):
+            at = pl.ds(pl.multiple_of(r * 64, 64), 64)
+            ahead = gcon[c, pl.ds(pl.multiple_of(r * 64, 64), 72), :]
+            behind = gext[c, pl.ds(pl.multiple_of(r * 64, 64), 72), :]
+            grad = ahead[0:64]
+            gated = tap(0, c) * ahead[2:66] + tap(1, c) * ahead[1:65] + tap(2, c) * grad
+            for k in range(3):
+                product = (grad * behind[6 + k : 70 + k]).reshape(8, 8, WIDE)
+                taps_sum[c, k] += jnp.sum(product, axis=0)
+            gp[c, at, :] = (gated * proj[4 + c, at, :]).astype(BF16)
+            gp[4 + c, at, :] = (gated * proj[c, at, :]).astype(BF16)
+
+    for i in range(6):
+        part_q[2 * chunks + i] = times(nt[...], gp[i]).astype(BF16).reshape(part_q.shape[1:])
+        quads.run1(2 * chunks + i, i % 2 == 0)
+    for i in range(6):
+        slot = i % 4
+        win(i, slot).wait()
+        for q in range(cols):
+            span = slice(q * WIDE, (q + 1) * WIDE)
+            term = times_t(gp[i], wbuf[slot, span, :])
+            if i == 0:
+                out_acc[:, span] = term
+            else:
+                out_acc[:, span] += term
+        if i + 4 < 6:
+            win(i + 4, slot).start()
+    for q in range(cols):
+        exchange(1, sb, rb, q).wait_send()
+    for q in range(cols):
+        exchange(2, sa, ra, q).wait_recv()
+    for q in range(cols):
+        span = slice(q * WIDE, (q + 1) * WIDE)
+        sb[:, span] = out_acc[:, span].astype(BF16)
+        exchange(3, sb, rb, q).start()
+
+    for q in range(cols):
+        exchange(2, sa, ra, q).wait_send()
+
+    @pl.loop(0, rows // 16)
+    def _(r):
+        at = pl.ds(pl.multiple_of(r * 16, 16), 16)
+        sa[at, :] = (mid[at, :] + (sa[at, :].astype(F32) + ra[at, :].astype(F32))).astype(BF16)
+
+    out_copy = pltpu.make_async_copy(sa, out_hbm, load_sem.at[4])
+    out_copy.start()
+
+    for q in range(cols):
+        exchange(3, sb, rb, q).wait_recv()
+
+    @pl.loop(0, rows // 16)
+    def _(r):
+        at = pl.ds(pl.multiple_of(r * 16, 16), 16)
+        grad = sb[at, :].astype(F32) + rb[at, :].astype(F32)
+        stream = og[at, :].astype(F32)
+        scale = lax.rsqrt(mean_of(stream * stream) + EPSILON)
+        weighted = grad * gain_mix[...].astype(F32)
+        sums[0] += fold(grad * stream * scale)
+        gn_acc[at, :] += scale * weighted - stream * (scale * scale * scale) * mean_of(weighted * stream)
+
+    in_copy = pltpu.make_async_copy(gn_acc, in_grad_hbm, load_sem.at[5])
+    in_copy.start()
+
+    lines = [jnp.sum(sums[0], axis=0, keepdims=True), jnp.sum(sums[1], axis=0, keepdims=True)]
+    tap_lines = [[jnp.sum(taps_sum[c, k], axis=0, keepdims=True) for c in range(2)] for k in range(3)]
+    for k in range(8):
+        piece = [line[:, k * 128 : (k + 1) * 128] for line in lines]
+        group = k // 2
+        start = (group % 2) * 128
+        piece += [tap_lines[t][group // 2][:, start : start + 128] for t in range(3)]
+        tile = jnp.concatenate(piece + [jnp.zeros((3, 128), F32)], axis=0)
+        for side in range(2):
+            part_s[0, k // 2, k % 2, side] = tile
+    smalls.run1(0, True)
+
+    todo = []
+    for j in range(5, chunks):
+        todo += [(quads, j, True), (quads, chunks + j, False)]
+    early = [(quads, j, True) for j in range(5)] + [(quads, chunks + j, False) for j in range(5)]
+    todo += [(downs, q, q % 2 == 0) for q in range(cols)]
+    todo += [(smalls, 0, True)]
+    todo += [(outs, q, q % 2 == 1) for q in range(cols)]
+    todo += [(quads, 2 * chunks + i, i % 2 == 0) for i in range(6)]
+    staging = {id(quads): stage_q, id(downs): stage_d, id(outs): stage_o, id(smalls): stage_s}
+
+    def target(group, u):
+        if group is quads:
+            if u < chunks:
+                return gate_hbm.at[:, pl.ds(u * WIDE, WIDE)]
+            if u < 2 * chunks:
+                return up_hbm.at[:, pl.ds((u - chunks) * WIDE, WIDE)]
+            i = u - 2 * chunks
+            return in_hbm.at[i // 2, :, pl.ds((i % 2) * WIDE, WIDE)]
+        if group is downs:
+            return down_hbm.at[:, pl.ds(u * WIDE, WIDE)]
+        if group is outs:
+            return outw_hbm.at[:, pl.ds(u * WIDE, WIDE)]
+        return small_hbm
+
+    stores = []
+
+    def finish(group, u, x_first):
+        spot = staging[id(group)].at[u]
+        spot[...] = group.run4(u, x_first)
+        copy = pltpu.make_async_copy(spot, target(group, u), store_sem.at[group.base + u])
+        copy.start()
+        stores.append(copy)
+
+    pairs = [early[k] for j in range(5) for k in (j, 5 + j)]
+    queue2 = list(todo)
+    queue3 = pairs + todo
+    queue4 = pairs + todo
+    LAG = 4
+    done3 = done4 = 0
+    for step in range(len(queue3) + LAG):
+        if step < len(queue2):
+            group, u, x_first = queue2[step]
+            group.run2(u, x_first)
+        if step < len(queue3):
+            group, u, x_first = queue3[step]
+            group.run3(u, x_first)
+        if step >= LAG:
+            group, u, x_first = queue4[step - LAG]
+            finish(group, u, x_first)
+    for group, u, x_first in queue4:
+        group.drain(u, x_first)
+    for copy in stores:
+        copy.wait()
+    out_copy.wait()
+    in_copy.wait()
+    for q in range(cols):
+        exchange(3, sb, rb, q).wait_send()
+    for c in range(2):
+
+        @pl.when(me < last)
+        def _():
+            halo_fwd(c).wait_send()
+
+        @pl.when(me > 0)
+        def _():
+            halo_back(c).wait_send()
+
+
+def whole_block(inputs, out_grad, mix_gain, in_weight, conv_weight, out_weight, ffn_gain, gate_weight, up_weight, down_weight):
+    rows, width = inputs.shape[1:]
+    hidden = gate_weight.shape[2]
+    channels = out_weight.shape[1]
+    chunks = hidden // WIDE
+    quads, cols = 2 * chunks + 3 * channels // WIDE, width // WIDE
+    n = lax.axis_size("seq")
+
+    def buffers(count, length, lanes, kind):
+        return [
+            pltpu.VMEM((count, 4, 2, 2, length, lanes), kind),
+            pltpu.VMEM((count, 4, 2, length, lanes), kind),
+            pltpu.VMEM((count, 4, length, lanes), kind),
+            pltpu.VMEM((count, 3, length, lanes), kind),
+        ]
+
+    lq, ld, lo = width // n, hidden // n, channels // n
+    total = quads + 2 * cols + 1
+    hbm = pl.BlockSpec(memory_space=pl.ANY)
+    vmem = pl.BlockSpec(memory_space=pltpu.VMEM)
+    big = pltpu.VMEM((rows, width), BF16)
+    wide = pltpu.VMEM((rows, width), F32)
+    results = pl.pallas_call(
+        block_kernel,
+        out_shape=[
+            jax.ShapeDtypeStruct((rows, width), BF16),
+            jax.ShapeDtypeStruct((rows, width), F32),
+            jax.ShapeDtypeStruct((lq, hidden), F32),
+            jax.ShapeDtypeStruct((lq, hidden), F32),
+            jax.ShapeDtypeStruct((ld, width), F32),
+            jax.ShapeDtypeStruct((3, lq, channels), F32),
+            jax.ShapeDtypeStruct((lo, width), F32),
+            jax.ShapeDtypeStruct((8, 128), F32),
+        ],
+        in_specs=[hbm] * 7 + [vmem] * 3,
+        out_specs=[hbm] * 8,
+        scratch_shapes=[
+            big, big, pltpu.VMEM((width, rows), BF16), wide,
+            pltpu.VMEM((6, rows, WIDE), F32), pltpu.VMEM((2, rows + 8, WIDE), F32), pltpu.VMEM((2, rows + 8, WIDE), F32),
+            pltpu.VMEM((2, rows, WIDE), BF16), pltpu.VMEM((channels, width), BF16),
+            pltpu.VMEM((4, width, WIDE), BF16), pltpu.VMEM((2, WIDE, width), BF16), wide, wide,
+            big, big, big, big, pltpu.VMEM((6, rows, WIDE), BF16), pltpu.VMEM((3, rows, WIDE), F32),
+            pltpu.VMEM((2, 8, width), F32), pltpu.VMEM((2, 3, 8, WIDE), F32),
+            *buffers(quads, lq, WIDE, BF16), *buffers(cols, ld, WIDE, BF16),
+            *buffers(cols, lo, WIDE, BF16), *buffers(1, 8, 128, F32),
+            pltpu.VMEM((quads, lq, WIDE), F32), pltpu.VMEM((cols, ld, WIDE), F32),
+            pltpu.VMEM((cols, lo, WIDE), F32), pltpu.VMEM((1, 8, 128), F32),
+            *[pltpu.SemaphoreType.DMA((total,))] * 4, *[pltpu.SemaphoreType.DMA((total, 3))] * 2,
+            pltpu.SemaphoreType.DMA((6,)), pltpu.SemaphoreType.DMA((4,)), pltpu.SemaphoreType.DMA((2,)),
+            pltpu.SemaphoreType.DMA((4, cols)), pltpu.SemaphoreType.DMA((4, cols)),
+            pltpu.SemaphoreType.DMA((4,)), pltpu.SemaphoreType.DMA((4,)), pltpu.SemaphoreType.DMA((total,)),
+        ],
+        compiler_params=pltpu.CompilerParams(collective_id=0, has_side_effects=True, vmem_limit_bytes=VMEM_BYTES),
+    )(
+        inputs[0], out_grad[0], in_weight.reshape(width, 3 * channels), out_weight[0],
+        gate_weight[0], up_weight[0], down_weight[0], mix_gain, conv_weight[0], ffn_gain,
+    )
+    output, in_grad, gate_s, up_s, down_s, in_s, out_s, small = results
+    index = lax.axis_index("seq")
+    y, x = (index // 2) % 2, index % 2
+    gains = lax.dynamic_slice(small, (0, x * 64), (2, 64))
+    conv_s = lax.dynamic_slice(small, (2, y * 64 + x * 32), (3, 32))
+    return (
+        output[None], in_grad[None], gains[0:1], in_s.transpose(1, 0, 2)[None], conv_s[None],
+        out_s[None], gains[1:2], gate_s[None], up_s[None], down_s[None],
+    )
+
+
 def inverse_rms(stream):
     return lax.rsqrt(jnp.mean(stream * stream, axis=-1, keepdims=True) + EPSILON)
 
@@ -291,6 +898,10 @@
     up_weight,
     down_weight,
 ):
+    if lax.axis_size("seq") == 16:
+        return whole_block(
+            inputs, out_grad, mix_gain, in_weight, conv_weight, out_weight, ffn_gain, gate_weight, up_weight, down_weight
+        )
     layer_count = mix_gain.shape[0]
 
     def weights_of(number):

time: 403 us -> 251 us (0.62); the launches traced: 396 us -> 251 us
  Pallas kernels: 0 us -> 234 us
  starting transfers between devices: 127 us -> 0 us
  waiting for transfers between devices: 117 us -> 0 us
  other arithmetic: 71.1 us -> 0 us
  matrix products: 55.1 us -> 0 us
  local copies, waits for them, and re-layouts: 22.9 us -> 16.4 us
    pallas_call x0 -> x1, Pallas kernels: none -> 234 us  [whole_block(): pl.pallas_call(block_kernel, out_shape=[jax.ShapeDtypeStruct((rows, width...]
    ppermute x54 -> x0, starting transfers between devices: 127 us -> none  [the longest x36 108 us: hop(): return lax.ppermute(block, 'seq', route)]
    ppermute x54 -> x0, waiting for transfers between devices: 117 us -> none  [the longest x12 51.7 us: scatter_sum(): lax.ppermute(sent, 'seq', [(i, i + stride * (1 - 2 * (i // stride % 2)))...]
    dot_general x15 -> x0, matrix products: 55.1 us -> none  [the longest x1 8.54 us: forward_block(): jnp.dot(flat_ffn, weight_gate, preferred_element_type=jnp.float32)]
    convert_element_type x31 -> x0, other arithmetic: 43.4 us -> none  [the longest x23 31.9 us: scatter_sum(): carried = hop(sent.astype(wire), dims, dim, step, spots)]
    broadcast_in_dim x5 -> x0, other arithmetic: 9.65 us -> none  [the longest x1 2.14 us: local(): gate_s[None]]
    squeeze x6 -> x0, local copies, waits for them, and re-layouts: 6.99 us -> none  [pick(): return lax.dynamic_index_in_dim(array, at, axis, keepdims=False)]
    another operation x3 -> x0, other arithmetic: 5.62 us -> none
  transfers between devices with their start and end apart: 54 -> 0, of which waited for: 14 -> 0; matrix products, arithmetic and copies ran while one was open for 25% -> 0% of each run, Pallas kernels for 0% -> 0%
where the time goes in v3:
time: 251 us
  Pallas kernels  234 us (93%)
  local copies, waits for them, and re-layouts  16.4 us (7%)
    pallas_call x1, Pallas kernels, whole_block(): pl.pallas_call(block_kernel, out_shape=[jax.ShapeDtypeStruct((rows, width...  234 us
    unnamed x21, local copies, waits for them, and re-layouts  11.3 us

profile of v3, /device:TPU:0, one launch (start us, length us, event | category | flops | bytes accessed | tf_op | source)
XLA Modules:
  0.0 250.8 jit_solution(12332101858435392821)
XLA Ops:
  0.6 3.2 %copy.22 = bf16[1,1024,3,512]{1,3,2,0:T(8,128)(2,1)S(1)} copy(bf16[1,1024,3,512]{3,1,2,0:T(8,128)(2,1)} %param.13) | data formatting | bytes 6291456 | tf_op args[3]
  3.8 3.0 %copy.23.win_hbm = bf16[1024,1536]{1,0:T(8,128)(2,1)} copy(bf16[1024,1536]{0,1:T(8,128)(2,1)S(1)} %bitcast.19) | data formatting | bytes 6291456 | tf_op jit(solution)/shard_map/reshape | solution.py:681
  6.8 233.7 %shard_map.177 = (bf16[512,1024]{1,0:T(8,128)(2,1)}, f32[512,1024]{1,0:T(8,128)}, f32[64,2304]{1,0:T(8,128)}, f32[64,2304]{1,0:T(8,128)}, f32[144,1024]{1,0:T(8,...) custom-call(bf16[512,1024]{1,0:T(8,128)(2,1)} %bitcast.25, bf16[512,1024]{1,0:T(8,128)(2,1)} %bitcast.26, ...), custom_call_target="tpu_custom_call" | custom-call | tf_op jit(solution)/shard_map/pallas_call | solution.py:649
  240.5 0.0 copy-start
  240.5 0.9 constant_dynamic-slice_fusion
  241.4 0.5 fusion
  242.0 0.8 dynamic-slice_bitcast_fusion
  242.7 0.6 copy.24
  243.3 0.0 copy-start.4
  243.3 0.0 copy-start.5
  243.3 2.3 copy.32
  245.6 0.0 copy-done
  245.6 0.0 copy-start.3
  245.6 0.0 copy-start.2
  245.6 0.0 copy-start.1
  245.6 1.3 copy.33
  246.9 0.0 copy-done.4
  246.9 0.7 copy.34
  247.7 0.0 copy-done.5
  247.7 0.7 copy.35
  248.3 0.0 copy-done.3
  248.4 0.8 copy.36
  249.2 0.0 copy-done.2
  249.2 0.8 copy.37
  250.0 0.0 copy-done.1
  250.0 0.8 copy.38
Async XLA Ops:
  240.5 5.1 %copy-start = (f32[512,1024]{1,0:T(8,128)S(1)}, f32[512,1024]{1,0:T(8,128)}, u32[]{:S(2)}) copy-start(f32[512,1024]{1,0:T(8,128)} %get-tuple-element.19) | copy-start | bytes 6291460
  243.3 3.7 %copy-start.4 = (f32[3,64,512]{2,1,0:T(8,128)S(1)}, f32[3,64,512]{2,1,0:T(8,128)}, u32[]{:S(2)}) copy-start(f32[3,64,512]{2,1,0:T(8,128)} %get-tuple-element.21) | copy-start | bytes 1179652
  243.3 4.4 %copy-start.5 = (f32[32,1024]{1,0:T(8,128)S(1)}, f32[32,1024]{1,0:T(8,128)}, u32[]{:S(2)}) copy-start(f32[32,1024]{1,0:T(8,128)} %get-tuple-element.22) | copy-start | bytes 393220
  245.6 2.7 %copy-start.3 = (f32[64,2304]{1,0:T(8,128)S(1)}, f32[64,2304]{1,0:T(8,128)}, u32[]{:S(2)}) copy-start(f32[64,2304]{1,0:T(8,128)} %get-tuple-element.23) | copy-start | bytes 1769476
  245.6 3.6 %copy-start.2 = (f32[64,2304]{1,0:T(8,128)S(1)}, f32[64,2304]{1,0:T(8,128)}, u32[]{:S(2)}) copy-start(f32[64,2304]{1,0:T(8,128)} %get-tuple-element.24) | copy-start | bytes 1769476
  245.6 4.4 %copy-start.1 = (f32[144,1024]{1,0:T(8,128)S(1)}, f32[144,1024]{1,0:T(8,128)}, u32[]{:S(2)}) copy-start(f32[144,1024]{1,0:T(8,128)} %get-tuple-element.25) | copy-start | bytes 1769476

commit v4 on v1

--- a/solution.py
+++ b/solution.py
@@ -1,6 +1,8 @@
 import jax
 import jax.numpy as jnp
 from jax import lax
+from jax.experimental import pallas as pl
+from jax.experimental.pallas import tpu as pltpu
 from jax.sharding import PartitionSpec as P
 
 EPSILON = 1e-05
@@ -85,6 +87,987 @@
     return sum(part.astype(jnp.float32) for part, _ in parts)
 
 
+MESH = pl.DeviceIdType.MESH
+VMEM_BYTES = 67043328
+F32, BF16 = jnp.float32, jnp.bfloat16
+WIDE = 256
+
+
+def times(a, b):
+    return jnp.dot(a, b, preferred_element_type=F32)
+
+
+def times_t(a, b):
+    return lax.dot_general(a, b, (((1,), (1,)), ((), ())), preferred_element_type=F32)
+
+
+def device_of(z, y, x):
+    return {"seq": z * 4 + y * 2 + x}
+
+
+class Scatter:
+    def __init__(self, base, part, first, second, third, sems):
+        self.base, self.part = base, part
+        self.first, self.second, self.third = first, second, third
+        self.send1, self.recv1, self.send2, self.recv2, self.send3, self.recv3 = sems
+        me = lax.axis_index("seq")
+        self.z, self.y, self.x = me // 4, (me // 2) % 2, me % 2
+
+    def stage1(self, u, x_first):
+        z, y, x = self.z, self.y, self.x
+        if x_first:
+            source, target = self.part(u).at[:, :, 1 - x], device_of(z, y, 1 - x)
+        else:
+            source, target = self.part(u).at[:, 1 - y], device_of(z, 1 - y, x)
+        k = self.base + u
+        return pltpu.make_async_remote_copy(
+            source, self.first.at[u], self.send1.at[k], self.recv1.at[k], device_id=target, device_id_type=MESH
+        )
+
+    def stage2(self, u, x_first):
+        z, y, x = self.z, self.y, self.x
+        if x_first:
+            source, target = self.first.at[u, :, 1 - y], device_of(z, 1 - y, x)
+        else:
+            source, target = self.first.at[u, :, 1 - x], device_of(z, y, 1 - x)
+        k = self.base + u
+        return pltpu.make_async_remote_copy(
+            source, self.second.at[u], self.send2.at[k], self.recv2.at[k], device_id=target, device_id_type=MESH
+        )
+
+    def stage3(self, u, d):
+        other = (self.z + d) % 4
+        k = self.base + u
+        return pltpu.make_async_remote_copy(
+            self.second.at[u, other], self.third.at[u, d - 1], self.send3.at[k, d - 1], self.recv3.at[k, d - 1],
+            device_id=device_of(other, self.y, self.x), device_id_type=MESH,
+        )
+
+    def run1(self, u, x_first):
+        self.stage1(u, x_first).start()
+
+    def run2(self, u, x_first):
+        y, x = self.y, self.x
+        self.stage1(u, x_first).wait_recv()
+
+        @pl.loop(0, 4)
+        def _(at):
+            if x_first:
+                mine, spot = self.part(u).at[at, 1 - y, x], self.first.at[u, at, 1 - y]
+            else:
+                mine, spot = self.part(u).at[at, y, 1 - x], self.first.at[u, at, 1 - x]
+            spot[...] = (mine[...].astype(F32) + spot[...].astype(F32)).astype(spot.dtype)
+
+        self.stage2(u, x_first).start()
+
+    def kept(self, u, x_first, at):
+        y, x = self.y, self.x
+        near = self.first.at[u, at, y if x_first else x]
+        return (
+            self.part(u)[at, y, x].astype(F32) + near[...].astype(F32) + self.second[u, at].astype(F32)
+        )
+
+    def run3(self, u, x_first):
+        self.stage2(u, x_first).wait_recv()
+
+        @pl.loop(1, 4)
+        def _(d):
+            other = (self.z + d) % 4
+            self.second[u, other] = self.kept(u, x_first, other).astype(self.second.dtype)
+
+        for d in range(1, 4):
+            self.stage3(u, d).start()
+
+    def run4(self, u, x_first):
+        for d in range(1, 4):
+            self.stage3(u, d).wait_recv()
+        total = self.kept(u, x_first, self.z)
+        for d in range(1, 4):
+            total = total + self.third[u, d - 1].astype(F32)
+        return total
+
+    def drain(self, u, x_first):
+        self.stage1(u, x_first).wait_send()
+        self.stage2(u, x_first).wait_send()
+        for d in range(1, 4):
+            self.stage3(u, d).wait_send()
+
+
+class Halves:
+    def __init__(self, part, first, third, across_send, across_recv, sems):
+        self.part, self.first, self.third = part, first, third
+        self.across_send, self.across_recv = across_send, across_recv
+        self.send1, self.recv1, self.send3, self.recv3, self.send4, self.recv4 = sems
+        me = lax.axis_index("seq")
+        self.z, self.y, self.x = me // 4, (me // 2) % 2, me % 2
+
+    def stage1(self, u):
+        return pltpu.make_async_remote_copy(
+            self.part(u).at[:, 1 - self.y], self.first.at[u], self.send1.at[u], self.recv1.at[u],
+            device_id=device_of(self.z, 1 - self.y, self.x), device_id_type=MESH,
+        )
+
+    def stage3(self, u, d):
+        other = (self.z + d) % 4
+        return pltpu.make_async_remote_copy(
+            self.first.at[u, other], self.third.at[u, d - 1], self.send3.at[u, d - 1], self.recv3.at[u, d - 1],
+            device_id=device_of(other, self.y, self.x), device_id_type=MESH,
+        )
+
+    def stage4(self, u):
+        return pltpu.make_async_remote_copy(
+            self.across_send.at[u], self.across_recv.at[u], self.send4.at[u], self.recv4.at[u],
+            device_id=device_of(self.z, self.y, 1 - self.x), device_id_type=MESH,
+        )
+
+    def run1(self, u):
+        self.stage1(u).start()
+
+    def run2(self, u):
+        self.stage1(u).wait_recv()
+
+        @pl.loop(0, 6)
+        def _(k):
+            other, side = (self.z + 1 + k // 2) % 4, k % 2
+            spot = self.first.at[u, other, side]
+            spot[...] = (self.part(u)[other, self.y, side].astype(F32) + spot[...].astype(F32)).astype(BF16)
+
+        for d in range(1, 4):
+            self.stage3(u, d).start()
+
+    def total(self, u, side):
+        value = self.part(u)[self.z, self.y, side].astype(F32) + self.first[u, self.z, side].astype(F32)
+        for d in range(1, 4):
+            value = value + self.third[u, d - 1, side].astype(F32)
+        return value
+
+    def run3(self, u):
+        for d in range(1, 4):
+            self.stage3(u, d).wait_recv()
+        self.across_send[u] = self.total(u, 1 - self.x).astype(BF16)
+        self.stage4(u).start()
+        return self.total(u, self.x)
+
+    def run4(self, u):
+        self.stage4(u).wait_recv()
+        return self.across_recv[u].astype(F32)
+
+    def drain(self, u):
+        self.stage1(u).wait_send()
+        for d in range(1, 4):
+            self.stage3(u, d).wait_send()
+        self.stage4(u).wait_send()
+
+
+class Line:
+    def __init__(self, part, first, chain, extra, across_send, across_recv, sems):
+        self.part, self.first, self.chain, self.extra = part, first, chain, extra
+        self.across_send, self.across_recv = across_send, across_recv
+        (self.send1, self.recv1, self.send2, self.recv2, self.send3, self.recv3, self.send4, self.recv4) = sems
+        me = lax.axis_index("seq")
+        self.z, self.y, self.x = me // 4, (me // 2) % 2, me % 2
+        self.place = self.z + self.x * (3 - 2 * self.z)
+        self.nearer = (self.z + 3 + 2 * self.x) % 4
+        self.farther = (self.z + 1 + 2 * self.x) % 4
+        self.block0, self.block1 = self.x, 1 - self.x
+
+    def stage1(self, q):
+        return pltpu.make_async_remote_copy(
+            self.part.at[q, :, 1 - self.y], self.first.at[q], self.send1.at[q], self.recv1.at[q],
+            device_id=device_of(self.z, 1 - self.y, self.x), device_id_type=MESH,
+        )
+
+    def both(self, q):
+        return pltpu.make_async_remote_copy(
+            self.first.at[q], self.chain.at[q], self.send2.at[q], self.recv2.at[q],
+            device_id=device_of(self.nearer, self.y, self.x), device_id_type=MESH,
+        )
+
+    def inward(self, q):
+        return pltpu.make_async_remote_copy(
+            self.first.at[q, self.block0], self.extra.at[q], self.send3.at[q], self.recv3.at[q],
+            device_id=device_of(self.nearer, self.y, self.x), device_id_type=MESH,
+        )
+
+    def outward(self, q):
+        return pltpu.make_async_remote_copy(
+            self.first.at[q, self.block1], self.extra.at[q], self.send3.at[q], self.recv3.at[q],
+            device_id=device_of(self.farther, self.y, self.x), device_id_type=MESH,
+        )
+
+    def stage4(self, q):
+        return pltpu.make_async_remote_copy(
+            self.across_send.at[q], self.across_recv.at[q], self.send4.at[q], self.recv4.at[q],
+            device_id=device_of(self.z, self.y, 1 - self.x), device_id_type=MESH,
+        )
+
+    def run1(self, q):
+        self.stage1(q).start()
+
+    def add(self, q, block, other):
+        @pl.loop(0, 2)
+        def _(side):
+            spot = self.first.at[q, block, side]
+            spot[...] = (spot[...].astype(F32) + other[block, side].astype(F32)).astype(BF16)
+
+    def run2(self, q):
+        self.stage1(q).wait_recv()
+        for block in range(2):
+            self.add(q, block, self.part.at[q, :, self.y])
+
+        @pl.when(self.place == 3)
+        def _():
+            self.both(q).start()
+
+        @pl.when(self.place == 0)
+        def _():
+            self.outward(q).start()
+
+    def run3(self, q):
+        @pl.when(self.place == 2)
+        def _():
+            self.both(q).wait_recv()
+            for block in range(2):
+                self.add(q, block, self.chain.at[q])
+            self.both(q).start()
+
+    def run4(self, q):
+        @pl.when(self.place == 1)
+        def _():
+            self.both(q).wait_recv()
+            for block in range(2):
+                self.add(q, block, self.chain.at[q])
+            self.inward(q).start()
+
+    def run5(self, q, spot):
+        @pl.when(self.place < 2)
+        def _():
+            self.inward(q).wait_recv()
+            block = (self.place + self.x) % 2
+            far = self.first[q, block, 1 - self.x].astype(F32) + self.extra[q, 1 - self.x].astype(F32)
+            self.across_send[q] = far.astype(BF16)
+            self.stage4(q).start()
+            spot[...] = self.first[q, block, self.x].astype(F32) + self.extra[q, self.x].astype(F32)
+
+    def run6(self, q, spot):
+        @pl.when(self.place >= 2)
+        def _():
+            self.stage4(q).wait_recv()
+            spot[...] = self.across_recv[q].astype(F32)
+
+    def drain(self, q):
+        self.stage1(q).wait_send()
+
+        @pl.when(self.place >= 2)
+        def _():
+            self.both(q).wait_send()
+
+        @pl.when(self.place < 2)
+        def _():
+            self.inward(q).wait_send()
+            self.stage4(q).wait_send()
+
+
+def block_kernel(
+    x_hbm, og_hbm, win_hbm, wout_hbm, wg_hbm, wu_hbm, wd_hbm, gain_mix, taps, gain_ffn,
+    out_hbm, in_grad_hbm, gate_hbm, up_hbm, down_hbm, in_hbm, outw_hbm, small_hbm,
+    xb, og, nf, nt, act, gg, gu, mid, gm, gno, proj, gext, gcon, mixed, wout, wg, wu, wd, hid,
+    sa, ra, gnp, gnr, gnx, outp, outr, outx, sums, taps_sum,
+    part_g, part_u, first_g, third_g, asend_g, arecv_g,
+    part_d, first_d, chain_d, extra_d, asend_d, arecv_d,
+    first_i, second_i, third_i, first_o, second_o, third_o,
+    part_s, first_s, second_s, third_s, recv_s,
+    stage_g, stage_d, stage_i, stage_o, stage_s,
+    gs1, gr1, gs3, gr3, gs4, gr4, ds1, dr1, ds2, dr2, ds3, dr3, ds4, dr4,
+    send1, recv1, send2, recv2, send3, recv3,
+    load_sem, lsend, lrecv, mid_send, mid_recv, halo_send, halo_recv, g_sem, d_sem, m_sem,
+):
+    rows, width = x_hbm.shape
+    half = rows // 2
+    me = lax.axis_index("seq")
+    last = lax.axis_size("seq") - 1
+    core = lax.axis_index("tensor")
+    z, y, x = me // 4, (me // 2) % 2, me % 2
+    mate, across = {"tensor": 1 - core}, device_of(z, y, 1 - x)
+    share = wd.shape[0]
+    cols = width // WIDE
+    GROUP = 384
+    groups = share // GROUP
+    spans = ((0, 512), (512, share - 512))
+
+    def rows_of(block):
+        return pl.ds(pl.multiple_of(block * half, half), half)
+
+    mine, theirs = rows_of(core), rows_of(1 - core)
+    mine_x, theirs_x = rows_of(2 + core), rows_of(3 - core)
+
+    def columns(ref, start, size):
+        return ref.at[:, :, :, :, pl.ds(start, size)]
+
+    grads = Halves(
+        lambda u: columns(part_g if u < groups else part_u, (u % groups) * GROUP, GROUP),
+        first_g, third_g, asend_g, arecv_g, (gs1, gr1, gs3, gr3, gs4, gr4),
+    )
+    downs = Line(part_d, first_d, chain_d, extra_d, asend_d, arecv_d, (ds1, dr1, ds2, dr2, ds3, dr3, ds4, dr4))
+    sems = (send1, recv1, send2, recv2, send3, recv3)
+    ins = Scatter(0, lambda u: columns(gg if u < 4 else gu, (u % 4) * WIDE, WIDE), first_i, second_i, third_i, sems)
+    outs = Scatter(6, lambda u: act.at[:, :, :, 0:32, pl.ds(u * WIDE, WIDE)], first_o, second_o, third_o, sems)
+    smalls = Scatter(10, lambda u: part_s, first_s, second_s, third_s, sems)
+
+    def load(index, source, target):
+        return pltpu.make_async_copy(source, target, load_sem.at[index])
+
+    def send(index, source, target, device):
+        return pltpu.make_async_remote_copy(
+            source, target, lsend.at[index], lrecv.at[index], device_id=device, device_id_type=MESH
+        )
+
+    x_og = send(0, og_hbm.at[mine], og.at[mine_x], across)
+    m_og = send(1, og.at[mine_x], og.at[mine_x], mate)
+    m_nf = send(2, nf.at[mine], nf.at[mine], mate)
+    x_nf = send(3, nf.at[mine], nf.at[mine_x], across)
+    m_nfx = send(4, nf.at[mine_x], nf.at[mine_x], mate)
+    m_gn0 = send(5, gnp.at[1 - core], gnr.at[0], mate)
+    m_gn1 = send(6, gnp.at[3 - core], gnr.at[1], mate)
+    x_gn = send(7, gnp.at[2 + core], gnx, across)
+    m_out0 = send(8, outp.at[1 - core], outr.at[0], mate)
+    m_out1 = send(9, outp.at[3 - core], outr.at[1], mate)
+    x_out = send(10, outp.at[2 + core], outx, across)
+    m_rmid = send(11, xb.at[mine], xb.at[mine], mate)
+    m_in = send(12, gm, in_grad_hbm.at[mine], mate)
+    m_small = send(14, stage_s, recv_s, mate)
+
+    def m_mid(turn, q):
+        span = pl.ds(q * WIDE, WIDE)
+        return pltpu.make_async_remote_copy(
+            sa.at[:, span], ra.at[:, span], mid_send.at[turn, q], mid_recv.at[turn, q], device_id=mate, device_id_type=MESH
+        )
+
+    def win_loads():
+        return (
+            load(2, win_hbm.at[:, pl.ds(0, 1024)], wg.at[:, pl.ds(0, 1024)]),
+            load(3, win_hbm.at[:, pl.ds(1024, 512)], wu.at[:, pl.ds(0, 512)]),
+        )
+
+    first_column = pl.multiple_of(x * share, 128)
+    gate_load = load(4, wg_hbm.at[:, pl.ds(first_column, share)], wg)
+    up_load = load(5, wu_hbm.at[:, pl.ds(first_column, share)], wu)
+    down_load = load(6, wd_hbm.at[pl.ds(first_column, share)], wd)
+
+    load(0, x_hbm, xb).start()
+    for copy in win_loads():
+        copy.start()
+    load(1, og_hbm, og.at[pl.ds(0, rows)]).start()
+    load(7, wout_hbm, wout).start()
+    down_load.start()
+
+    barrier = pltpu.get_barrier_semaphore()
+    near = [across, device_of(z, 1 - y, x), *(device_of((z + d) % 4, y, x) for d in range(1, 4))]
+    near += [mate, {"seq": (me + last) % (last + 1)}, {"seq": (me + 1) % (last + 1)}]
+    for target in near:
+        pl.semaphore_signal(barrier, inc=1, device_id=target, device_id_type=MESH)
+
+    def mean_of(value):
+        return jnp.mean(value, axis=-1, keepdims=True)
+
+    def fold(value):
+        return value[0:8] + value[8:16]
+
+    pl.semaphore_wait(barrier, len(near))
+    x_og.start()
+
+    load(0, x_hbm, xb).wait()
+
+    @pl.loop(0, rows // 16, unroll=4)
+    def _(r):
+        at = pl.ds(pl.multiple_of(r * 16, 16), 16)
+        stream = xb[at, :].astype(F32)
+        scale = lax.rsqrt(mean_of(stream * stream) + EPSILON)
+        nf[at, :] = (stream * scale * gain_mix[...].astype(F32)).astype(BF16)
+
+    def halo_fwd(c):
+        return pltpu.make_async_remote_copy(
+            gext.at[c, pl.ds(rows, 8)], gext.at[c, pl.ds(0, 8)], halo_send.at[c], halo_recv.at[c],
+            device_id={"seq": me + 1}, device_id_type=MESH,
+        )
+
+    def halo_back(c):
+        return pltpu.make_async_remote_copy(
+            gcon.at[c, pl.ds(0, 8)], gcon.at[c, pl.ds(rows, 8)], halo_send.at[2 + c], halo_recv.at[2 + c],
+            device_id={"seq": me - 1}, device_id_type=MESH,
+        )
+
+    for copy in win_loads():
+        copy.wait()
+    for i in (0, 4, 1, 5, 2, 3):
+        weight = wg[:, i * WIDE : (i + 1) * WIDE] if i < 4 else wu[:, (i - 4) * WIDE : (i - 3) * WIDE]
+        proj[i] = times(nf[0:rows, :], weight)
+        if i >= 4:
+            c = i - 4
+
+            @pl.loop(0, rows // 64, unroll=2)
+            def _(r):
+                at = pl.ds(pl.multiple_of(r * 64, 64), 64)
+                to = pl.ds(pl.multiple_of(r * 64 + 8, 8), 64)
+                gext[c, to, :] = proj[c, at, :] * proj[4 + c, at, :]
+
+            @pl.when(me < last)
+            def _():
+                halo_fwd(c).start()
+
+            @pl.when(me == 0)
+            def _():
+                gext[c, 0:8, :] = jnp.zeros((8, WIDE), F32)
+
+    gate_load.start()
+    up_load.start()
+
+    def tap(k, c):
+        return taps[k : k + 1, c * WIDE : (c + 1) * WIDE].astype(F32)
+
+    def convolved(c, r):
+        span = gext[c, pl.ds(pl.multiple_of(r * 64, 64), 72), :]
+        return tap(0, c) * span[6:70] + tap(1, c) * span[7:71] + tap(2, c) * span[8:72]
+
+    for c in range(2):
+
+        @pl.when(me > 0)
+        def _():
+            halo_fwd(c).wait_recv()
+
+        @pl.loop(0, rows // 64, unroll=2)
+        def _(r):
+            at = pl.ds(pl.multiple_of(r * 64, 64), 64)
+            mixed[c, at, :] = (proj[2 + c, at, :] * convolved(c, r)).astype(BF16)
+
+    load(7, wout_hbm, wout).wait()
+
+    def out_part(at, q):
+        span = slice(q * WIDE, (q + 1) * WIDE)
+        return times(mixed[0, at, :], wout[0:WIDE, span]) + times(mixed[1, at, :], wout[WIDE : 2 * WIDE, span])
+
+    for q in range(cols):
+        sa[:, q * WIDE : (q + 1) * WIDE] = out_part(theirs, q).astype(BF16)
+        m_mid(0, q).start()
+    for q in range(cols):
+        mid[:, q * WIDE : (q + 1) * WIDE] = out_part(mine, q)
+    for q in range(cols):
+        m_mid(0, q).wait_recv()
+
+    @pl.loop(0, half // 16, unroll=4)
+    def _(r):
+        at = pl.ds(pl.multiple_of(r * 16, 16), 16)
+        here = pl.ds(pl.multiple_of(core * half + r * 16, 16), 16)
+        stream = xb[here, :].astype(F32) + (mid[at, :] + ra[at, :].astype(F32))
+        mid[at, :] = stream
+        scale = lax.rsqrt(mean_of(stream * stream) + EPSILON)
+        nf[here, :] = (stream * scale * gain_ffn[...].astype(F32)).astype(BF16)
+
+    m_nf.start()
+    x_nf.start()
+
+    def turn_block(block):
+        nt[:, rows_of(block)] = nf[rows_of(block), :].T
+
+    def hidden_of(block):
+        at = rows_of(block)
+        for start, size in spans:
+            hid[0, :, 0:size] = times(nf[at, :], wg[:, start : start + size])
+            hid[1, :, 0:size] = times(nf[at, :], wu[:, start : start + size])
+            hid[2, :, 0:size] = times_t(og[at, :], wd[start : start + size, :])
+
+            @pl.loop(0, half // 16, unroll=4)
+            def _(r):
+                line = pl.ds(pl.multiple_of(r * 16, 16), 16)
+                spot = (block, r // 8, (r // 4) % 2, pl.ds(pl.multiple_of((r % 4) * 16, 16), 16), slice(start, start + size))
+                gate, up, back = hid[0, line, 0:size], hid[1, line, 0:size], hid[2, line, 0:size]
+                s = jax.nn.sigmoid(gate)
+                silu = gate * s
+                act[spot] = (silu * up).astype(BF16)
+                gg[spot] = (back * up * s * (1.0 + gate * (1.0 - s))).astype(BF16)
+                gu[spot] = (back * silu).astype(BF16)
+
+    def gradient_of(block):
+        for q in range(cols):
+            span = slice(q * WIDE, (q + 1) * WIDE)
+            gnp[block, :, span] = (
+                times_t(gg[block].reshape(half, share), wg[span, :]) + times_t(gu[block].reshape(half, share), wu[span, :])
+            ).astype(BF16)
+
+    def output_of(block):
+        for q in range(cols):
+            span = slice(q * WIDE, (q + 1) * WIDE)
+            outp[block, :, span] = times(act[block].reshape(half, share), wd[:, span]).astype(BF16)
+
+    load(1, og_hbm, og.at[pl.ds(0, rows)]).wait()
+    gate_load.wait()
+    up_load.wait()
+    down_load.wait()
+
+    @pl.loop(0, 2)
+    def _(i):
+        @pl.when(i == 1)
+        def _():
+            m_nf.wait_recv()
+            x_og.wait_recv()
+            m_og.start()
+
+        block = (core + i) % 2
+        turn_block(block)
+        hidden_of(block)
+
+    @pl.loop(0, 2)
+    def _(i):
+        block = (core + 1 + i) % 2
+        gradient_of(block)
+        output_of(block)
+
+        @pl.when(i == 0)
+        def _():
+            m_gn0.start()
+            m_out0.start()
+
+    @pl.loop(0, 2)
+    def _(i):
+        @pl.when(i == 0)
+        def _():
+            x_nf.wait_recv()
+            m_nfx.start()
+
+        @pl.when(i == 1)
+        def _():
+            m_og.wait_recv()
+            m_nfx.wait_recv()
+
+        block = 2 + (core + i) % 2
+        turn_block(block)
+        hidden_of(block)
+
+    for copy in (m_nf, x_nf, m_nfx, m_og):
+        copy.wait_send()
+    tokens = 2 * rows
+    pieces = [(nf, 0, 288), (nf, 288, 288), (nf, 576, 288), (nf, 864, 160), (xb, 0, 128)]
+
+    def turn_activated():
+        for piece in range(groups):
+            size = min(GROUP, 2 * rows - piece * GROUP)
+            turned = act[:, :, :, :, piece * GROUP : (piece + 1) * GROUP].reshape(tokens, GROUP).T
+            nf[piece * GROUP : piece * GROUP + size, :] = turned[0:size]
+            if size < GROUP:
+                xb[0 : GROUP - size, :] = turned[size:GROUP]
+
+    def down_part(q):
+        row = 0
+        for source, start, size in pieces:
+            block = times(source[start : start + size, :], og[:, q * WIDE : (q + 1) * WIDE]).astype(BF16)
+            at = 0
+            while at < size:
+                shard, offset = divmod(row + at, 144)
+                count = min(144 - offset, size - at)
+                part_d[q, shard // 4, (shard // 2) % 2, shard % 2, offset : offset + count, :] = block[at : at + count]
+                at += count
+            row += size
+        if q == cols - 1:
+            load(0, x_hbm, og.at[pl.ds(rows, rows)]).start()
+
+    def hidden_part(part, source):
+        for start, size in spans:
+
+            @pl.loop(0, 4)
+            def _(m):
+                lhs = nt[pl.ds(pl.multiple_of(m * WIDE, WIDE), WIDE), :]
+                block = times(lhs, source[:, :, :, :, start : start + size].reshape(tokens, size))
+                part[m, :, :, :, start : start + size] = block.astype(BF16).reshape(2, 2, 64, size)
+
+    def join(mine_part, other_part):
+        @pl.loop(0, half // 32, unroll=2)
+        def _(r):
+            at = pl.ds(pl.multiple_of(r * 32, 32), 32)
+            mine_part[at, :] = (mine_part[at, :].astype(F32) + other_part[at, :].astype(F32)).astype(BF16)
+
+    def gradient_theirs():
+        gradient_of(3 - core)
+        m_gn1.start()
+
+    def gradient_mine():
+        gradient_of(2 + core)
+        m_gn1.wait_recv()
+        join(gnp.at[2 + core], gnr.at[1])
+        x_gn.start()
+
+    def output_both():
+        output_of(3 - core)
+        m_out1.start()
+        output_of(2 + core)
+        m_out1.wait_recv()
+        join(outp.at[2 + core], outr.at[1])
+        x_out.start()
+        for copy in win_loads():
+            copy.start()
+
+    def ffn_norm():
+        m_gn0.wait_recv()
+        x_gn.wait_recv()
+        sums[...] = jnp.zeros_like(sums)
+
+        @pl.loop(0, half // 16, unroll=4)
+        def _(r):
+            at = pl.ds(pl.multiple_of(r * 16, 16), 16)
+            here = pl.ds(pl.multiple_of(core * half + r * 16, 16), 16)
+            grad = gnp[core, at, :].astype(F32) + gnr[0, at, :].astype(F32) + gnx[at, :].astype(F32)
+            stream = mid[at, :]
+            scale = lax.rsqrt(mean_of(stream * stream) + EPSILON)
+            weighted = grad * gain_ffn[...].astype(F32)
+            sums[1] += fold(grad * stream * scale)
+            middle = og[here, :].astype(F32) + (
+                scale * weighted - stream * (scale * scale * scale) * mean_of(weighted * stream)
+            )
+            gm[at, :] = middle
+            xb[here, :] = middle.astype(BF16)
+
+        m_rmid.start()
+        load(0, x_hbm, og.at[pl.ds(rows, rows)]).wait()
+
+        @pl.loop(0, rows // 128)
+        def _(r):
+            at = pl.ds(pl.multiple_of(r * 128, 128), 128)
+            stream = og[pl.ds(pl.multiple_of(rows + r * 128, 128), 128), :].astype(F32)
+            scale = lax.rsqrt(mean_of(stream * stream) + EPSILON)
+            nt[:, at] = (stream * scale * gain_mix[...].astype(F32)).astype(BF16).T
+
+        m_rmid.wait_recv()
+
+    def mixer_back():
+        @pl.loop(0, 2)
+        def _(h):
+            hid[h, :, 0 : 2 * WIDE] = times_t(xb[rows_of(h), :], wout[...])
+
+        for c in range(2):
+            span = slice(c * WIDE, (c + 1) * WIDE)
+
+            @pl.loop(0, rows // 64, unroll=2)
+            def _(r):
+                at = pl.ds(pl.multiple_of(r * 64, 64), 64)
+                grad = hid[r // 4, pl.ds(pl.multiple_of((r % 4) * 64, 64), 64), span]
+                gcon[c, at, :] = grad * proj[2 + c, at, :]
+                nf[at, (2 + c) * WIDE : (3 + c) * WIDE] = (grad * convolved(c, r)).astype(BF16)
+
+            @pl.when(me > 0)
+            def _():
+                halo_back(c).start()
+
+            @pl.when(me == last)
+            def _():
+                gcon[c, rows : rows + 8, :] = jnp.zeros((8, WIDE), F32)
+
+
+    def in_grad_of(i):
+        source = nf[0:rows, i * WIDE : (i + 1) * WIDE] if i < 4 else nf[rows : 2 * rows, (i - 4) * WIDE : (i - 3) * WIDE]
+        block = times(nt[:, 0:rows], source).astype(BF16).reshape(4, 2, 2, 64, WIDE)
+        columns(gg if i < 4 else gu, (i % 4) * WIDE, WIDE)[...] = block
+
+    def gated_back(c):
+
+        @pl.when(me < last)
+        def _():
+            halo_back(c).wait_recv()
+
+        taps_sum[c] = jnp.zeros_like(taps_sum[c])
+
+        @pl.loop(0, rows // 64, unroll=2)
+        def _(r):
+            at = pl.ds(pl.multiple_of(r * 64, 64), 64)
+            ahead = gcon[c, pl.ds(pl.multiple_of(r * 64, 64), 72), :]
+            behind = gext[c, pl.ds(pl.multiple_of(r * 64, 64), 72), :]
+            grad = ahead[0:64]
+            gated = tap(0, c) * ahead[2:66] + tap(1, c) * ahead[1:65] + tap(2, c) * grad
+            for k in range(3):
+                product = (grad * behind[6 + k : 70 + k]).reshape(8, 8, WIDE)
+                taps_sum[c, k] += jnp.sum(product, axis=0)
+            nf[at, c * WIDE : (c + 1) * WIDE] = (gated * proj[4 + c, at, :]).astype(BF16)
+            nf[pl.ds(pl.multiple_of(rows + r * 64, 64), 64), c * WIDE : (c + 1) * WIDE] = (
+                gated * proj[c, at, :]
+            ).astype(BF16)
+
+    def out_grad_of(c):
+        mixed_t = mixed[c].T
+        for q in range(cols):
+            block = times(mixed_t, xb[:, q * WIDE : (q + 1) * WIDE]).astype(BF16)
+            act[2 * c : 2 * c + 2, :, :, 0:32, q * WIDE : (q + 1) * WIDE] = block.reshape(2, 2, 2, 32, WIDE)
+    def mix_gradient():
+        for copy in win_loads():
+            copy.wait()
+
+        def mix_part(block, q):
+            span = slice(q * WIDE, (q + 1) * WIDE)
+            return times_t(nf[rows_of(block), :], wg[span, 0:1024]) + times_t(nf[rows_of(2 + block), 0:512], wu[span, 0:512])
+
+        for q in range(cols):
+            m_mid(0, q).wait_send()
+        for q in range(cols):
+            sa[:, q * WIDE : (q + 1) * WIDE] = mix_part(1 - core, q).astype(BF16)
+            m_mid(1, q).start()
+        for q in range(cols):
+            gno[:, q * WIDE : (q + 1) * WIDE] = mix_part(core, q)
+
+
+    def final_output():
+        m_out0.wait_recv()
+        x_out.wait_recv()
+        m_out0.wait_send()
+
+        @pl.loop(0, half // 16, unroll=4)
+        def _(r):
+            at = pl.ds(pl.multiple_of(r * 16, 16), 16)
+            outp[core, at, :] = (
+                mid[at, :]
+                + (outp[core, at, :].astype(F32) + outr[0, at, :].astype(F32) + outx[at, :].astype(F32))
+            ).astype(BF16)
+
+
+        m_final.start()
+        out_copy.start()
+
+    def input_gradient():
+        for q in range(cols):
+            m_mid(1, q).wait_recv()
+
+        @pl.loop(0, half // 16, unroll=4)
+        def _(r):
+            at = pl.ds(pl.multiple_of(r * 16, 16), 16)
+            grad = gno[at, :] + ra[at, :].astype(F32)
+            stream = og[pl.ds(pl.multiple_of(rows + core * half + r * 16, 16), 16), :].astype(F32)
+            scale = lax.rsqrt(mean_of(stream * stream) + EPSILON)
+            weighted = grad * gain_mix[...].astype(F32)
+            sums[0] += fold(grad * stream * scale)
+            gm[at, :] += scale * weighted - stream * (scale * scale * scale) * mean_of(weighted * stream)
+
+        m_in.start()
+        in_copy.start()
+
+
+    def gains_and_taps():
+        lines = [jnp.sum(sums[0], axis=0, keepdims=True), jnp.sum(sums[1], axis=0, keepdims=True)]
+        tap_lines = [[jnp.sum(taps_sum[c, k], axis=0, keepdims=True) for c in range(2)] for k in range(3)]
+        for k in range(8):
+            piece = [line[:, k * 128 : (k + 1) * 128] for line in lines]
+            group = k // 2
+            start = (group % 2) * 128
+            piece += [tap_lines[t][group // 2][:, start : start + 128] for t in range(3)]
+            tile = jnp.concatenate(piece + [jnp.zeros((3, 128), F32)], axis=0)
+            for side in range(2):
+                part_s[k // 2, k % 2, side] = tile
+
+    m_final = send(13, outp.at[core], out_hbm.at[mine], mate)
+    out_copy = load(8, outp.at[core], out_hbm.at[mine])
+    in_copy = load(9, gm, in_grad_hbm.at[mine])
+
+    stores = []
+
+    def own_column(u):
+        return pl.multiple_of(x * share + (u % groups) * GROUP, 128)
+
+    def other_column(u):
+        return pl.multiple_of((1 - x) * share + (u % groups) * GROUP, 128)
+
+    def g_store(u, k):
+        target = gate_hbm if u < groups else up_hbm
+        column = own_column(u) if k == 0 else other_column(u)
+        return pltpu.make_async_copy(stage_g.at[u, k], target.at[:, pl.ds(column, GROUP)], g_sem.at[u, k])
+
+    def d_store(q):
+        return pltpu.make_async_copy(stage_d.at[q], down_hbm.at[:, pl.ds(q * WIDE, WIDE)], d_sem.at[q])
+
+    def i_store(i):
+        return pltpu.make_async_copy(stage_i.at[i], in_hbm.at[i // 2, :, pl.ds((i % 2) * WIDE, WIDE)], m_sem.at[i])
+
+    def o_store(q):
+        return pltpu.make_async_copy(stage_o.at[q], outw_hbm.at[:, pl.ds(q * WIDE, WIDE)], m_sem.at[6 + q])
+
+    def g3(u):
+        stage_g[u, 0] = grads.run3(u)
+        g_store(u, 0).start()
+
+    def g4(u):
+        stage_g[u, 1] = grads.run4(u)
+        g_store(u, 1).start()
+
+    def d6(q):
+        downs.run6(q, stage_d.at[q])
+        d_store(q).start()
+
+    def i4(i):
+        stage_i[i] = ins.run4(i, IN_FIRST[i])
+        i_store(i).start()
+
+    def o4(q):
+        stage_o[q] = outs.run4(q, OUT_FIRST[q])
+        o_store(q).start()
+
+    def s4(u):
+        stage_s[...] = smalls.run4(u, True)
+        m_small.start()
+
+    table = {
+        "d1": downs.run1, "d2": downs.run2, "d3": downs.run3, "d4": downs.run4, "d5": lambda q: downs.run5(q, stage_d.at[q]), "d6": d6,
+        "g1": grads.run1, "g2": grads.run2, "g3": g3, "g4": g4,
+        "i1": lambda i: ins.run1(i, IN_FIRST[i]), "o1": lambda q: outs.run1(q, OUT_FIRST[q]), "s1": lambda u: smalls.run1(u, True),
+        "i2": lambda i: ins.run2(i, IN_FIRST[i]), "i3": lambda i: ins.run3(i, IN_FIRST[i]), "i4": i4,
+        "o2": lambda q: outs.run2(q, OUT_FIRST[q]), "o3": lambda q: outs.run3(q, OUT_FIRST[q]), "o4": o4,
+        "s2": lambda u: smalls.run2(u, True), "s3": lambda u: smalls.run3(u, True), "s4": s4,
+    }
+
+    steps = {
+        "Wt": [turn_activated],
+        "Wd": [lambda q=q: down_part(q) for q in range(cols)],
+        "Wg": [lambda: hidden_part(part_g, gg)],
+        "Wu": [lambda: hidden_part(part_u, gu)],
+        "gn0": [gradient_theirs],
+        "gn1": [gradient_mine],
+        "out": [output_both],
+        "norm": [ffn_norm],
+        "mixb": [mixer_back],
+        "iA": [lambda i=i: in_grad_of(i) for i in (2, 3, 0, 4, 1, 5)],
+        "hw": [lambda: gated_back(0)],
+        "el": [lambda: gated_back(1)],
+        "oA": [lambda c=c: out_grad_of(c) for c in range(2)],
+        "gnm": [mix_gradient],
+        "outf": [final_output],
+        "ing": [input_gradient],
+        "gain": [gains_and_taps],
+    }
+    for word in PROGRAM:
+        if word in steps:
+            steps[word].pop(0)()
+        else:
+            table[word[:2]](int(word[2:]))
+
+    m_small.wait_recv()
+    m_small.wait_send()
+    keep = lax.broadcasted_iota(jnp.int32, (8, 128), 0) < 2
+    stage_s[...] = stage_s[...] + jnp.where(keep, recv_s[...], 0.0)
+    small_copy = load(10, stage_s, small_hbm)
+    small_copy.start()
+
+    for u in range(2 * groups):
+        grads.drain(u)
+        g_store(u, 0).wait()
+        g_store(u, 1).wait()
+    for q in range(cols):
+        downs.drain(q)
+        d_store(q).wait()
+    for i in range(6):
+        ins.drain(i, IN_FIRST[i])
+        i_store(i).wait()
+    for q in range(cols):
+        outs.drain(q, OUT_FIRST[q])
+        o_store(q).wait()
+    smalls.drain(0, True)
+    for copy in (small_copy, out_copy, in_copy):
+        copy.wait()
+    for copy in (x_og, m_gn0, m_gn1, x_gn, m_out1, x_out, m_rmid, m_in, m_final):
+        copy.wait_send()
+    m_in.wait_recv()
+    m_final.wait_recv()
+    for q in range(cols):
+        m_mid(1, q).wait_send()
+    for c in range(2):
+
+        @pl.when(me < last)
+        def _():
+            halo_fwd(c).wait_send()
+
+        @pl.when(me > 0)
+        def _():
+            halo_back(c).wait_send()
+
+
+IN_FIRST = (True, True, True, True, True, True)
+OUT_FIRST = (False, True, False, True)
+PROGRAM = (
+    "Wt", "Wd", "d10", "Wd", "Wd", "Wd", "Wg", "g12", "d11", "d20", "Wu", "d30", "g15", "gn0",
+    "d12", "gn1", "d13", "g22", "out", "d21", "d31", "norm", "g25", "mixb", "d41", "iA", "i12", "iA",
+    "d22", "g11", "hw", "g14", "iA", "g10", "d23", "d32", "d33", "iA", "i10", "el", "iA", "d42",
+    "iA", "g21", "d43", "i14", "oA", "g13", "d40", "oA", "o13", "g24", "i13", "i22", "g20", "i15",
+    "g31", "o11", "d52", "gnm", "i20", "i32", "g32", "g23", "i11", "o12", "d50", "i24", "i25", "i34",
+    "o22", "o10", "o20", "outf", "i21", "i35", "d53", "o21", "d51", "g35", "i23", "ing", "o23", "g33",
+    "i30", "o31", "i31", "g45", "gain", "g30", "s10", "o33", "g34", "o32", "i33", "o30", "i40", "d63",
+    "g44", "g42", "i41", "i45", "o41", "d60", "d61", "i44", "g43", "s20", "s30", "o42", "g41", "i42",
+    "g40", "d62", "o40", "i43", "o43", "s40",
+)
+
+
+def whole_block(inputs, out_grad, mix_gain, in_weight, conv_weight, out_weight, ffn_gain, gate_weight, up_weight, down_weight):
+    rows, width = inputs.shape[1:]
+    hidden = gate_weight.shape[2]
+    channels = out_weight.shape[1]
+    cols, share, half = width // WIDE, hidden // 2, rows // 2
+    n = lax.axis_size("seq")
+
+    def vm(*shape, kind=BF16):
+        return pltpu.VMEM(shape, kind)
+
+    def dma(*shape):
+        return pltpu.SemaphoreType.DMA(shape)
+
+    def buffers(count, length, lanes, kind):
+        return [vm(count, 4, 2, length, lanes, kind=kind), vm(count, 4, length, lanes, kind=kind), vm(count, 3, length, lanes, kind=kind)]
+
+    lq, ld, lo = width // n, hidden // n, channels // n
+    hbm = pl.BlockSpec(memory_space=pl.ANY)
+    vmem = pl.BlockSpec(memory_space=pltpu.VMEM)
+    results = pl.pallas_call(
+        block_kernel,
+        out_shape=[
+            jax.ShapeDtypeStruct((rows, width), BF16),
+            jax.ShapeDtypeStruct((rows, width), F32),
+            jax.ShapeDtypeStruct((lq, hidden), F32),
+            jax.ShapeDtypeStruct((lq, hidden), F32),
+            jax.ShapeDtypeStruct((ld, width), F32),
+            jax.ShapeDtypeStruct((3, lq, channels), F32),
+            jax.ShapeDtypeStruct((lo, width), F32),
+            jax.ShapeDtypeStruct((8, 128), F32),
+        ],
+        in_specs=[hbm] * 7 + [vmem] * 3,
+        out_specs=[hbm] * 8,
+        scratch_shapes=[
+            vm(rows, width), vm(2 * rows, width), vm(2 * rows, width), vm(width, 2 * rows),
+            *[vm(4, 2, 2, 64, share)] * 3,
+            *[vm(half, width, kind=F32)] * 3,
+            vm(6, rows, WIDE, kind=F32), vm(2, rows + 8, WIDE, kind=F32), vm(2, rows + 8, WIDE, kind=F32),
+            vm(2, rows, WIDE), vm(channels, width), vm(width, share), vm(width, share), vm(share, width),
+            vm(3, half, share - 512, kind=F32),
+            vm(half, width), vm(half, width),
+            *[vm(4, half, width), vm(2, half, width), vm(half, width)] * 2,
+            vm(2, 8, width, kind=F32), vm(2, 3, 8, WIDE, kind=F32),
+            vm(4, 2, 2, lq, share), vm(4, 2, 2, lq, share),
+            vm(6, 4, 2, lq, 384), vm(6, 3, 2, lq, 384), vm(6, lq, 384), vm(6, lq, 384),
+            vm(cols, 2, 2, 2, ld, WIDE), vm(cols, 2, 2, ld, WIDE), vm(cols, 2, 2, ld, WIDE), vm(cols, 2, ld, WIDE),
+            vm(cols, ld, WIDE), vm(cols, ld, WIDE),
+            *buffers(6, lq, WIDE, BF16), *buffers(cols, lo, WIDE, BF16),
+            vm(4, 2, 2, 8, 128, kind=F32), *buffers(1, 8, 128, F32), vm(8, 128, kind=F32),
+            vm(6, 2, lq, 384, kind=F32), vm(cols, ld, WIDE, kind=F32), vm(6, lq, WIDE, kind=F32), vm(cols, lo, WIDE, kind=F32),
+            vm(8, 128, kind=F32),
+            dma(6), dma(6), dma(6, 3), dma(6, 3), dma(6), dma(6), *[dma(cols)] * 8,
+            *[dma(11)] * 4, *[dma(11, 3)] * 2,
+            dma(11), dma(15), dma(15), dma(2, cols), dma(2, cols), dma(4), dma(4), dma(6, 2), dma(cols), dma(10),
+        ],
+        compiler_params=pltpu.CompilerParams(collective_id=0, has_side_effects=True, vmem_limit_bytes=VMEM_BYTES),
+    )(
+        inputs[0], out_grad[0], in_weight.reshape(width, 3 * channels), out_weight[0],
+        gate_weight[0], up_weight[0], down_weight[0], mix_gain, conv_weight[0], ffn_gain,
+    )
+    output, in_grad, gate_s, up_s, down_s, in_s, out_s, small = results
+    index = lax.axis_index("seq")
+    y, x = (index // 2) % 2, index % 2
+    gains = lax.dynamic_slice(small, (0, x * 64), (2, 64))
+    conv_s = lax.dynamic_slice(small, (2, y * 64 + x * 32), (3, 32))
+    return (
+        output[None], in_grad[None], gains[0:1], in_s.transpose(1, 0, 2)[None], conv_s[None],
+        out_s[None], gains[1:2], gate_s[None], up_s[None], down_s[None],
+    )
+
+
 def inverse_rms(stream):
     return lax.rsqrt(jnp.mean(stream * stream, axis=-1, keepdims=True) + EPSILON)
 
@@ -291,6 +1274,10 @@
     up_weight,
     down_weight,
 ):
+    if lax.axis_size("seq") == 16:
+        return whole_block(
+            inputs, out_grad, mix_gain, in_weight, conv_weight, out_weight, ffn_gain, gate_weight, up_weight, down_weight
+        )
     layer_count = mix_gain.shape[0]
 
     def weights_of(number):

time: 403 us -> 189 us (0.47); the launches traced: 396 us -> 189 us
  Pallas kernels: 0 us -> 172 us
  starting transfers between devices: 127 us -> 0 us
  waiting for transfers between devices: 117 us -> 0 us
  other arithmetic: 71.1 us -> 0 us
  matrix products: 55.1 us -> 0 us
  local copies, waits for them, and re-layouts: 22.9 us -> 16.4 us
    pallas_call x0 -> x1, Pallas kernels: none -> 172 us  [whole_block(): pl.pallas_call(block_kernel, out_shape=[jax.ShapeDtypeStruct((rows, width...]
    ppermute x54 -> x0, starting transfers between devices: 127 us -> none  [the longest x36 108 us: hop(): return lax.ppermute(block, 'seq', route)]
    ppermute x54 -> x0, waiting for transfers between devices: 117 us -> none  [the longest x12 51.7 us: scatter_sum(): lax.ppermute(sent, 'seq', [(i, i + stride * (1 - 2 * (i // stride % 2)))...]
    dot_general x15 -> x0, matrix products: 55.1 us -> none  [the longest x1 8.54 us: forward_block(): jnp.dot(flat_ffn, weight_gate, preferred_element_type=jnp.float32)]
    convert_element_type x31 -> x0, other arithmetic: 43.4 us -> none  [the longest x23 31.9 us: scatter_sum(): carried = hop(sent.astype(wire), dims, dim, step, spots)]
    broadcast_in_dim x5 -> x0, other arithmetic: 9.65 us -> none  [the longest x1 2.14 us: local(): gate_s[None]]
    squeeze x6 -> x0, local copies, waits for them, and re-layouts: 6.99 us -> none  [pick(): return lax.dynamic_index_in_dim(array, at, axis, keepdims=False)]
    another operation x3 -> x0, other arithmetic: 5.62 us -> none
  transfers between devices with their start and end apart: 54 -> 0, of which waited for: 14 -> 0; matrix products, arithmetic and copies ran while one was open for 25% -> 0% of each run, Pallas kernels for 0% -> 0%
where the time goes in v4:
time: 189 us
  Pallas kernels  172 us (91%)
  local copies, waits for them, and re-layouts  16.4 us (9%)
    pallas_call x1, Pallas kernels, whole_block(): pl.pallas_call(block_kernel, out_shape=[jax.ShapeDtypeStruct((rows, width...  172 us
    unnamed x21, local copies, waits for them, and re-layouts  11.3 us

profile of v4, /device:TPU:0, one launch (start us, length us, event | category | flops | bytes accessed | tf_op | source)
XLA Modules:
  0.0 189.2 jit_solution(5703486742202748240)
XLA Ops:
  0.6 3.2 %copy.22 = bf16[1,1024,3,512]{1,3,2,0:T(8,128)(2,1)S(1)} copy(bf16[1,1024,3,512]{3,1,2,0:T(8,128)(2,1)} %param.13) | data formatting | bytes 6291456 | tf_op args[3]
  3.8 3.0 %copy.23.win_hbm = bf16[1024,1536]{1,0:T(8,128)(2,1)} copy(bf16[1024,1536]{0,1:T(8,128)(2,1)S(1)} %bitcast.19) | data formatting | bytes 6291456 | tf_op jit(solution)/shard_map/reshape | solution.py:1057
  6.8 172.1 %shard_map.177 = (bf16[512,1024]{1,0:T(8,128)(2,1)}, f32[512,1024]{1,0:T(8,128)}, f32[64,2304]{1,0:T(8,128)}, f32[64,2304]{1,0:T(8,128)}, f32[144,1024]{1,0:T(8,...) custom-call(bf16[512,1024]{1,0:T(8,128)(2,1)} %bitcast.25, bf16[512,1024]{1,0:T(8,128)(2,1)} %bitcast.26, ...), custom_call_target="tpu_custom_call" | custom-call | tf_op jit(solution)/shard_map/pallas_call | solution.py:1019
  178.9 0.0 copy-start
  178.9 0.9 constant_dynamic-slice_fusion
  179.8 0.5 fusion
  180.4 0.8 dynamic-slice_bitcast_fusion
  181.1 0.6 copy.24
  181.7 0.0 copy-start.4
  181.7 0.0 copy-start.5
  181.7 2.3 %copy.32 = bf16[1,512,1024]{2,1,0:T(8,128)(2,1)} copy(bf16[1,512,1024]{2,1,0:T(8,128)(2,1)} %bitcast.24) | data formatting | bytes 2097152
  184.0 0.0 copy-done
  184.0 0.0 copy-start.3
  184.0 0.0 copy-start.2
  184.0 0.0 copy-start.1
  184.0 1.3 copy.33
  185.3 0.0 copy-done.4
  185.3 0.7 copy.34
  186.1 0.0 copy-done.5
  186.1 0.7 copy.35
  186.7 0.0 copy-done.3
  186.7 0.8 copy.36
  187.6 0.0 copy-done.2
  187.6 0.8 copy.37
  188.4 0.0 copy-done.1
  188.4 0.8 copy.38
Async XLA Ops:
  178.9 5.1 %copy-start = (f32[512,1024]{1,0:T(8,128)S(1)}, f32[512,1024]{1,0:T(8,128)}, u32[]{:S(2)}) copy-start(f32[512,1024]{1,0:T(8,128)} %get-tuple-element.19) | copy-start | bytes 6291460
  181.7 3.7 %copy-start.4 = (f32[3,64,512]{2,1,0:T(8,128)S(1)}, f32[3,64,512]{2,1,0:T(8,128)}, u32[]{:S(2)}) copy-start(f32[3,64,512]{2,1,0:T(8,128)} %get-tuple-element.21) | copy-start | bytes 1179652
  181.7 4.4 %copy-start.5 = (f32[32,1024]{1,0:T(8,128)S(1)}, f32[32,1024]{1,0:T(8,128)}, u32[]{:S(2)}) copy-start(f32[32,1024]{1,0:T(8,128)} %get-tuple-element.22) | copy-start | bytes 393220
  184.0 2.7 %copy-start.3 = (f32[64,2304]{1,0:T(8,128)S(1)}, f32[64,2304]{1,0:T(8,128)}, u32[]{:S(2)}) copy-start(f32[64,2304]{1,0:T(8,128)} %get-tuple-element.23) | copy-start | bytes 1769476
  184.0 3.6 %copy-start.2 = (f32[64,2304]{1,0:T(8,128)S(1)}, f32[64,2304]{1,0:T(8,128)}, u32[]{:S(2)}) copy-start(f32[64,2304]{1,0:T(8,128)} %get-tuple-element.24) | copy-start | bytes 1769476
  184.0 4.4 %copy-start.1 = (f32[144,1024]{1,0:T(8,128)S(1)}, f32[144,1024]{1,0:T(8,128)}, u32[]{:S(2)}) copy-start(f32[144,1024]{1,0:T(8,128)} %get-tuple-element.25) | copy-start | bytes 1769476
